TPU v7x, 32 devices: a whole 2x2x4 slice. The times are simulated.
32 devices in a mesh: gx: 8 (over y, x, core), gy: 4 (over z).
Axes of the slice: x: 2, y: 2, z: 4, core: 2. Of those that a mesh axis runs over, the one named last changes fastest.
Arguments:
- fields: float32 [8, 2048, 2048], P(None, 'gx', 'gy'), may hold values from -6 to 6
- wave_order: int32 [1024], replicated, may hold values from 0 to 1023, as said below
- kept_mask: int32 [1024, 2048], P('gx', 'gy'), may hold values from 0 to 1, as said below
Outputs:
- spectral: float32 [2, 8, 1024, 2048], P(None, None, 'gx', 'gy')
Inputs may be any that keep to these rules, and one draw needn't show every extreme that they name: `wave_order`: each x-wavenumber 0 to 1023 once. `kept_mask`: in each row the kept y-wavenumbers q are those with min(q, 2048 - q) up to a bound that does not grow with the row's x-wavenumber.
All inputs are finite; a program needn't handle non-finite values.
Results may differ from a plain program's by a relative error of at most 0.00007.
Values sent between devices are 32-bit elements; how exact they have to be, the bound alone decides.
No kernel may reach another device: no remote copies, remote signals or barrier semaphores. Data moves between devices by JAX's collectives and lax.ppermute only.
A program may use at most 192 MiB of HBM per device.

v0:
```python
import math
from functools import partial

import jax
import jax.numpy as jnp
from jax import lax
from jax.experimental import pallas as pl
from jax.experimental.pallas import tpu as pltpu
from jax.sharding import PartitionSpec as P


X_RADIX = 8
Y_RADIX = 4
HALVES = 2
LANES = 128


def roots(numbers, period):
    angles = (numbers % period).astype(jnp.float32) * (2.0 * math.pi / period)
    return jnp.cos(angles), jnp.sin(angles)


def two_parts(values):
    high = lax.reduce_precision(values, 8, 7)
    return high.astype(jnp.bfloat16), (values - high).astype(jnp.bfloat16)


def x_table(period, kept, zero):
    points = jnp.arange(period // X_RADIX, dtype=jnp.int32) + zero
    units = jnp.arange(kept // X_RADIX, dtype=jnp.int32) * X_RADIX
    pairs = jnp.array([[0, 4], [1, 7], [2, 6], [3, 5]], dtype=jnp.int32)
    waves = pairs[:, :, None] + units[None, None, :]
    cos, sin = roots(waves[..., None] * points, period)
    table = jnp.stack([cos, sin], axis=2).reshape(4, 4 * units.shape[0], points.shape[0])
    return jnp.concatenate(two_parts(table), axis=2)


def y_table(period, scale, zero):
    short = period // Y_RADIX
    ids = jnp.arange(short, dtype=jnp.int32) + zero
    cos, sin = roots(ids[:, None] * ids[None, :], short)
    return jnp.stack(two_parts(jnp.concatenate([cos, sin], axis=1) * scale))


def y_twiddles(period, zero):
    ids = jnp.arange(period // Y_RADIX, dtype=jnp.int32) + zero
    cos, sin = roots(jnp.arange(Y_RADIX, dtype=jnp.int32)[:, None] * ids[None, :], period)
    return jnp.concatenate([cos, sin], axis=0)


def dot(left, right):
    return jnp.dot(left, right, preferred_element_type=jnp.float32)


def split(values):
    high = values.astype(jnp.bfloat16)
    return high, (values - high.astype(jnp.float32)).astype(jnp.bfloat16)


def pack_body(me_ref, *refs):
    count = len(refs) // 2
    for at in range(count):
        refs[count + at][...] = refs[at][0]


def pack(me, fields, first, columns):
    stack_count, rows, width = fields.shape
    lanes = width // columns
    gx = (stack_count // HALVES) * columns

    def spec(step):
        def index(_, me_ref):
            to = jnp.bitwise_xor(me_ref[0], step)
            return (first + to // columns, 0, to % columns)

        return pl.BlockSpec((1, rows, lanes), index)

    block = jax.ShapeDtypeStruct((rows, lanes), jnp.float32)
    return pl.pallas_call(
        pack_body,
        grid_spec=pltpu.PrefetchScalarGridSpec(
            num_scalar_prefetch=1,
            grid=(1,),
            in_specs=[spec(step) for step in range(1, gx)],
            out_specs=[pl.BlockSpec((rows, lanes), lambda *_: (0, 0)) for _ in range(1, gx)],
        ),
        out_shape=[block] * (gx - 1),
        name="pack",
    )(me, *([fields] * (gx - 1)))


def x_body(me_ref, where_ref, own_ref, *refs):
    others = refs[: X_RADIX - 1]
    table_ref, out_ref, line_ref, real_ref, imag_ref = refs[X_RADIX - 1 :]
    me = me_ref[0]
    line_ref[me] = own_ref[0]
    for step, ref in enumerate(others, 1):
        line_ref[jnp.bitwise_xor(me, step)] = ref[...]
    points, lanes = own_ref.shape[1:]
    units = real_ref.shape[0] // X_RADIX
    half = math.sqrt(0.5)
    f = [line_ref[at] for at in range(X_RADIX)]
    a = [f[at] + f[at + 4] for at in range(4)]
    d = [f[at] - f[at + 4] for at in range(4)]
    even, odd = a[0] + a[2], a[1] + a[3]
    less, more = (d[1] - d[3]) * half, (d[1] + d[3]) * half
    groups = (
        (0, 4, even + odd, even - odd),
        (1, 7, d[0] + less, -(d[2] + more)),
        (2, 6, a[0] - a[2], -(a[1] - a[3])),
        (3, 5, d[0] - less, d[2] - more),
    )
    for at, (c, e, left, right) in enumerate(groups):
        high, low = split(jnp.concatenate([left, right], axis=1))
        top = table_ref[at, :, :points]
        product = dot(top, high) + dot(table_ref[at, :, points:], high) + dot(top, low)
        cos_c, sin_c = product[:units], product[units : 2 * units]
        cos_e, sin_e = product[2 * units : 3 * units], product[3 * units :]
        rows_c, rows_e = pl.ds(c * units, units), pl.ds(e * units, units)
        if c == 0:
            real_ref[rows_c] = cos_c[:, :lanes]
            imag_ref[rows_c] = -sin_c[:, :lanes]
            real_ref[rows_e] = cos_e[:, lanes:]
            imag_ref[rows_e] = -sin_e[:, lanes:]
        else:
            real_ref[rows_c] = cos_c[:, :lanes] + sin_c[:, lanes:]
            imag_ref[rows_c] = cos_c[:, lanes:] - sin_c[:, :lanes]
            real_ref[rows_e] = cos_e[:, :lanes] - sin_e[:, lanes:]
            imag_ref[rows_e] = -cos_e[:, lanes:] - sin_e[:, :lanes]

    count, _, rows, _ = out_ref.shape

    def place(to, carry):
        for row in range(rows):
            source = where_ref[to * rows + row]
            out_ref[to, 0, pl.ds(row, 1), :] = real_ref[pl.ds(source, 1), :]
            out_ref[to, 1, pl.ds(row, 1), :] = imag_ref[pl.ds(source, 1), :]
        return carry

    lax.fori_loop(0, count, place, 0)


def x_lines(me, where, fields, first, columns, others, table, count):
    _, rows, width = fields.shape
    lanes = width // columns
    kept = where.shape[0]

    def own(_, me_ref, where_ref):
        return (first + me_ref[0] // columns, 0, me_ref[0] % columns)

    whole = lambda *shape: pl.BlockSpec(shape, lambda *_: (0,) * len(shape))
    out = (count, 2, kept // count, lanes)
    return pl.pallas_call(
        x_body,
        grid_spec=pltpu.PrefetchScalarGridSpec(
            num_scalar_prefetch=2,
            grid=(1,),
            in_specs=[pl.BlockSpec((1, rows, lanes), own)]
            + [whole(rows, lanes)] * len(others)
            + [whole(*table.shape)],
            out_specs=whole(*out),
            scratch_shapes=[
                pltpu.VMEM((X_RADIX, rows, lanes), jnp.float32),
                pltpu.VMEM((kept, lanes), jnp.float32),
                pltpu.VMEM((kept, lanes), jnp.float32),
            ],
        ),
        out_shape=jax.ShapeDtypeStruct(out, jnp.float32),
        name="x_lines",
    )(me, where, fields, *others, table)


def y_body(me_ref, in_ref, twiddle_ref, table_ref, *refs):
    outs = refs[:Y_RADIX]
    high_ref, low_ref, wave_ref = refs[Y_RADIX:]
    me = me_ref[0]
    sources, _, rows, lanes = in_ref.shape
    short = table_ref.shape[1]
    columns = short // lanes
    levels = sources // (Y_RADIX * columns)
    block = levels * rows
    for level in range(levels):
        for column in range(columns):
            base = (level * columns + column) * Y_RADIX
            re = [in_ref[base + at, 0] for at in range(Y_RADIX)]
            im = [in_ref[base + at, 1] for at in range(Y_RADIX)]
            even_r, even_i, odd_r, odd_i = re[0] + re[2], im[0] + im[2], re[1] + re[3], im[1] + im[3]
            less_r, less_i, more_r, more_i = re[0] - re[2], im[0] - im[2], re[1] - re[3], im[1] - im[3]
            folded = (
                (even_r + odd_r, even_i + odd_i),
                (less_r + more_i, less_i - more_r),
                (even_r - odd_r, even_i - odd_i),
                (less_r - more_i, less_i + more_r),
            )
            span = pl.ds(column * lanes, lanes)
            for c, (real, imag) in enumerate(folded):
                if c:
                    cos = twiddle_ref[pl.ds(c, 1), span]
                    sin = twiddle_ref[pl.ds(Y_RADIX + c, 1), span]
                    real, imag = real * cos + imag * sin, imag * cos - real * sin
                for part, values in enumerate((real, imag)):
                    high, low = split(values)
                    at = pl.ds((c * 2 + part) * block + level * rows, rows)
                    high_ref[at, span] = high
                    low_ref[at, span] = low
    for c in range(Y_RADIX):
        at = pl.ds(c * 2 * block, 2 * block)
        product = dot(high_ref[at], table_ref[0]) + dot(low_ref[at], table_ref[0]) + dot(high_ref[at], table_ref[1])
        real = product[:block, :short] + product[block:, short:]
        imag = product[block:, :short] - product[:block, short:]
        for to in range(Y_RADIX):
            piece = slice(to * (short // Y_RADIX), (to + 1) * (short // Y_RADIX))
            wave_ref[c, to, :block] = real[:, piece]
            wave_ref[c, to, block:] = imag[:, piece]
    lane = lax.broadcasted_iota(jnp.int32, (rows, LANES), 1)
    residue = lane % Y_RADIX
    for step in range(Y_RADIX):
        to = jnp.bitwise_xor(me, step)
        for part in range(2):
            for level in range(levels):
                at = pl.ds(part * block + level * rows, rows)
                pieces = [wave_ref[c, to, at, :] for c in range(Y_RADIX)]
                for tile in range(Y_RADIX):
                    index = tile * (LANES // Y_RADIX) + lane // Y_RADIX
                    value = jnp.take_along_axis(pieces[0], index, axis=1, mode="promise_in_bounds")
                    for c in range(1, Y_RADIX):
                        other = jnp.take_along_axis(pieces[c], index, axis=1, mode="promise_in_bounds")
                        value = jnp.where(residue == c, other, value)
                    outs[step][part, level, :, pl.ds(tile * LANES, LANES)] = value


def y_lines(me, spectra, twiddles, table):
    sources, _, rows, lanes = spectra.shape
    short = table.shape[1]
    levels = sources * lanes // (Y_RADIX * short)
    whole = lambda *shape: pl.BlockSpec(shape, lambda *_: (0,) * len(shape))
    out = (2, levels, rows, short)
    tall = Y_RADIX * 2 * levels * rows
    return pl.pallas_call(
        y_body,
        grid_spec=pltpu.PrefetchScalarGridSpec(
            num_scalar_prefetch=1,
            grid=(1,),
            in_specs=[whole(*spectra.shape), whole(*twiddles.shape), whole(*table.shape)],
            out_specs=[whole(*out)] * Y_RADIX,
            scratch_shapes=[
                pltpu.VMEM((tall, short), jnp.bfloat16),
                pltpu.VMEM((tall, short), jnp.bfloat16),
                pltpu.VMEM((Y_RADIX, Y_RADIX, 2 * levels * rows, short // Y_RADIX), jnp.float32),
            ],
        ),
        out_shape=[jax.ShapeDtypeStruct(out, jnp.float32)] * Y_RADIX,
        name="y_lines",
    )(me, spectra, twiddles, table)


def finish_body(me_ref, *refs):
    blocks, mask_ref, out_ref = refs[:Y_RADIX], refs[Y_RADIX], refs[-1]
    rows = blocks[0].shape[2]
    for step, ref in enumerate(blocks):
        at = pl.ds(pl.multiple_of(jnp.bitwise_xor(me_ref[0], step) * rows, 8), rows)
        weight = mask_ref[at, :].astype(jnp.float32)
        for part in range(2):
            out_ref[part, 0, at, :] = ref[part, 0] * weight


def finish(me, blocks, kept_mask, first, stack_count, before):
    _, levels, rows, width = blocks[0].shape
    block = pl.BlockSpec((2, 1, rows, width), lambda level, me_ref: (0, level, 0, 0))
    extra = [] if before is None else [before]
    return pl.pallas_call(
        finish_body,
        grid_spec=pltpu.PrefetchScalarGridSpec(
            num_scalar_prefetch=1,
            grid=(levels,),
            in_specs=[block] * Y_RADIX
            + [pl.BlockSpec(kept_mask.shape, lambda level, me_ref: (0, 0))]
            + [pl.BlockSpec(memory_space=pl.ANY)] * len(extra),
            out_specs=pl.BlockSpec(
                (2, 1) + kept_mask.shape, lambda level, me_ref: (0, first + level, 0, 0)
            ),
        ),
        out_shape=jax.ShapeDtypeStruct((2, stack_count) + kept_mask.shape, jnp.float32),
        input_output_aliases={} if before is None else {2 + Y_RADIX: 0},
        name="finish",
    )(me, *blocks, kept_mask, *extra)


def turn(values):
    lane = lax.broadcasted_iota(jnp.int32, values.shape, 1)
    rolled = pltpu.roll(values, LANES // 2, 1)
    return jnp.where(lane < LANES // 2, rolled, -rolled)


def y_first_body(scale, me_ref, own_ref, *refs):
    others = refs[: Y_RADIX - 1]
    twiddle_ref, table_ref = refs[Y_RADIX - 1 : Y_RADIX + 1]
    outs = refs[Y_RADIX + 1 : Y_RADIX + 1 + X_RADIX]
    field_ref, wave_ref = refs[Y_RADIX + 1 + X_RADIX :]
    me_x, me_y = me_ref[0], me_ref[1]
    rows, short = own_ref.shape[1:]
    half = short // 2
    field_ref[me_y] = own_ref[0]
    for step, ref in enumerate(others, 1):
        field_ref[jnp.bitwise_xor(me_y, step)] = ref[...]
    even, odd = field_ref[0] + field_ref[2], field_ref[1] + field_ref[3]
    less, more = field_ref[0] - field_ref[2], field_ref[1] - field_ref[3]
    folded = ((even + odd, None), (less, -more), (even - odd, None), (less, more))
    for c, (real, imag) in enumerate(folded):
        if c:
            cos, sin = twiddle_ref[pl.ds(c, 1), :], twiddle_ref[pl.ds(Y_RADIX + c, 1), :]
            if imag is None:
                real, imag = real * cos, -real * sin
            else:
                real, imag = real * cos + imag * sin, imag * cos - real * sin
        tall = real if imag is None else jnp.concatenate([real, imag], axis=0)
        high, low = split(tall)
        parts = []
        for span in (pl.ds(0, half), pl.ds(short, half)):
            parts.append(dot(high, table_ref[0, :, span]) + dot(low, table_ref[0, :, span]) + dot(high, table_ref[1, :, span]))
        by_cos, by_sin = parts
        if imag is None:
            point = lax.broadcasted_iota(jnp.int32, real.shape, 1)
            top = jnp.sum(jnp.where(point % 2 == 0, real, -real), axis=1, keepdims=True) * scale
            unit = lax.broadcasted_iota(jnp.int32, by_sin.shape, 1)
            wave_ref[c, 0] = by_cos
            wave_ref[c, 1] = jnp.where(unit == 0, top, -by_sin)
        else:
            wave_ref[c, 0] = by_cos[:rows] + by_sin[rows:]
            wave_ref[c, 1] = by_cos[rows:] - by_sin[:rows]
    chunk = 32

    def place(at, carry):
        span = pl.ds(pl.multiple_of(at * chunk, chunk), chunk)
        lane = lax.broadcasted_iota(jnp.int32, (chunk, LANES), 1)
        local = lane % (LANES // 2)
        for step in range(X_RADIX):
            to = jnp.bitwise_xor(me_x, step)
            index = to * (LANES // 2 // Y_RADIX) + local // Y_RADIX
            for side in range(2):
                units = pl.ds(side * LANES, LANES)
                value = None
                for c in range(Y_RADIX):
                    pair = [
                        jnp.take_along_axis(wave_ref[c, part, span, units], index, axis=1, mode="promise_in_bounds")
                        for part in range(2)
                    ]
                    both = jnp.where(lane < LANES // 2, *pair)
                    value = both if c == 0 else jnp.where(lane % Y_RADIX == c, both, value)
                outs[step][span, units] = value
        return carry

    lax.fori_loop(0, rows // chunk, place, 0)


def y_first(me, scale, fields, first, others, twiddles, table):
    _, rows, short = fields.shape
    whole = lambda *shape: pl.BlockSpec(shape, lambda *_: (0,) * len(shape))
    out = (rows, 2 * LANES)
    return pl.pallas_call(
        partial(y_first_body, scale),
        grid_spec=pltpu.PrefetchScalarGridSpec(
            num_scalar_prefetch=1,
            grid=(1,),
            in_specs=[pl.BlockSpec((1, rows, short), lambda _, me_ref: (first + me_ref[1], 0, 0))]
            + [whole(rows, short)] * len(others)
            + [whole(*twiddles.shape), whole(*table.shape)],
            out_specs=[whole(*out)] * X_RADIX,
            scratch_shapes=[
                pltpu.VMEM((Y_RADIX, rows, short), jnp.float32),
                pltpu.VMEM((Y_RADIX, 2, rows, short // 2), jnp.float32),
            ],
        ),
        out_shape=[jax.ShapeDtypeStruct(out, jnp.float32)] * X_RADIX,
        name="y_first",
    )(me, fields, *others, twiddles, table)


def x_second_body(me_ref, where_ref, *refs):
    blocks = refs[:X_RADIX]
    table_ref, out_ref, fold_ref, wave_ref = refs[X_RADIX:]
    me = me_ref[0]
    points = blocks[0].shape[0]
    units = wave_ref.shape[1] // X_RADIX
    for step, ref in enumerate(blocks):
        fold_ref[jnp.bitwise_xor(me, step)] = ref[...]
    half = math.sqrt(0.5)
    for side in range(2):
        span = pl.ds(side * LANES, LANES)
        f = [fold_ref[at, :, span] for at in range(X_RADIX)]
        a = [f[at] + f[at + 4] for at in range(4)]
        d = [f[at] - f[at + 4] for at in range(4)]
        even, odd, less, more = a[0] + a[2], a[1] + a[3], a[0] - a[2], turn(a[1] - a[3])
        across, along = turn(d[2]), turn(d[1] + d[3])
        one = (d[1] - d[3] + along) * half
        three = (along - d[1] + d[3]) * half
        folded = {
            0: even + odd,
            4: even - odd,
            2: less + more,
            6: less - more,
            1: d[0] + across + one,
            5: d[0] + across - one,
            3: d[0] - across + three,
            7: d[0] - across - three,
        }
        for c, values in folded.items():
            fold_ref[c, :, span] = values
    lane = lax.broadcasted_iota(jnp.int32, (points, 2 * LANES), 1)
    sign = jnp.where(lane % LANES < LANES // 2, 1.0, -1.0)
    lane = lax.broadcasted_iota(jnp.int32, (units, LANES), 1)
    special = jnp.logical_and(lane % (LANES // 2) == 0, me == 0)
    for at, pair in enumerate(((0, 4), (1, 7), (2, 6), (3, 5))):
        for side, c in enumerate(pair):
            data = jnp.concatenate([fold_ref[c], fold_ref[-c % X_RADIX] * sign], axis=1)
            high, low = split(data)
            rows = pl.ds(side * 2 * units, 2 * units)
            top = table_ref[at, rows, :points]
            product = dot(top, high) + dot(table_ref[at, rows, points:], high) + dot(top, low)
            plus_low, plus_high, minus_low, minus_high = (
                product[:units, piece * LANES : (piece + 1) * LANES]
                + turn(product[units:, piece * LANES : (piece + 1) * LANES])
                for piece in range(4)
            )
            rows = pl.ds(c * units, units)
            wave_ref[0, rows] = jnp.where(special, (plus_low + minus_low) * 0.5, plus_low)
            wave_ref[1, rows] = plus_high
            wave_ref[2, rows] = jnp.where(special, turn(plus_low - minus_low) * 0.5, minus_high)
            wave_ref[3, rows] = jnp.where(special, minus_high, minus_low)

    count, rows, _ = out_ref.shape
    unroll = 32

    def place(at, carry):
        to, start = at // (rows // unroll) * Y_RADIX, at % (rows // unroll) * unroll
        for row in range(unroll):
            source = where_ref[at * unroll + row]
            for piece in range(Y_RADIX):
                out_ref[to + piece, pl.ds(start + row, 1), :] = wave_ref[piece, pl.ds(source, 1), :]
        return carry

    lax.fori_loop(0, count // Y_RADIX * (rows // unroll), place, 0)


def x_second(me, where, blocks, table, gx):
    points, lanes = blocks[0].shape
    kept = where.shape[0]
    whole = lambda *shape: pl.BlockSpec(shape, lambda *_: (0,) * len(shape))
    out = (gx * Y_RADIX, kept // gx, LANES)
    return pl.pallas_call(
        x_second_body,
        grid_spec=pltpu.PrefetchScalarGridSpec(
            num_scalar_prefetch=2,
            grid=(1,),
            in_specs=[whole(points, lanes)] * X_RADIX + [whole(*table.shape)],
            out_specs=whole(*out),
            scratch_shapes=[
                pltpu.VMEM((X_RADIX, points, lanes), jnp.float32),
                pltpu.VMEM((Y_RADIX, kept, LANES), jnp.float32),
            ],
        ),
        out_shape=jax.ShapeDtypeStruct(out, jnp.float32),
        name="x_second",
    )(me, where, *blocks, table)


def finish_second_body(me_ref, in_ref, mask_ref, before_ref, out_ref):
    mirrored = me_ref[0] >= Y_RADIX // 2
    rows = mask_ref.shape[0]
    chunk = 32

    def place(at, carry):
        span = pl.ds(pl.multiple_of(at * chunk, chunk), chunk)
        lane = lax.broadcasted_iota(jnp.int32, (chunk, LANES), 1)
        left = lane < LANES // 2
        index = jnp.where(mirrored, (LANES - lane) % LANES, lane)
        for tile in range(Y_RADIX):
            body = jnp.where(mirrored, Y_RADIX - 1 - tile, tile)
            head = jnp.where(mirrored, (Y_RADIX - tile) % Y_RADIX, tile)
            here, there = in_ref[2 * body, 0, span, :], in_ref[2 * body + 1, 0, span, :]
            start = in_ref[2 * head, 0, span, :]
            real = jnp.where(left, here, pltpu.roll(there, LANES // 2, 1))
            imag = jnp.where(left, pltpu.roll(here, LANES // 2, 1), there)
            lanes = pl.ds(tile * LANES, LANES)
            weight = mask_ref[span, lanes].astype(jnp.float32)
            for part, (values, edge) in enumerate(((real, start), (imag, pltpu.roll(start, LANES // 2, 1)))):
                values = jnp.take_along_axis(values, index, axis=1, mode="promise_in_bounds")
                out_ref[part, 0, span, lanes] = jnp.where(lane == 0, edge, values) * weight
        return carry

    lax.fori_loop(0, rows // chunk, place, 0)


def finish_second(me, blocks, kept_mask, first, before):
    gx, levels, rows, lanes = blocks.shape
    return pl.pallas_call(
        finish_second_body,
        grid_spec=pltpu.PrefetchScalarGridSpec(
            num_scalar_prefetch=1,
            grid=(levels,),
            in_specs=[
                pl.BlockSpec((gx, 1, rows, lanes), lambda level, me_ref: (0, level, 0, 0)),
                pl.BlockSpec(kept_mask.shape, lambda level, me_ref: (0, 0)),
                pl.BlockSpec(memory_space=pl.ANY),
            ],
            out_specs=pl.BlockSpec(
                (2, 1) + kept_mask.shape, lambda level, me_ref: (0, first + level, 0, 0)
            ),
        ),
        out_shape=jax.ShapeDtypeStruct(before.shape, jnp.float32),
        input_output_aliases={3: 0},
        name="finish_second",
    )(me, blocks, kept_mask, before)


def exchange(blocks, axis, size):
    return [
        lax.ppermute(block, axis, [(at, at ^ step) for at in range(size)])
        for step, block in enumerate(blocks, 1)
    ]


def fast_shards(gx, gy, nx, ny, fields, wave_order, kept_mask):
    stack_count = fields.shape[0]
    kept = wave_order.shape[0]
    levels = stack_count // HALVES
    columns = gx // levels
    me_x, me_y = lax.axis_index("gx"), lax.axis_index("gy")
    zero = me_x // gx
    x_me, y_me = me_x.reshape(1).astype(jnp.int32), me_y.reshape(1).astype(jnp.int32)
    where = (wave_order % X_RADIX) * (kept // X_RADIX) + wave_order // X_RADIX
    both_me = jnp.concatenate([x_me, y_me])
    scale = 1.0 / math.sqrt(nx * ny)
    whole = ("gx", "gy")
    second = levels
    fields_second = exchange(pack(y_me, fields, second, 1), "gy", gy)
    lines = exchange(pack(x_me, fields, 0, columns), "gx", gx)
    table_x = x_table(nx, kept, zero)
    table_y = y_table(ny, scale, zero)
    twiddles = y_twiddles(ny, zero)
    spectra = x_lines(x_me, where, fields, 0, columns, lines, table_x, gx * gy)
    spectra = lax.all_to_all(spectra, whole, split_axis=0, concat_axis=0, tiled=True)
    half_waves = y_first(both_me, scale, fields, second, fields_second, twiddles, table_y)
    half_waves = [half_waves[0]] + exchange(half_waves[1:], "gx", gx)
    waves = y_lines(y_me, spectra, twiddles, table_y)
    waves = [waves[0]] + exchange(waves[1:], "gy", gy)
    owned = x_second(x_me, where, half_waves, table_x, gx)
    owned = lax.all_to_all(owned, whole, split_axis=0, concat_axis=0, tiled=True)
    result = finish(y_me, waves, kept_mask, 0, stack_count, None)
    owned = owned.reshape((gx, gy) + owned.shape[1:])
    return finish_second(y_me, owned, kept_mask, second, result)


def wave_angles(wave_ids, points, period):
    phases = wave_ids[:, None] * points[None, :] % period
    angles = phases.astype(jnp.float32) * (2.0 * math.pi / period)
    return (jnp.cos(angles), jnp.sin(angles))


def x_terms(cos_table, sin_table, values):
    stack_count, x_count, y_count = values.shape
    waves = cos_table.shape[0]
    table = jnp.concatenate([cos_table, -sin_table], axis=0)
    flat = jnp.transpose(values, (1, 0, 2)).reshape(x_count, stack_count * y_count)
    product = jnp.dot(
        table, flat, precision=lax.Precision.HIGHEST, preferred_element_type=jnp.float32
    )
    product = product.reshape(2, waves, stack_count, y_count)
    return jnp.transpose(product, (1, 0, 2, 3))


def y_terms(cos_table, sin_table, spectra):
    rows, parts, stack_count, y_count = spectra.shape
    waves = cos_table.shape[0]
    table = jnp.concatenate([cos_table, sin_table], axis=0)
    flat = spectra.reshape(rows * parts * stack_count, y_count)
    product = jnp.dot(
        flat, table.T, precision=lax.Precision.HIGHEST, preferred_element_type=jnp.float32
    )
    product = product.reshape(rows, parts, stack_count, 2, waves)
    real_part = product[:, 0, :, 0] + product[:, 1, :, 1]
    imag_part = product[:, 1, :, 0] - product[:, 0, :, 1]
    return jnp.stack([real_part, imag_part], axis=1)


def plain_shards(nx, ny, fields, wave_order, kept_mask):
    x_every = jnp.arange(nx, dtype=jnp.int32)
    x_cos, x_sin = wave_angles(wave_order, x_every, nx)
    partial_terms = x_terms(
        x_cos, x_sin, lax.all_to_all(fields, "gx", split_axis=2, concat_axis=1, tiled=True)
    )
    spectra = lax.all_to_all(partial_terms, "gx", split_axis=0, concat_axis=3, tiled=True)
    y_every = jnp.arange(ny, dtype=jnp.int32)
    y_cos, y_sin = wave_angles(y_every, y_every, ny)
    y_spectra = y_terms(
        y_cos, y_sin, lax.all_to_all(spectra, "gy", split_axis=0, concat_axis=3, tiled=True)
    )
    result = lax.all_to_all(y_spectra, "gy", split_axis=3, concat_axis=0, tiled=True)
    weight = kept_mask.astype(jnp.float32) * (1.0 / math.sqrt(nx * ny))
    return jnp.transpose(result, (1, 2, 0, 3)) * weight[None, None]


def fits(gx, gy, stack_count, nx, ny, kept):
    levels = stack_count // HALVES
    if gx != X_RADIX or gy != Y_RADIX or levels != gy or stack_count % HALVES:
        return False
    lanes = ny // gy // (gx // levels)
    return (
        lanes % LANES == 0
        and ny == Y_RADIX * Y_RADIX * LANES
        and nx % (X_RADIX * LANES) == 0
        and kept % (X_RADIX * LANES) == 0
        and kept <= nx
        and kept // (gx * gy) % 16 == 0
    )


def solution(mesh):
    gx, gy = mesh.shape["gx"], mesh.shape["gy"]

    def call(fields, wave_order, kept_mask):
        stack_count, nx, ny = fields.shape
        if fits(gx, gy, stack_count, nx, ny, wave_order.shape[0]):
            body = partial(fast_shards, gx, gy, nx, ny)
        else:
            body = partial(plain_shards, nx, ny)
        return jax.shard_map(
            body,
            mesh=mesh,
            in_specs=(P(None, "gx", "gy"), P(), P("gx", "gy")),
            out_specs=P(None, None, "gx", "gy"),
            check_vma=False,
        )(fields, wave_order, kept_mask)

    return call
```

profile of v0, /device:TPU:8, one launch (start us, length us, event | category | flops | bytes accessed | tf_op | source)
XLA Modules:
  0.0 296.3 jit_solution(12309974508337811146)
XLA Ops:
  0.0 2.7 pack.3
  2.7 1.5 collective-permute-start.11
  4.5 1.5 collective-permute-start.13
  6.3 4.1 %fusion.9 = (f32[4,2,1,128,256]{4,3,2,1,0:T(8,128)S(1)}, f32[4,2,1,128,256]{4,3,2,1,0:T(8,128)S(1)}) fusion(s32[256]{0:T(256)S(1)} %iota_add_fusion.1, s32[4,2,128]{2,1,0:T(2,128)S(1)} %broadcast_add_fusion), kind=kLoop, calls=%fused_computation.29 | loop fusion | flops 3670016 | bytes 2102272 | tf_op jit(solution)/shard_map/cos | solution.py:20
  11.6 2.4 collective-permute-start.15
  14.4 1.5 pad_maximum_fusion.2.refs_8_.refs_7_
  16.8 12.4 %collective-permute-done.14.refs_4_ = f32[256,256]{1,0:T(8,128)S(1)} collective-permute-done((f32[256,256]{1,0:T(8,128)}, f32[256,256]{1,0:T(8,128)S(1)}, u32[]{:S(2)}, u32[]{:S(2)}) %collective-permute-start.14) | collective-permute-done | bytes 262176 | tf_op jit(solution)/shard_map/ppermute | solution.py:518
  30.8 9.2 %x_lines.1 = f32[32,2,32,256]{3,2,1,0:T(8,128)} custom-call(s32[1]{0:T(128)} %bitcast.1.me_ref, s32[1024]{0:T(1024)} %fusion.14.where_ref, f32[8,256,512]{2,1,0:T(8,128)} %own_ref.3, f32[256,256]{1,0:T(8,128)} %copy-done.6, f32[256,256]{1,0:T(8,128)} %copy-done.7, f32[256,256]{1,0:T(8,128)} %copy-done.8, f32[256,256]{1,0:T(8,128)} %copy-done.9, ...), custom_call_target="tpu_custom_call" | custom-call | tf_op jit(solution)/shard_map/x_lines/pallas_call | solution.py:153
  40.0 6.3 %all-to-all-start.1 = ((f32[32,2,32,256]{3,2,1,0:T(8,128)}), f32[32,2,32,256]{3,2,1,0:T(8,128)S(1)}, u32[]{:S(2)}, u32[]{:S(2)}) async-start(f32[32,2,32,256]{3,2,1,0:T(8,128)} %x_lines.1), calls=%async_computation.1 | async-start | bytes 4194304 | tf_op jit(solution)/shard_map/all_to_all | solution.py:542
  46.3 2.6 pack.2
  49.3 2.5 collective-permute-start.1
  52.5 4.2 %cosine_bitcast_fusion = (f32[1,512,512]{2,1,0:T(8,128)S(1)}, f32[1,512,512]{2,1,0:T(8,128)S(1)}) fusion(s32[512]{0:T(512)S(1)} %iota_add_fusion), kind=kLoop, calls=%fused_computation.27 | loop fusion | flops 3670016 | bytes 2099200 | tf_op jit(solution)/shard_map/concatenate | solution.py:42
  58.3 1.5 pad_maximum_fusion.refs_4_.table_ref
  59.8 33.4 %collective-permute-done.refs_0_ = f32[256,512]{1,0:T(8,128)S(1)} collective-permute-done((f32[256,512]{1,0:T(8,128)}, f32[256,512]{1,0:T(8,128)S(1)}, u32[]{:S(2)}, u32[]{:S(2)}) %collective-permute-start) | collective-permute-done | bytes 524320 | tf_op jit(solution)/shard_map/ppermute | solution.py:518
  93.3 33.0 %collective-permute-done.1.refs_1_ = f32[256,512]{1,0:T(8,128)S(1)} collective-permute-done((f32[256,512]{1,0:T(8,128)}, f32[256,512]{1,0:T(8,128)S(1)}, u32[]{:S(2)}, u32[]{:S(2)}) %collective-permute-start.1) | collective-permute-done | bytes 524320 | tf_op jit(solution)/shard_map/ppermute | solution.py:518
  126.3 12.8 %collective-permute-done.2.refs_2_ = f32[256,512]{1,0:T(8,128)} collective-permute-done((f32[256,512]{1,0:T(8,128)}, f32[256,512]{1,0:T(8,128)}, u32[]{:S(2)}, u32[]{:S(2)}) %collective-permute-start.2) | collective-permute-done | bytes 524320 | tf_op jit(solution)/shard_map/ppermute | solution.py:518
  139.1 12.3 %y_first.1 = (f32[256,256]{1,0:T(8,128)}, f32[256,256]{1,0:T(8,128)}, f32[256,256]{1,0:T(8,128)}, f32[256,256]{1,0:T(8,128)}, f32[256,256]{1,0:T(8,128)}, /*inde...) custom-call(s32[2]{0:T(128)} %pad_add_fusion.me_ref, f32[8,256,512]{2,1,0:T(8,128)} %own_ref.3, ...), custom_call_target="tpu_custom_call" | custom-call | tf_op jit(solution)/shard_map/y_first/pallas_call | solution.py:360
  153.3 1.5 collective-permute-start.6
  155.0 2.2 collective-permute-start.8
  157.2 3.7 %collective-permute-done.4.refs_2_ = f32[256,256]{1,0:T(8,128)S(1)} collective-permute-done((f32[256,256]{1,0:T(8,128)}, f32[256,256]{1,0:T(8,128)S(1)}, u32[]{:S(2)}, u32[]{:S(2)}) %collective-permute-start.4) | collective-permute-done | bytes 262176 | tf_op jit(solution)/shard_map/ppermute | solution.py:518
  161.8 3.7 %collective-permute-done.5.refs_3_ = f32[256,256]{1,0:T(8,128)S(1)} collective-permute-done((f32[256,256]{1,0:T(8,128)}, f32[256,256]{1,0:T(8,128)S(1)}, u32[]{:S(2)}, u32[]{:S(2)}) %collective-permute-start.5) | collective-permute-done | bytes 262176 | tf_op jit(solution)/shard_map/ppermute | solution.py:518
  165.5 12.6 %collective-permute-done.7.refs_5_ = f32[256,256]{1,0:T(8,128)S(1)} collective-permute-done((f32[256,256]{1,0:T(8,128)}, f32[256,256]{1,0:T(8,128)S(1)}, u32[]{:S(2)}, u32[]{:S(2)}) %collective-permute-start.7) | collective-permute-done | bytes 262176 | tf_op jit(solution)/shard_map/ppermute | solution.py:518
  178.7 9.2 %x_second.1 = f32[32,128,128]{2,1,0:T(8,128)} custom-call(s32[1]{0:T(128)} %bitcast.1.me_ref, s32[1024]{0:T(1024)} %fusion.14.where_ref, f32[256,256]{1,0:T(8,128)} %get-tuple-element.30.refs_0_, f32[256,256]{1,0:T(8,128)} %copy-done.11, f32[256,256]{1,0:T(8,128)} %copy-done.12, f32[256,256]{1,0:T(8,128)} %copy-done.13, f32[256,256]{1,0:T(8,128)} %copy-done.14, ...), custom_call_target="tpu_custom_call" | custom-call | tf_op jit(solution)/shard_map/x_second/pallas_call | solution.py:450
  187.9 1.4 copy-done
  189.3 4.1 %all-to-all-start = ((f32[32,128,128]{2,1,0:T(8,128)}), f32[32,128,128]{2,1,0:T(8,128)}, u32[]{:S(2)}, u32[]{:S(2)}) async-start(f32[32,128,128]{2,1,0:T(8,128)} %x_second.1), calls=%async_computation | async-start | bytes 4194304 | tf_op jit(solution)/shard_map/all_to_all | solution.py:548
  193.4 9.2 %y_lines.1 = (f32[2,4,32,512]{3,2,1,0:T(8,128)}, f32[2,4,32,512]{3,2,1,0:T(8,128)}, f32[2,4,32,512]{3,2,1,0:T(8,128)}, f32[2,4,32,512]{3,2,1,0:T(8,128)}) custom-call(s32[1]{0:T(128)} %bitcast.me_ref, f32[32,2,32,256]{3,2,1,0:T(8,128)} %copy-done, f32[8,512]{1,0:T(8,128)} %pad_maximum_fusion.3.refs_3_.twiddle_ref, ...), custom_call_target="tpu_custom_call" | custom-call | tf_op jit(solution)/shard_map/y_lines/pallas_call | solution.py:239
  203.2 2.4 collective-permute-start.18
  206.1 34.2 %collective-permute-done.17.refs_1_ = f32[2,4,32,512]{3,2,1,0:T(8,128)S(1)} collective-permute-done((f32[2,4,32,512]{3,2,1,0:T(8,128)}, f32[2,4,32,512]{3,2,1,0:T(8,128)S(1)}, u32[]{:S(2)}, u32[]{:S(2)}) %collective-permute-start.17) | collective-permute-done | bytes 524320 | tf_op jit(solution)/shard_map/ppermute | solution.py:518
  240.3 33.0 %collective-permute-done.18.refs_2_ = f32[2,4,32,512]{3,2,1,0:T(8,128)S(1)} collective-permute-done((f32[2,4,32,512]{3,2,1,0:T(8,128)}, f32[2,4,32,512]{3,2,1,0:T(8,128)S(1)}, u32[]{:S(2)}, u32[]{:S(2)}) %collective-permute-start.18) | collective-permute-done | bytes 524320 | tf_op jit(solution)/shard_map/ppermute | solution.py:518
  273.3 12.7 %collective-permute-done.19.refs_3_ = f32[2,4,32,512]{3,2,1,0:T(8,128)S(1)} collective-permute-done((f32[2,4,32,512]{3,2,1,0:T(8,128)}, f32[2,4,32,512]{3,2,1,0:T(8,128)S(1)}, u32[]{:S(2)}, u32[]{:S(2)}) %collective-permute-start.19) | collective-permute-done | bytes 524320 | tf_op jit(solution)/shard_map/ppermute | solution.py:518
  286.8 4.0 %finish.1.before_ref = f32[2,8,128,512]{3,2,1,0:T(8,128)} custom-call(s32[1]{0:T(128)} %bitcast.me_ref, f32[2,4,32,512]{3,2,1,0:T(8,128)} %get-tuple-element.45.refs_0_, f32[2,4,32,512]{3,2,1,0:T(8,128)} %copy-done.3, f32[2,4,32,512]{3,2,1,0:T(8,128)} %copy-done.4, f32[2,4,32,512]{3,2,1,0:T(8,128)} %copy-done.5, s32[128,512]{1,0:T(8,128)} %mask_ref.1), custom_call_target="tpu_custom_call" | custom-call | tf_op jit(solution)/shard_map/finish/pallas_call | solution.py:271
  290.8 5.5 %finish_second.1 = f32[2,8,128,512]{3,2,1,0:T(8,128)} custom-call(s32[1]{0:T(128)} %bitcast.me_ref, f32[8,4,128,128]{3,2,1,0:T(8,128)} %bitcast.5.in_ref, s32[128,512]{1,0:T(8,128)} %mask_ref.1, f32[2,8,128,512]{3,2,1,0:T(8,128)} %finish.1.before_ref), custom_call_target="tpu_custom_call", output_to_operand_aliasing={{}: (3, {})} | custom-call | tf_op jit(solution)/shard_map/finish_second/pallas_call | solution.py:496
  (79 shorter events, 12.7 us)
Async XLA Ops:
  2.7 8.3 %collective-permute-start.10 = (f32[256,256]{1,0:T(8,128)}, f32[256,256]{1,0:T(8,128)S(1)}, u32[]{:S(2)}, u32[]{:S(2)}) collective-permute-start(f32[256,256]{1,0:T(8,128)} %get-tuple-element.38), channel_id=1, source_target_pairs={{0,4},{4,0},{8,12},{12,8},{16,20},{20,16},{24,28},{28,24},{1,5},{5... | collective-permute-start | bytes 786440 | tf_op jit(solution)/shard_map/ppermute | solution.py:518
  2.7 11.3 %collective-permute-start.11 = (f32[256,256]{1,0:T(8,128)}, f32[256,256]{1,0:T(8,128)S(1)}, u32[]{:S(2)}, u32[]{:S(2)}) collective-permute-start(f32[256,256]{1,0:T(8,128)} %get-tuple-element.39), channel_id=1, source_target_pairs={{0,8},{4,12},{8,0},{12,4},{16,24},{20,28},{24,16},{28,20},{1,9},{5... | collective-permute-start | bytes 786440 | tf_op jit(solution)/shard_map/ppermute | solution.py:518
  4.2 12.6 %collective-permute-start.12 = (f32[256,256]{1,0:T(8,128)}, f32[256,256]{1,0:T(8,128)S(1)}, u32[]{:S(2)}, u32[]{:S(2)}) collective-permute-start(f32[256,256]{1,0:T(8,128)} %get-tuple-element.40), channel_id=1, source_target_pairs={{0,12},{4,8},{8,4},{12,0},{16,28},{20,24},{24,20},{28,16},{1,13},{... | collective-permute-start | bytes 786440 | tf_op jit(solution)/shard_map/ppermute | solution.py:518
  4.5 12.3 %collective-permute-start.13 = (f32[256,256]{1,0:T(8,128)}, f32[256,256]{1,0:T(8,128)S(1)}, u32[]{:S(2)}, u32[]{:S(2)}) collective-permute-start(f32[256,256]{1,0:T(8,128)} %get-tuple-element.41), channel_id=1, source_target_pairs={{0,16},{4,20},{8,24},{12,28},{16,0},{20,4},{24,8},{28,12},{1,17},{... | collective-permute-start | bytes 786440 | tf_op jit(solution)/shard_map/ppermute | solution.py:518
  6.1 23.2 %collective-permute-start.14 = (f32[256,256]{1,0:T(8,128)}, f32[256,256]{1,0:T(8,128)S(1)}, u32[]{:S(2)}, u32[]{:S(2)}) collective-permute-start(f32[256,256]{1,0:T(8,128)} %get-tuple-element.42), channel_id=1, source_target_pairs={{0,20},{4,16},{8,28},{12,24},{16,4},{20,0},{24,12},{28,8},{1,21},{... | collective-permute-start | bytes 786440 | tf_op jit(solution)/shard_map/ppermute | solution.py:518
  11.6 17.7 %collective-permute-start.15 = (f32[256,256]{1,0:T(8,128)S(1)}, f32[256,256]{1,0:T(8,128)S(1)}, u32[]{:S(2)}, u32[]{:S(2)}) collective-permute-start(f32[256,256]{1,0:T(8,128)S(1)} %copy-done.21), channel_id=1, source_target_pairs={{0,24},{4,28},{8,16},{12,20},{16,8},{20,12},{24,0},{28,4},{1,25},{... | collective-permute-start | bytes 786440 | tf_op jit(solution)/shard_map/ppermute | solution.py:518
  14.0 15.2 %collective-permute-start.16 = (f32[256,256]{1,0:T(8,128)S(1)}, f32[256,256]{1,0:T(8,128)S(1)}, u32[]{:S(2)}, u32[]{:S(2)}) collective-permute-start(f32[256,256]{1,0:T(8,128)S(1)} %copy-done.20), channel_id=1, source_target_pairs={{0,28},{4,24},{8,20},{12,16},{16,12},{20,8},{24,4},{28,0},{1,29},{... | collective-permute-start | bytes 786440 | tf_op jit(solution)/shard_map/ppermute | solution.py:518
  16.8 12.5 %copy-start.8 = (f32[256,256]{1,0:T(8,128)}, f32[256,256]{1,0:T(8,128)S(1)}, u32[]{:S(2)}) copy-start(f32[256,256]{1,0:T(8,128)S(1)} %collective-permute-done.12.refs_2_) | copy-start | bytes 786436
  16.8 12.5 %copy-start.9 = (f32[256,256]{1,0:T(8,128)}, f32[256,256]{1,0:T(8,128)S(1)}, u32[]{:S(2)}) copy-start(f32[256,256]{1,0:T(8,128)S(1)} %collective-permute-done.13.refs_3_) | copy-start | bytes 786436
  40.0 147.9 %all-to-all-start.1 = ((f32[32,2,32,256]{3,2,1,0:T(8,128)}), f32[32,2,32,256]{3,2,1,0:T(8,128)S(1)}, u32[]{:S(2)}, u32[]{:S(2)}) async-start(f32[32,2,32,256]{3,2,1,0:T(8,128)} %x_lines.1), calls=%async_computation.1 | async-start | bytes 4194304 | tf_op jit(solution)/shard_map/all_to_all | solution.py:542
  48.9 44.4 %collective-permute-start = (f32[256,512]{1,0:T(8,128)}, f32[256,512]{1,0:T(8,128)S(1)}, u32[]{:S(2)}, u32[]{:S(2)}) collective-permute-start(f32[256,512]{1,0:T(8,128)} %get-tuple-element.27), channel_id=1, source_target_pairs={{0,1},{1,0},{2,3},{3,2},{4,5},{5,4},{6,7},{7,6},{8,9},{9,8},{10,11... | collective-permute-start | bytes 1572872 | tf_op jit(solution)/shard_map/ppermute | solution.py:518
  49.3 76.9 %collective-permute-start.1 = (f32[256,512]{1,0:T(8,128)}, f32[256,512]{1,0:T(8,128)S(1)}, u32[]{:S(2)}, u32[]{:S(2)}) collective-permute-start(f32[256,512]{1,0:T(8,128)} %get-tuple-element.28), channel_id=1, source_target_pairs={{0,2},{1,3},{2,0},{3,1},{4,6},{5,7},{6,4},{7,5},{8,10},{9,11},{10,... | collective-permute-start | bytes 1572872 | tf_op jit(solution)/shard_map/ppermute | solution.py:518
  51.8 87.3 %collective-permute-start.2 = (f32[256,512]{1,0:T(8,128)}, f32[256,512]{1,0:T(8,128)}, u32[]{:S(2)}, u32[]{:S(2)}) collective-permute-start(f32[256,512]{1,0:T(8,128)} %get-tuple-element.29), channel_id=1, source_target_pairs={{0,3},{1,2},{2,1},{3,0},{4,7},{5,6},{6,5},{7,4},{8,11},{9,10},{10,... | collective-permute-start | bytes 1572872 | tf_op jit(solution)/shard_map/ppermute | solution.py:518
  93.3 45.8 %copy-start.1 = (f32[256,512]{1,0:T(8,128)}, f32[256,512]{1,0:T(8,128)S(1)}, u32[]{:S(2)}) copy-start(f32[256,512]{1,0:T(8,128)S(1)} %collective-permute-done.refs_0_) | copy-start | bytes 1572868
  126.3 12.8 %copy-start.2 = (f32[256,512]{1,0:T(8,128)}, f32[256,512]{1,0:T(8,128)S(1)}, u32[]{:S(2)}) copy-start(f32[256,512]{1,0:T(8,128)S(1)} %collective-permute-done.1.refs_1_) | copy-start | bytes 1572868
  151.4 3.5 %collective-permute-start.3 = (f32[256,256]{1,0:T(8,128)}, f32[256,256]{1,0:T(8,128)S(1)}, u32[]{:S(2)}, u32[]{:S(2)}) collective-permute-start(f32[256,256]{1,0:T(8,128)} %get-tuple-element.31), channel_id=1, source_target_pairs={{0,4},{4,0},{8,12},{12,8},{16,20},{20,16},{24,28},{28,24},{1,5},{5... | collective-permute-start | bytes 786440 | tf_op jit(solution)/shard_map/ppermute | solution.py:518
  151.4 9.4 %collective-permute-start.4 = (f32[256,256]{1,0:T(8,128)}, f32[256,256]{1,0:T(8,128)S(1)}, u32[]{:S(2)}, u32[]{:S(2)}) collective-permute-start(f32[256,256]{1,0:T(8,128)} %get-tuple-element.32), channel_id=1, source_target_pairs={{0,8},{4,12},{8,0},{12,4},{16,24},{20,28},{24,16},{28,20},{1,9},{5... | collective-permute-start | bytes 786440 | tf_op jit(solution)/shard_map/ppermute | solution.py:518
  152.7 12.7 %collective-permute-start.5 = (f32[256,256]{1,0:T(8,128)}, f32[256,256]{1,0:T(8,128)S(1)}, u32[]{:S(2)}, u32[]{:S(2)}) collective-permute-start(f32[256,256]{1,0:T(8,128)} %get-tuple-element.33), channel_id=1, source_target_pairs={{0,12},{4,8},{8,4},{12,0},{16,28},{20,24},{24,20},{28,16},{1,13},{... | collective-permute-start | bytes 786440 | tf_op jit(solution)/shard_map/ppermute | solution.py:518
  153.3 12.2 %collective-permute-start.6 = (f32[256,256]{1,0:T(8,128)}, f32[256,256]{1,0:T(8,128)S(1)}, u32[]{:S(2)}, u32[]{:S(2)}) collective-permute-start(f32[256,256]{1,0:T(8,128)} %get-tuple-element.34), channel_id=1, source_target_pairs={{0,16},{4,20},{8,24},{12,28},{16,0},{20,4},{24,8},{28,12},{1,17},{... | collective-permute-start | bytes 786440 | tf_op jit(solution)/shard_map/ppermute | solution.py:518
  154.8 23.2 %collective-permute-start.7 = (f32[256,256]{1,0:T(8,128)}, f32[256,256]{1,0:T(8,128)S(1)}, u32[]{:S(2)}, u32[]{:S(2)}) collective-permute-start(f32[256,256]{1,0:T(8,128)} %get-tuple-element.35), channel_id=1, source_target_pairs={{0,20},{4,16},{8,28},{12,24},{16,4},{20,0},{24,12},{28,8},{1,21},{... | collective-permute-start | bytes 786440 | tf_op jit(solution)/shard_map/ppermute | solution.py:518
  155.0 23.1 %copy-start.11 = (f32[256,256]{1,0:T(8,128)}, f32[256,256]{1,0:T(8,128)S(1)}, u32[]{:S(2)}) copy-start(f32[256,256]{1,0:T(8,128)S(1)} %collective-permute-done.3.refs_1_) | copy-start | bytes 786436
  155.0 23.1 %collective-permute-start.8 = (f32[256,256]{1,0:T(8,128)}, f32[256,256]{1,0:T(8,128)}, u32[]{:S(2)}, u32[]{:S(2)}) collective-permute-start(f32[256,256]{1,0:T(8,128)} %get-tuple-element.36), channel_id=1, source_target_pairs={{0,24},{4,28},{8,16},{12,20},{16,8},{20,12},{24,0},{28,4},{1,25},{... | collective-permute-start | bytes 786440 | tf_op jit(solution)/shard_map/ppermute | solution.py:518
  160.9 17.2 %copy-start.12 = (f32[256,256]{1,0:T(8,128)}, f32[256,256]{1,0:T(8,128)S(1)}, u32[]{:S(2)}) copy-start(f32[256,256]{1,0:T(8,128)S(1)} %collective-permute-done.4.refs_2_) | copy-start | bytes 786436
  160.9 17.2 %collective-permute-start.9 = (f32[256,256]{1,0:T(8,128)}, f32[256,256]{1,0:T(8,128)}, u32[]{:S(2)}, u32[]{:S(2)}) collective-permute-start(f32[256,256]{1,0:T(8,128)} %get-tuple-element.37), channel_id=1, source_target_pairs={{0,28},{4,24},{8,20},{12,16},{16,12},{20,8},{24,4},{28,0},{1,29},{... | collective-permute-start | bytes 786440 | tf_op jit(solution)/shard_map/ppermute | solution.py:518
  165.5 12.6 %copy-start.13 = (f32[256,256]{1,0:T(8,128)}, f32[256,256]{1,0:T(8,128)S(1)}, u32[]{:S(2)}) copy-start(f32[256,256]{1,0:T(8,128)S(1)} %collective-permute-done.5.refs_3_) | copy-start | bytes 786436
  165.5 12.6 %copy-start.14 = (f32[256,256]{1,0:T(8,128)}, f32[256,256]{1,0:T(8,128)S(1)}, u32[]{:S(2)}) copy-start(f32[256,256]{1,0:T(8,128)S(1)} %collective-permute-done.6.refs_4_) | copy-start | bytes 786436
  189.3 101.5 %all-to-all-start = ((f32[32,128,128]{2,1,0:T(8,128)}), f32[32,128,128]{2,1,0:T(8,128)}, u32[]{:S(2)}, u32[]{:S(2)}) async-start(f32[32,128,128]{2,1,0:T(8,128)} %x_second.1), calls=%async_computation | async-start | bytes 4194304 | tf_op jit(solution)/shard_map/all_to_all | solution.py:548
  202.6 37.7 %collective-permute-start.17 = (f32[2,4,32,512]{3,2,1,0:T(8,128)}, f32[2,4,32,512]{3,2,1,0:T(8,128)S(1)}, u32[]{:S(2)}, u32[]{:S(2)}) collective-permute-start(f32[2,4,32,512]{3,2,1,0:T(8,128)} %get-tuple-element.46), channel_id=1, source_target_pairs={{0,1},{1,0},{2,3},{3,2},{4,5},{5,4},{6,7},{7,6},{8,9},{9,8},{10,11... | collective-permute-start | bytes 1572872 | tf_op jit(solution)/shard_map/ppermute | solution.py:518
  203.2 70.1 %collective-permute-start.18 = (f32[2,4,32,512]{3,2,1,0:T(8,128)}, f32[2,4,32,512]{3,2,1,0:T(8,128)S(1)}, u32[]{:S(2)}, u32[]{:S(2)}) collective-permute-start(f32[2,4,32,512]{3,2,1,0:T(8,128)} %get-tuple-element.47), channel_id=1, source_target_pairs={{0,2},{1,3},{2,0},{3,1},{4,6},{5,7},{6,4},{7,5},{8,10},{9,11},{10,... | collective-permute-start | bytes 1572872 | tf_op jit(solution)/shard_map/ppermute | solution.py:518
  205.6 80.4 %collective-permute-start.19 = (f32[2,4,32,512]{3,2,1,0:T(8,128)}, f32[2,4,32,512]{3,2,1,0:T(8,128)S(1)}, u32[]{:S(2)}, u32[]{:S(2)}) collective-permute-start(f32[2,4,32,512]{3,2,1,0:T(8,128)} %get-tuple-element.48), channel_id=1, source_target_pairs={{0,3},{1,2},{2,1},{3,0},{4,7},{5,6},{6,5},{7,4},{8,11},{9,10},{10,... | collective-permute-start | bytes 1572872 | tf_op jit(solution)/shard_map/ppermute | solution.py:518
  240.3 45.7 %copy-start.3 = (f32[2,4,32,512]{3,2,1,0:T(8,128)}, f32[2,4,32,512]{3,2,1,0:T(8,128)S(1)}, u32[]{:S(2)}) copy-start(f32[2,4,32,512]{3,2,1,0:T(8,128)S(1)} %collective-permute-done.17.refs_1_) | copy-start | bytes 1572868
  273.3 12.7 %copy-start.4 = (f32[2,4,32,512]{3,2,1,0:T(8,128)}, f32[2,4,32,512]{3,2,1,0:T(8,128)S(1)}, u32[]{:S(2)}) copy-start(f32[2,4,32,512]{3,2,1,0:T(8,128)S(1)} %collective-permute-done.18.refs_2_) | copy-start | bytes 1572868
  (12 other events, 23.9 us)
where the time goes:
time: 297 us; the launch traced here: 296 us
  waiting for transfers between devices  192 us (65%)
  Pallas kernels  54.6 us (18%)
  starting transfers between devices  30.4 us (10%)
  other arithmetic  14.3 us (5%)
  local copies, waits for them, and re-layouts  4.86 us (2%)
    ppermute x20, waiting for transfers between devices, exchange(): lax.ppermute(block, axis, [(at, at ^ step) for at in range(size)])  192 us
    ppermute x20, starting transfers between devices, exchange(): lax.ppermute(block, axis, [(at, at ^ step) for at in range(size)])  19.9 us
    pallas_call x1, Pallas kernels, y_first(): pl.pallas_call(partial(y_first_body, scale), grid_spec=pltpu.PrefetchScal...  12.3 us
    pallas_call x1, Pallas kernels, y_lines(): pl.pallas_call(y_body, grid_spec=pltpu.PrefetchScalarGridSpec(num_scalar_...  9.24 us
    pallas_call x1, Pallas kernels, x_lines(): pl.pallas_call(x_body, grid_spec=pltpu.PrefetchScalarGridSpec(num_scalar_...  9.23 us
    pallas_call x1, Pallas kernels, x_second(): pl.pallas_call(x_second_body, grid_spec=pltpu.PrefetchScalarGridSpec(num_...  9.15 us
    all_to_all x1, starting transfers between devices, fast_shards(): lax.all_to_all(spectra, whole, split_axis=0, concat_axis=0, tiled=True)  6.33 us
  transfers between devices with their start and end apart: 22, of which 11 were waited for; matrix products, arithmetic and copies ran while one was open for 5% of the time, Pallas kernels for 13%

commit v1 on v0

--- a/solution.py
+++ b/solution.py
@@ -12,6 +12,7 @@
 X_RADIX = 8
 Y_RADIX = 4
 HALVES = 2
+PIECES = 2
 LANES = 128
 
 
@@ -89,9 +90,10 @@
     )(me, *([fields] * (gx - 1)))
 
 
-def x_body(me_ref, where_ref, own_ref, *refs):
+def x_body(gy, me_ref, where_ref, own_ref, *refs):
     others = refs[: X_RADIX - 1]
-    table_ref, out_ref, line_ref, real_ref, imag_ref = refs[X_RADIX - 1 :]
+    table_ref, line_ref, real_ref, imag_ref = refs[X_RADIX - 1], *refs[X_RADIX + PIECES :]
+    outs = refs[X_RADIX : X_RADIX + PIECES]
     me = me_ref[0]
     line_ref[me] = own_ref[0]
     for step, ref in enumerate(others, 1):
@@ -128,19 +130,21 @@
             real_ref[rows_e] = cos_e[:, :lanes] - sin_e[:, lanes:]
             imag_ref[rows_e] = -cos_e[:, lanes:] - sin_e[:, :lanes]
 
-    count, _, rows, _ = out_ref.shape
+    count, _, rows, _ = outs[0].shape
 
     def place(to, carry):
-        for row in range(rows):
-            source = where_ref[to * rows + row]
-            out_ref[to, 0, pl.ds(row, 1), :] = real_ref[pl.ds(source, 1), :]
-            out_ref[to, 1, pl.ds(row, 1), :] = imag_ref[pl.ds(source, 1), :]
+        start = to // gy * (gy * PIECES) + to % gy
+        for piece, out_ref in enumerate(outs):
+            for row in range(rows):
+                source = where_ref[(start + piece * gy) * rows + row]
+                out_ref[to, 0, pl.ds(row, 1), :] = real_ref[pl.ds(source, 1), :]
+                out_ref[to, 1, pl.ds(row, 1), :] = imag_ref[pl.ds(source, 1), :]
         return carry
 
     lax.fori_loop(0, count, place, 0)
 
 
-def x_lines(me, where, fields, first, columns, others, table, count):
+def x_lines(me, where, fields, first, columns, others, table, gx, gy):
     _, rows, width = fields.shape
     lanes = width // columns
     kept = where.shape[0]
@@ -149,23 +153,23 @@
         return (first + me_ref[0] // columns, 0, me_ref[0] % columns)
 
     whole = lambda *shape: pl.BlockSpec(shape, lambda *_: (0,) * len(shape))
-    out = (count, 2, kept // count, lanes)
+    out = (gx * gy, 2, kept // (gx * gy * PIECES), lanes)
     return pl.pallas_call(
-        x_body,
+        partial(x_body, gy),
         grid_spec=pltpu.PrefetchScalarGridSpec(
             num_scalar_prefetch=2,
             grid=(1,),
             in_specs=[pl.BlockSpec((1, rows, lanes), own)]
             + [whole(rows, lanes)] * len(others)
             + [whole(*table.shape)],
-            out_specs=whole(*out),
+            out_specs=[whole(*out)] * PIECES,
             scratch_shapes=[
                 pltpu.VMEM((X_RADIX, rows, lanes), jnp.float32),
                 pltpu.VMEM((kept, lanes), jnp.float32),
                 pltpu.VMEM((kept, lanes), jnp.float32),
             ],
         ),
-        out_shape=jax.ShapeDtypeStruct(out, jnp.float32),
+        out_shape=[jax.ShapeDtypeStruct(out, jnp.float32)] * PIECES,
         name="x_lines",
     )(me, where, fields, *others, table)
 
@@ -203,9 +207,9 @@
                     at = pl.ds((c * 2 + part) * block + level * rows, rows)
                     high_ref[at, span] = high
                     low_ref[at, span] = low
+    whole = dot(high_ref[...], table_ref[0]) + dot(low_ref[...], table_ref[0]) + dot(high_ref[...], table_ref[1])
     for c in range(Y_RADIX):
-        at = pl.ds(c * 2 * block, 2 * block)
-        product = dot(high_ref[at], table_ref[0]) + dot(low_ref[at], table_ref[0]) + dot(high_ref[at], table_ref[1])
+        product = whole[c * 2 * block : (c + 1) * 2 * block]
         real = product[:block, :short] + product[block:, short:]
         imag = product[block:, :short] - product[:block, short:]
         for to in range(Y_RADIX):
@@ -264,8 +268,9 @@
             out_ref[part, 0, at, :] = ref[part, 0] * weight
 
 
-def finish(me, blocks, kept_mask, first, stack_count, before):
+def finish(me, blocks, kept_mask, piece, stack_count, before):
     _, levels, rows, width = blocks[0].shape
+    rows_out = rows * Y_RADIX
     block = pl.BlockSpec((2, 1, rows, width), lambda level, me_ref: (0, level, 0, 0))
     extra = [] if before is None else [before]
     return pl.pallas_call(
@@ -274,10 +279,10 @@
             num_scalar_prefetch=1,
             grid=(levels,),
             in_specs=[block] * Y_RADIX
-            + [pl.BlockSpec(kept_mask.shape, lambda level, me_ref: (0, 0))]
+            + [pl.BlockSpec((rows_out, width), lambda level, me_ref: (piece, 0))]
             + [pl.BlockSpec(memory_space=pl.ANY)] * len(extra),
             out_specs=pl.BlockSpec(
-                (2, 1) + kept_mask.shape, lambda level, me_ref: (0, first + level, 0, 0)
+                (2, 1, rows_out, width), lambda level, me_ref: (0, level, piece, 0)
             ),
         ),
         out_shape=jax.ShapeDtypeStruct((2, stack_count) + kept_mask.shape, jnp.float32),
@@ -535,20 +540,25 @@
     second = levels
     fields_second = exchange(pack(y_me, fields, second, 1), "gy", gy)
     lines = exchange(pack(x_me, fields, 0, columns), "gx", gx)
-    table_x = x_table(nx, kept, zero)
-    table_y = y_table(ny, scale, zero)
-    twiddles = y_twiddles(ny, zero)
-    spectra = x_lines(x_me, where, fields, 0, columns, lines, table_x, gx * gy)
-    spectra = lax.all_to_all(spectra, whole, split_axis=0, concat_axis=0, tiled=True)
+    tables = x_table(nx, kept, zero), y_table(ny, scale, zero), y_twiddles(ny, zero)
+    table_x, table_y, twiddles = lax.optimization_barrier(tables)
+    spectra = x_lines(x_me, where, fields, 0, columns, lines, table_x, gx, gy)
+    spectra = list(spectra)
+    for piece in range(PIECES):
+        spectra[piece] = lax.all_to_all(spectra[piece], whole, split_axis=0, concat_axis=0, tiled=True)
     half_waves = y_first(both_me, scale, fields, second, fields_second, twiddles, table_y)
     half_waves = [half_waves[0]] + exchange(half_waves[1:], "gx", gx)
-    waves = y_lines(y_me, spectra, twiddles, table_y)
-    waves = [waves[0]] + exchange(waves[1:], "gy", gy)
     owned = x_second(x_me, where, half_waves, table_x, gx)
     owned = lax.all_to_all(owned, whole, split_axis=0, concat_axis=0, tiled=True)
-    result = finish(y_me, waves, kept_mask, 0, stack_count, None)
-    owned = owned.reshape((gx, gy) + owned.shape[1:])
-    return finish_second(y_me, owned, kept_mask, second, result)
+    result = None
+    for piece in range(PIECES):
+        waves = y_lines(y_me, spectra[piece], twiddles, table_y)
+        waves = [waves[0]] + exchange(waves[1:], "gy", gy)
+        if piece == PIECES - 1:
+            owned = owned.reshape((gx, gy) + owned.shape[1:])
+            result = finish_second(y_me, owned, kept_mask, second, result)
+        result = finish(y_me, waves, kept_mask, piece, stack_count, result)
+    return result
 
 
 def wave_angles(wave_ids, points, period):
@@ -611,7 +621,7 @@
         and nx % (X_RADIX * LANES) == 0
         and kept % (X_RADIX * LANES) == 0
         and kept <= nx
-        and kept // (gx * gy) % 16 == 0
+        and kept // (gx * gy) % (16 * PIECES) == 0
     )
 
 

time: 297 us -> 302 us (1.017)
  the two profiles are of different devices: /device:TPU:8 before, /device:TPU:0 now
where the time goes in v1:
time: 302 us; the launch traced here: 299 us
  waiting for transfers between devices  137 us (45%)
  Pallas kernels  60.9 us (20%)
  starting transfers between devices  48.6 us (16%)
  blocking collectives  31.2 us (10%)
  other arithmetic  14.2 us (5%)
  local copies, waits for them, and re-layouts  7.09 us (2%)
    ppermute x23, waiting for transfers between devices, exchange(): lax.ppermute(block, axis, [(at, at ^ step) for at in range(size)])  137 us
    all_to_all x1, blocking collectives, fast_shards(): lax.all_to_all(spectra[piece], whole, split_axis=0, concat_axis=0, tiled=...  31.2 us
    ppermute x23, starting transfers between devices, exchange(): lax.ppermute(block, axis, [(at, at ^ step) for at in range(size)])  31.1 us
    all_to_all x1, starting transfers between devices, fast_shards(): lax.all_to_all(owned, whole, split_axis=0, concat_axis=0, tiled=True)  12.9 us
    pallas_call x1, Pallas kernels, y_first(): pl.pallas_call(partial(y_first_body, scale), grid_spec=pltpu.PrefetchScal...  12.4 us
    pallas_call x2, Pallas kernels, y_lines(): pl.pallas_call(y_body, grid_spec=pltpu.PrefetchScalarGridSpec(num_scalar_...  12 us
    pallas_call x1, Pallas kernels, x_lines(): pl.pallas_call(partial(x_body, gy), grid_spec=pltpu.PrefetchScalarGridSpe...  9.6 us
    pallas_call x1, Pallas kernels, x_second(): pl.pallas_call(x_second_body, grid_spec=pltpu.PrefetchScalarGridSpec(num_...  9.17 us
  transfers between devices with their start and end apart: 25, of which 10 were waited for; matrix products, arithmetic and copies ran while one was open for 5% of the time, Pallas kernels for 15%

profile of v1, /device:TPU:0, one launch (start us, length us, event | category | flops | bytes accessed | tf_op | source)
XLA Modules:
  0.0 299.1 jit_solution(15747079758474024475)
XLA Ops:
  0.0 2.7 pack.2
  3.2 2.5 collective-permute-start.1
  5.8 1.8 collective-permute-start.3
  7.7 4.1 %fusion.9 = (f32[4,2,1,128,256]{4,3,2,1,0:T(8,128)S(1)}, f32[4,2,1,128,256]{4,3,2,1,0:T(8,128)S(1)}) fusion(s32[256]{0:T(256)S(1)} %iota_add_fusion.1, s32[4,2,128]{2,1,0:T(2,128)S(1)} %broadcast_add_fusion), kind=kLoop, calls=%fused_computation.29 | loop fusion | flops 3670016 | bytes 2102272 | tf_op jit(solution)/shard_map/cos | solution.py:21
  12.4 4.1 %cosine_bitcast_fusion = (f32[1,512,512]{2,1,0:T(8,128)S(1)}, f32[1,512,512]{2,1,0:T(8,128)S(1)}) fusion(s32[512]{0:T(512)S(1)} %iota_add_fusion), kind=kLoop, calls=%fused_computation.27 | loop fusion | flops 3670016 | bytes 2099200 | tf_op jit(solution)/shard_map/concatenate | solution.py:43
  20.1 2.6 collective-permute-start.5
  24.2 6.1 %collective-permute-done.5.refs_5_ = f32[256,256]{1,0:T(8,128)S(1)} collective-permute-done((f32[256,256]{1,0:T(8,128)S(1)}, f32[256,256]{1,0:T(8,128)S(1)}, u32[]{:S(2)}, u32[]{:S(2)}) %collective-permute-start.5) | collective-permute-done | bytes 262176 | tf_op jit(solution)/shard_map/ppermute | solution.py:523
  30.3 4.5 %collective-permute-done.6.refs_6_ = f32[256,256]{1,0:T(8,128)S(1)} collective-permute-done((f32[256,256]{1,0:T(8,128)S(1)}, f32[256,256]{1,0:T(8,128)S(1)}, u32[]{:S(2)}, u32[]{:S(2)}) %collective-permute-start.6) | collective-permute-done | bytes 262176 | tf_op jit(solution)/shard_map/ppermute | solution.py:523
  35.6 9.6 %x_lines.1 = (f32[32,2,16,256]{3,2,1,0:T(8,128)}, f32[32,2,16,256]{3,2,1,0:T(8,128)}) custom-call(s32[1]{0:T(128)} %bitcast.1.me_ref, s32[1024]{0:T(1024)} %fusion.14.where_ref, f32[8,256,512]{2,1,0:T(8,128)} %own_ref.3, f32[256,256]{1,0:T(8,128)} %copy-done.17, f32[256,256]{1,0:T(8,128)} %copy-done.18, f32[256,256]{1,0:T(8,128)} %copy-done.19, ...), custom_call_target="tpu_custom_call" | custom-call | tf_op jit(solution)/shard_map/x_lines/pallas_call | solution.py:157
  45.2 31.2 %all_to_all.15.in_ref = f32[32,2,16,256]{3,2,1,0:T(8,128)} all-to-all(f32[32,2,16,256]{3,2,1,0:T(8,128)} %get-tuple-element.44), channel_id=1, replica_groups=mesh['gx'=8,'gy'=4] {'gx','gy'}, dimensions={0} | all-to-all | bytes 2097152 | tf_op jit(solution)/shard_map/all_to_all | solution.py:548
  76.3 4.6 %all-to-all-start.2 = ((f32[32,2,16,256]{3,2,1,0:T(8,128)}), f32[32,2,16,256]{3,2,1,0:T(8,128)S(1)}, u32[]{:S(2)}, u32[]{:S(2)}) async-start(f32[32,2,16,256]{3,2,1,0:T(8,128)} %get-tuple-element.62), calls=%async_computation.2 | async-start | bytes 2097152 | tf_op jit(solution)/shard_map/all_to_all | solution.py:548
  80.9 2.5 pack.3
  85.2 2.4 collective-permute-start.11
  88.4 30.1 %collective-permute-done.10.refs_0_ = f32[256,512]{1,0:T(8,128)S(1)} collective-permute-done((f32[256,512]{1,0:T(8,128)}, f32[256,512]{1,0:T(8,128)S(1)}, u32[]{:S(2)}, u32[]{:S(2)}) %collective-permute-start.10) | collective-permute-done | bytes 524320 | tf_op jit(solution)/shard_map/ppermute | solution.py:523
  118.5 22.9 %collective-permute-done.11.refs_1_ = f32[256,512]{1,0:T(8,128)S(1)} collective-permute-done((f32[256,512]{1,0:T(8,128)}, f32[256,512]{1,0:T(8,128)S(1)}, u32[]{:S(2)}, u32[]{:S(2)}) %collective-permute-start.11) | collective-permute-done | bytes 524320 | tf_op jit(solution)/shard_map/ppermute | solution.py:523
  142.9 12.4 %y_first.1 = (f32[256,256]{1,0:T(8,128)}, f32[256,256]{1,0:T(8,128)}, f32[256,256]{1,0:T(8,128)}, f32[256,256]{1,0:T(8,128)}, f32[256,256]{1,0:T(8,128)}, /*inde...) custom-call(s32[2]{0:T(128)} %pad_add_fusion.me_ref, f32[8,256,512]{2,1,0:T(8,128)} %own_ref.3, ...), custom_call_target="tpu_custom_call" | custom-call | tf_op jit(solution)/shard_map/y_first/pallas_call | solution.py:365
  158.9 2.4 collective-permute-start.18
  161.3 3.5 %collective-permute-done.14.refs_2_ = f32[256,256]{1,0:T(8,128)S(1)} collective-permute-done((f32[256,256]{1,0:T(8,128)}, f32[256,256]{1,0:T(8,128)S(1)}, u32[]{:S(2)}, u32[]{:S(2)}) %collective-permute-start.14) | collective-permute-done | bytes 262176 | tf_op jit(solution)/shard_map/ppermute | solution.py:523
  165.9 3.6 %collective-permute-done.15.refs_3_ = f32[256,256]{1,0:T(8,128)S(1)} collective-permute-done((f32[256,256]{1,0:T(8,128)}, f32[256,256]{1,0:T(8,128)S(1)}, u32[]{:S(2)}, u32[]{:S(2)}) %collective-permute-start.15) | collective-permute-done | bytes 262176 | tf_op jit(solution)/shard_map/ppermute | solution.py:523
  169.5 12.7 %collective-permute-done.17.refs_5_ = f32[256,256]{1,0:T(8,128)S(1)} collective-permute-done((f32[256,256]{1,0:T(8,128)}, f32[256,256]{1,0:T(8,128)S(1)}, u32[]{:S(2)}, u32[]{:S(2)}) %collective-permute-start.17) | collective-permute-done | bytes 262176 | tf_op jit(solution)/shard_map/ppermute | solution.py:523
  183.1 9.2 %x_second.1 = f32[32,128,128]{2,1,0:T(8,128)} custom-call(s32[1]{0:T(128)} %bitcast.1.me_ref, s32[1024]{0:T(1024)} %fusion.14.where_ref, f32[256,256]{1,0:T(8,128)} %get-tuple-element.54.refs_0_, f32[256,256]{1,0:T(8,128)} %copy-done.5, f32[256,256]{1,0:T(8,128)} %copy-done.6, f32[256,256]{1,0:T(8,128)} %copy-done.7, f32[256,256]{1,0:T(8,128)} %copy-done.9, ...), custom_call_target="tpu_custom_call" | custom-call | tf_op jit(solution)/shard_map/x_second/pallas_call | solution.py:455
  193.3 12.9 %all-to-all-start.1 = ((f32[32,128,128]{2,1,0:T(8,128)}), f32[32,128,128]{2,1,0:T(8,128)S(1)}, u32[]{:S(2)}, u32[]{:S(2)}) async-start(f32[32,128,128]{2,1,0:T(8,128)} %x_second.1), calls=%async_computation.1 | async-start | bytes 4194304 | tf_op jit(solution)/shard_map/all_to_all | solution.py:552
  206.2 6.0 %y_lines.3 = (f32[2,4,16,512]{3,2,1,0:T(8,128)}, f32[2,4,16,512]{3,2,1,0:T(8,128)}, f32[2,4,16,512]{3,2,1,0:T(8,128)}, f32[2,4,16,512]{3,2,1,0:T(8,128)}) custom-call(s32[1]{0:T(128)} %bitcast.me_ref, f32[32,2,16,256]{3,2,1,0:T(8,128)} %copy-done.1, f32[8,512]{1,0:T(8,128)} %pad_maximum_fusion.3.twiddle_ref.refs_3_, ...), custom_call_target="tpu_custom_call" | custom-call | tf_op jit(solution)/shard_map/y_lines/pallas_call | solution.py:243
  213.8 2.4 collective-permute-start.21
  216.6 6.0 %y_lines.2 = (f32[2,4,16,512]{3,2,1,0:T(8,128)}, f32[2,4,16,512]{3,2,1,0:T(8,128)}, f32[2,4,16,512]{3,2,1,0:T(8,128)}, f32[2,4,16,512]{3,2,1,0:T(8,128)}) custom-call(s32[1]{0:T(128)} %bitcast.me_ref, f32[32,2,16,256]{3,2,1,0:T(8,128)} %all_to_all.15.in_ref, f32[8,512]{1,0:T(8,128)} %pad_maximum_fusion.3.twiddle_ref.refs_3_, ...), custom_call_target="tpu_custom_call" | custom-call | tf_op jit(solution)/shard_map/y_lines/pallas_call | solution.py:243
  223.3 3.3 %collective-permute-start.8 = (f32[2,4,16,512]{3,2,1,0:T(8,128)}, f32[2,4,16,512]{3,2,1,0:T(8,128)S(1)}, u32[]{:S(2)}, u32[]{:S(2)}) collective-permute-start(f32[2,4,16,512]{3,2,1,0:T(8,128)} %get-tuple-element.49), channel_id=1, source_target_pairs={{0,2},{1,3},{2,0},{3,1},{4,6},{5,7},{6,4},{7,5},{8,10},{9,11},{10,... | collective-permute-start | bytes 786440 | tf_op jit(solution)/shard_map/ppermute | solution.py:523
  226.6 20.1 %collective-permute-done.20.refs_1_ = f32[2,4,16,512]{3,2,1,0:T(8,128)S(1)} collective-permute-done((f32[2,4,16,512]{3,2,1,0:T(8,128)}, f32[2,4,16,512]{3,2,1,0:T(8,128)S(1)}, u32[]{:S(2)}, u32[]{:S(2)}) %collective-permute-start.20) | collective-permute-done | bytes 262176 | tf_op jit(solution)/shard_map/ppermute | solution.py:523
  246.7 3.6 %collective-permute-start.9 = (f32[2,4,16,512]{3,2,1,0:T(8,128)}, f32[2,4,16,512]{3,2,1,0:T(8,128)S(1)}, u32[]{:S(2)}, u32[]{:S(2)}) collective-permute-start(f32[2,4,16,512]{3,2,1,0:T(8,128)} %get-tuple-element.50), channel_id=1, source_target_pairs={{0,3},{1,2},{2,1},{3,0},{4,7},{5,6},{6,5},{7,4},{8,11},{9,10},{10,... | collective-permute-start | bytes 786440 | tf_op jit(solution)/shard_map/ppermute | solution.py:523
  250.3 33.2 %collective-permute-done.21.refs_2_ = f32[2,4,16,512]{3,2,1,0:T(8,128)S(1)} collective-permute-done((f32[2,4,16,512]{3,2,1,0:T(8,128)}, f32[2,4,16,512]{3,2,1,0:T(8,128)S(1)}, u32[]{:S(2)}, u32[]{:S(2)}) %collective-permute-start.21) | collective-permute-done | bytes 262176 | tf_op jit(solution)/shard_map/ppermute | solution.py:523
  284.3 3.5 %finish.2.before_ref = f32[2,8,128,512]{3,2,1,0:T(8,128)} custom-call(s32[1]{0:T(128)} %bitcast.me_ref, f32[2,4,16,512]{3,2,1,0:T(8,128)} %get-tuple-element.63.refs_0_, f32[2,4,16,512]{3,2,1,0:T(8,128)} %copy-done.12, f32[2,4,16,512]{3,2,1,0:T(8,128)} %copy-done.13, f32[2,4,16,512]{3,2,1,0:T(8,128)} %collective-permute-done.22.refs_3_, s32[128,512]{1,0:T(8,128)} %refs_4_.5), custom_call_target="tpu_custom_call" | custom-call | tf_op jit(solution)/shard_map/finish/pallas_call | solution.py:276
  289.1 5.5 %finish_second.1.refs_5_ = f32[2,8,128,512]{3,2,1,0:T(8,128)} custom-call(s32[1]{0:T(128)} %bitcast.me_ref, f32[8,4,128,128]{3,2,1,0:T(8,128)} %bitcast.10, s32[128,512]{1,0:T(8,128)} %refs_4_.5, f32[2,8,128,512]{3,2,1,0:T(8,128)} %finish.2.before_ref), custom_call_target="tpu_custom_call", output_to_operand_aliasing={{}: (3, {})} | custom-call | tf_op jit(solution)/shard_map/finish_second/pallas_call | solution.py:501
  295.6 3.5 %finish.3 = f32[2,8,128,512]{3,2,1,0:T(8,128)} custom-call(s32[1]{0:T(128)} %bitcast.me_ref, f32[2,4,16,512]{3,2,1,0:T(8,128)} %get-tuple-element.47.refs_0_, f32[2,4,16,512]{3,2,1,0:T(8,128)} %copy-done.8, f32[2,4,16,512]{3,2,1,0:T(8,128)} %copy-done.10, f32[2,4,16,512]{3,2,1,0:T(8,128)} %copy-done.14, ...), custom_call_target="tpu_custom_call", output_to_operand_aliasing={{}: (6, {})} | custom-call | tf_op jit(solution)/shard_map/finish/pallas_call | solution.py:276
  (100 shorter events, 23.3 us)
Async XLA Ops:
  2.7 17.4 %collective-permute-start = (f32[256,256]{1,0:T(8,128)}, f32[256,256]{1,0:T(8,128)S(1)}, u32[]{:S(2)}, u32[]{:S(2)}) collective-permute-start(f32[256,256]{1,0:T(8,128)} %get-tuple-element.36), channel_id=1, source_target_pairs={{0,4},{4,0},{8,12},{12,8},{16,20},{20,16},{24,28},{28,24},{1,5},{5... | collective-permute-start | bytes 786440 | tf_op jit(solution)/shard_map/ppermute | solution.py:523
  3.2 19.5 %collective-permute-start.1 = (f32[256,256]{1,0:T(8,128)}, f32[256,256]{1,0:T(8,128)S(1)}, u32[]{:S(2)}, u32[]{:S(2)}) collective-permute-start(f32[256,256]{1,0:T(8,128)} %get-tuple-element.37), channel_id=1, source_target_pairs={{0,8},{4,12},{8,0},{12,4},{16,24},{20,28},{24,16},{28,20},{1,9},{5... | collective-permute-start | bytes 786440 | tf_op jit(solution)/shard_map/ppermute | solution.py:523
  5.7 18.5 %collective-permute-start.2 = (f32[256,256]{1,0:T(8,128)}, f32[256,256]{1,0:T(8,128)S(1)}, u32[]{:S(2)}, u32[]{:S(2)}) collective-permute-start(f32[256,256]{1,0:T(8,128)} %get-tuple-element.38), channel_id=1, source_target_pairs={{0,12},{4,8},{8,4},{12,0},{16,28},{20,24},{24,20},{28,16},{1,13},{... | collective-permute-start | bytes 786440 | tf_op jit(solution)/shard_map/ppermute | solution.py:523
  5.8 18.4 %collective-permute-start.3 = (f32[256,256]{1,0:T(8,128)}, f32[256,256]{1,0:T(8,128)S(1)}, u32[]{:S(2)}, u32[]{:S(2)}) collective-permute-start(f32[256,256]{1,0:T(8,128)} %get-tuple-element.39), channel_id=1, source_target_pairs={{0,16},{4,20},{8,24},{12,28},{16,0},{20,4},{24,8},{28,12},{1,17},{... | collective-permute-start | bytes 786440 | tf_op jit(solution)/shard_map/ppermute | solution.py:523
  7.6 16.6 %collective-permute-start.4 = (f32[256,256]{1,0:T(8,128)}, f32[256,256]{1,0:T(8,128)S(1)}, u32[]{:S(2)}, u32[]{:S(2)}) collective-permute-start(f32[256,256]{1,0:T(8,128)} %get-tuple-element.40), channel_id=1, source_target_pairs={{0,20},{4,16},{8,28},{12,24},{16,4},{20,0},{24,12},{28,8},{1,21},{... | collective-permute-start | bytes 786440 | tf_op jit(solution)/shard_map/ppermute | solution.py:523
  20.1 14.7 %copy-start.17 = (f32[256,256]{1,0:T(8,128)}, f32[256,256]{1,0:T(8,128)S(1)}, u32[]{:S(2)}) copy-start(f32[256,256]{1,0:T(8,128)S(1)} %collective-permute-done.refs_0_) | copy-start | bytes 786436
  20.1 10.1 %collective-permute-start.5 = (f32[256,256]{1,0:T(8,128)S(1)}, f32[256,256]{1,0:T(8,128)S(1)}, u32[]{:S(2)}, u32[]{:S(2)}) collective-permute-start(f32[256,256]{1,0:T(8,128)S(1)} %copy-done.27), channel_id=1, source_target_pairs={{0,24},{4,28},{8,16},{12,20},{16,8},{20,12},{24,0},{28,4},{1,25},{... | collective-permute-start | bytes 786440 | tf_op jit(solution)/shard_map/ppermute | solution.py:523
  22.8 12.0 %collective-permute-start.6 = (f32[256,256]{1,0:T(8,128)S(1)}, f32[256,256]{1,0:T(8,128)S(1)}, u32[]{:S(2)}, u32[]{:S(2)}) collective-permute-start(f32[256,256]{1,0:T(8,128)S(1)} %copy-done.26), channel_id=1, source_target_pairs={{0,28},{4,24},{8,20},{12,16},{16,12},{20,8},{24,4},{28,0},{1,29},{... | collective-permute-start | bytes 786440 | tf_op jit(solution)/shard_map/ppermute | solution.py:523
  76.3 116.0 %all-to-all-start.2 = ((f32[32,2,16,256]{3,2,1,0:T(8,128)}), f32[32,2,16,256]{3,2,1,0:T(8,128)S(1)}, u32[]{:S(2)}, u32[]{:S(2)}) async-start(f32[32,2,16,256]{3,2,1,0:T(8,128)} %get-tuple-element.62), calls=%async_computation.2 | async-start | bytes 2097152 | tf_op jit(solution)/shard_map/all_to_all | solution.py:548
  83.4 35.0 %collective-permute-start.10 = (f32[256,512]{1,0:T(8,128)}, f32[256,512]{1,0:T(8,128)S(1)}, u32[]{:S(2)}, u32[]{:S(2)}) collective-permute-start(f32[256,512]{1,0:T(8,128)} %get-tuple-element.51), channel_id=1, source_target_pairs={{0,1},{1,0},{2,3},{3,2},{4,5},{5,4},{6,7},{7,6},{8,9},{9,8},{10,11... | collective-permute-start | bytes 1572872 | tf_op jit(solution)/shard_map/ppermute | solution.py:523
  85.2 56.2 %collective-permute-start.11 = (f32[256,512]{1,0:T(8,128)}, f32[256,512]{1,0:T(8,128)S(1)}, u32[]{:S(2)}, u32[]{:S(2)}) collective-permute-start(f32[256,512]{1,0:T(8,128)} %get-tuple-element.52), channel_id=1, source_target_pairs={{0,2},{1,3},{2,0},{3,1},{4,6},{5,7},{6,4},{7,5},{8,10},{9,11},{10,... | collective-permute-start | bytes 1572872 | tf_op jit(solution)/shard_map/ppermute | solution.py:523
  87.6 53.8 %collective-permute-start.12 = (f32[256,512]{1,0:T(8,128)}, f32[256,512]{1,0:T(8,128)S(1)}, u32[]{:S(2)}, u32[]{:S(2)}) collective-permute-start(f32[256,512]{1,0:T(8,128)} %get-tuple-element.53), channel_id=1, source_target_pairs={{0,3},{1,2},{2,1},{3,0},{4,7},{5,6},{6,5},{7,4},{8,11},{9,10},{10,... | collective-permute-start | bytes 1572872 | tf_op jit(solution)/shard_map/ppermute | solution.py:523
  118.5 22.9 %copy-start.2 = (f32[256,512]{1,0:T(8,128)}, f32[256,512]{1,0:T(8,128)S(1)}, u32[]{:S(2)}) copy-start(f32[256,512]{1,0:T(8,128)S(1)} %collective-permute-done.10.refs_0_) | copy-start | bytes 1572868
  155.4 3.5 %collective-permute-start.13 = (f32[256,256]{1,0:T(8,128)}, f32[256,256]{1,0:T(8,128)S(1)}, u32[]{:S(2)}, u32[]{:S(2)}) collective-permute-start(f32[256,256]{1,0:T(8,128)} %get-tuple-element.55), channel_id=1, source_target_pairs={{0,4},{4,0},{8,12},{12,8},{16,20},{20,16},{24,28},{28,24},{1,5},{5... | collective-permute-start | bytes 786440 | tf_op jit(solution)/shard_map/ppermute | solution.py:523
  155.4 9.4 %collective-permute-start.14 = (f32[256,256]{1,0:T(8,128)}, f32[256,256]{1,0:T(8,128)S(1)}, u32[]{:S(2)}, u32[]{:S(2)}) collective-permute-start(f32[256,256]{1,0:T(8,128)} %get-tuple-element.56), channel_id=1, source_target_pairs={{0,8},{4,12},{8,0},{12,4},{16,24},{20,28},{24,16},{28,20},{1,9},{5... | collective-permute-start | bytes 786440 | tf_op jit(solution)/shard_map/ppermute | solution.py:523
  156.9 12.6 %collective-permute-start.15 = (f32[256,256]{1,0:T(8,128)}, f32[256,256]{1,0:T(8,128)S(1)}, u32[]{:S(2)}, u32[]{:S(2)}) collective-permute-start(f32[256,256]{1,0:T(8,128)} %get-tuple-element.57), channel_id=1, source_target_pairs={{0,12},{4,8},{8,4},{12,0},{16,28},{20,24},{24,20},{28,16},{1,13},{... | collective-permute-start | bytes 786440 | tf_op jit(solution)/shard_map/ppermute | solution.py:523
  157.2 12.3 %collective-permute-start.16 = (f32[256,256]{1,0:T(8,128)}, f32[256,256]{1,0:T(8,128)S(1)}, u32[]{:S(2)}, u32[]{:S(2)}) collective-permute-start(f32[256,256]{1,0:T(8,128)} %get-tuple-element.58), channel_id=1, source_target_pairs={{0,16},{4,20},{8,24},{12,28},{16,0},{20,4},{24,8},{28,12},{1,17},{... | collective-permute-start | bytes 786440 | tf_op jit(solution)/shard_map/ppermute | solution.py:523
  158.7 23.5 %collective-permute-start.17 = (f32[256,256]{1,0:T(8,128)}, f32[256,256]{1,0:T(8,128)S(1)}, u32[]{:S(2)}, u32[]{:S(2)}) collective-permute-start(f32[256,256]{1,0:T(8,128)} %get-tuple-element.59), channel_id=1, source_target_pairs={{0,20},{4,16},{8,28},{12,24},{16,4},{20,0},{24,12},{28,8},{1,21},{... | collective-permute-start | bytes 786440 | tf_op jit(solution)/shard_map/ppermute | solution.py:523
  158.9 23.3 %copy-start.5 = (f32[256,256]{1,0:T(8,128)}, f32[256,256]{1,0:T(8,128)S(1)}, u32[]{:S(2)}) copy-start(f32[256,256]{1,0:T(8,128)S(1)} %collective-permute-done.13.refs_1_) | copy-start | bytes 786436
  158.9 23.3 %collective-permute-start.18 = (f32[256,256]{1,0:T(8,128)}, f32[256,256]{1,0:T(8,128)S(1)}, u32[]{:S(2)}, u32[]{:S(2)}) collective-permute-start(f32[256,256]{1,0:T(8,128)} %get-tuple-element.60), channel_id=1, source_target_pairs={{0,24},{4,28},{8,16},{12,20},{16,8},{20,12},{24,0},{28,4},{1,25},{... | collective-permute-start | bytes 786440 | tf_op jit(solution)/shard_map/ppermute | solution.py:523
  164.8 17.4 %copy-start.6 = (f32[256,256]{1,0:T(8,128)}, f32[256,256]{1,0:T(8,128)S(1)}, u32[]{:S(2)}) copy-start(f32[256,256]{1,0:T(8,128)S(1)} %collective-permute-done.14.refs_2_) | copy-start | bytes 786436
  164.8 17.4 %collective-permute-start.19 = (f32[256,256]{1,0:T(8,128)}, f32[256,256]{1,0:T(8,128)S(1)}, u32[]{:S(2)}, u32[]{:S(2)}) collective-permute-start(f32[256,256]{1,0:T(8,128)} %get-tuple-element.61), channel_id=1, source_target_pairs={{0,28},{4,24},{8,20},{12,16},{16,12},{20,8},{24,4},{28,0},{1,29},{... | collective-permute-start | bytes 786440 | tf_op jit(solution)/shard_map/ppermute | solution.py:523
  169.5 12.7 %copy-start.7 = (f32[256,256]{1,0:T(8,128)}, f32[256,256]{1,0:T(8,128)S(1)}, u32[]{:S(2)}) copy-start(f32[256,256]{1,0:T(8,128)S(1)} %collective-permute-done.15.refs_3_) | copy-start | bytes 786436
  169.5 12.7 %copy-start.9 = (f32[256,256]{1,0:T(8,128)}, f32[256,256]{1,0:T(8,128)S(1)}, u32[]{:S(2)}) copy-start(f32[256,256]{1,0:T(8,128)S(1)} %collective-permute-done.16.refs_4_) | copy-start | bytes 786436
  193.3 94.5 %all-to-all-start.1 = ((f32[32,128,128]{2,1,0:T(8,128)}), f32[32,128,128]{2,1,0:T(8,128)S(1)}, u32[]{:S(2)}, u32[]{:S(2)}) async-start(f32[32,128,128]{2,1,0:T(8,128)} %x_second.1), calls=%async_computation.1 | async-start | bytes 4194304 | tf_op jit(solution)/shard_map/all_to_all | solution.py:552
  212.2 34.5 %collective-permute-start.20 = (f32[2,4,16,512]{3,2,1,0:T(8,128)}, f32[2,4,16,512]{3,2,1,0:T(8,128)S(1)}, u32[]{:S(2)}, u32[]{:S(2)}) collective-permute-start(f32[2,4,16,512]{3,2,1,0:T(8,128)} %get-tuple-element.64), channel_id=1, source_target_pairs={{0,1},{1,0},{2,3},{3,2},{4,5},{5,4},{6,7},{7,6},{8,9},{9,8},{10,11... | collective-permute-start | bytes 786440 | tf_op jit(solution)/shard_map/ppermute | solution.py:523
  213.8 69.8 %collective-permute-start.21 = (f32[2,4,16,512]{3,2,1,0:T(8,128)}, f32[2,4,16,512]{3,2,1,0:T(8,128)S(1)}, u32[]{:S(2)}, u32[]{:S(2)}) collective-permute-start(f32[2,4,16,512]{3,2,1,0:T(8,128)} %get-tuple-element.65), channel_id=1, source_target_pairs={{0,2},{1,3},{2,0},{3,1},{4,6},{5,7},{6,4},{7,5},{8,10},{9,11},{10,... | collective-permute-start | bytes 786440 | tf_op jit(solution)/shard_map/ppermute | solution.py:523
  216.2 67.4 %collective-permute-start.22 = (f32[2,4,16,512]{3,2,1,0:T(8,128)}, f32[2,4,16,512]{3,2,1,0:T(8,128)}, u32[]{:S(2)}, u32[]{:S(2)}) collective-permute-start(f32[2,4,16,512]{3,2,1,0:T(8,128)} %get-tuple-element.66), channel_id=1, source_target_pairs={{0,3},{1,2},{2,1},{3,0},{4,7},{5,6},{6,5},{7,4},{8,11},{9,10},{10,... | collective-permute-start | bytes 786440 | tf_op jit(solution)/shard_map/ppermute | solution.py:523
  222.6 72.0 %collective-permute-start.7 = (f32[2,4,16,512]{3,2,1,0:T(8,128)}, f32[2,4,16,512]{3,2,1,0:T(8,128)S(1)}, u32[]{:S(2)}, u32[]{:S(2)}) collective-permute-start(f32[2,4,16,512]{3,2,1,0:T(8,128)} %get-tuple-element.48), channel_id=1, source_target_pairs={{0,1},{1,0},{2,3},{3,2},{4,5},{5,4},{6,7},{7,6},{8,9},{9,8},{10,11... | collective-permute-start | bytes 786440 | tf_op jit(solution)/shard_map/ppermute | solution.py:523
  223.3 71.5 %collective-permute-start.8 = (f32[2,4,16,512]{3,2,1,0:T(8,128)}, f32[2,4,16,512]{3,2,1,0:T(8,128)S(1)}, u32[]{:S(2)}, u32[]{:S(2)}) collective-permute-start(f32[2,4,16,512]{3,2,1,0:T(8,128)} %get-tuple-element.49), channel_id=1, source_target_pairs={{0,2},{1,3},{2,0},{3,1},{4,6},{5,7},{6,4},{7,5},{8,10},{9,11},{10,... | collective-permute-start | bytes 786440 | tf_op jit(solution)/shard_map/ppermute | solution.py:523
  246.7 36.9 %copy-start.12 = (f32[2,4,16,512]{3,2,1,0:T(8,128)}, f32[2,4,16,512]{3,2,1,0:T(8,128)S(1)}, u32[]{:S(2)}) copy-start(f32[2,4,16,512]{3,2,1,0:T(8,128)S(1)} %collective-permute-done.20.refs_1_) | copy-start | bytes 786436
  246.7 48.1 %collective-permute-start.9 = (f32[2,4,16,512]{3,2,1,0:T(8,128)}, f32[2,4,16,512]{3,2,1,0:T(8,128)S(1)}, u32[]{:S(2)}, u32[]{:S(2)}) collective-permute-start(f32[2,4,16,512]{3,2,1,0:T(8,128)} %get-tuple-element.50), channel_id=1, source_target_pairs={{0,3},{1,2},{2,1},{3,0},{4,7},{5,6},{6,5},{7,4},{8,11},{9,10},{10,... | collective-permute-start | bytes 786440 | tf_op jit(solution)/shard_map/ppermute | solution.py:523
  (21 other events, 77.2 us)

commit v2 on v1

--- a/solution.py
+++ b/solution.py
@@ -40,7 +40,9 @@
     short = period // Y_RADIX
     ids = jnp.arange(short, dtype=jnp.int32) + zero
     cos, sin = roots(ids[:, None] * ids[None, :], short)
-    return jnp.stack(two_parts(jnp.concatenate([cos, sin], axis=1) * scale))
+    half = short // 2
+    table = jnp.concatenate([cos[:, :half], sin[:, :half], cos[:, half:], sin[:, half:]], axis=1)
+    return jnp.stack(two_parts(table * scale))
 
 
 def y_twiddles(period, zero):
@@ -49,6 +51,19 @@
     return jnp.concatenate([cos, sin], axis=0)
 
 
+IN_VMEM = pl.BlockSpec(memory_space=pltpu.VMEM)
+IN_HBM = pl.BlockSpec(memory_space=pltpu.HBM)
+LIMIT = pltpu.CompilerParams(vmem_limit_bytes=32 << 20)
+
+
+def in_hbm(array):
+    return pltpu.with_memory_space_constraint(array, pltpu.HBM)
+
+
+def on_chip(*arrays):
+    return [pltpu.with_memory_space_constraint(array, pltpu.VMEM) for array in arrays]
+
+
 def dot(left, right):
     return jnp.dot(left, right, preferred_element_type=jnp.float32)
 
@@ -58,47 +73,63 @@
     return high, (values - high.astype(jnp.float32)).astype(jnp.bfloat16)
 
 
-def pack_body(me_ref, *refs):
-    count = len(refs) // 2
-    for at in range(count):
-        refs[count + at][...] = refs[at][0]
+def copy_all(pairs, semaphore):
+    copies = [
+        pltpu.make_async_copy(source, target, semaphore.at[at])
+        for at, (source, target) in enumerate(pairs)
+    ]
+    for copy in copies:
+        copy.start()
+    return copies
+
+
+def column_block(fields_ref, first, columns, to, lanes):
+    if columns == 1:
+        return fields_ref.at[first + to]
+    start = pl.multiple_of(to % columns * lanes, LANES)
+    return fields_ref.at[first + to // columns, :, pl.ds(start, lanes)]
+
+
+def pack_body(first, columns, me_ref, fields_ref, *refs):
+    outs, semaphore = refs[:-1], refs[-1]
+    lanes = outs[0].shape[1]
+    pairs = [
+        (column_block(fields_ref, first, columns, jnp.bitwise_xor(me_ref[0], step), lanes), out)
+        for step, out in enumerate(outs, 1)
+    ]
+    for copy in copy_all(pairs, semaphore):
+        copy.wait()
 
 
 def pack(me, fields, first, columns):
     stack_count, rows, width = fields.shape
     lanes = width // columns
-    gx = (stack_count // HALVES) * columns
-
-    def spec(step):
-        def index(_, me_ref):
-            to = jnp.bitwise_xor(me_ref[0], step)
-            return (first + to // columns, 0, to % columns)
-
-        return pl.BlockSpec((1, rows, lanes), index)
-
-    block = jax.ShapeDtypeStruct((rows, lanes), jnp.float32)
+    count = (stack_count // HALVES) * columns - 1
     return pl.pallas_call(
-        pack_body,
+        partial(pack_body, first, columns),
         grid_spec=pltpu.PrefetchScalarGridSpec(
             num_scalar_prefetch=1,
             grid=(1,),
-            in_specs=[spec(step) for step in range(1, gx)],
-            out_specs=[pl.BlockSpec((rows, lanes), lambda *_: (0, 0)) for _ in range(1, gx)],
+            in_specs=[IN_HBM],
+            out_specs=[IN_VMEM] * count,
+            scratch_shapes=[pltpu.SemaphoreType.DMA((count,))],
         ),
-        out_shape=[block] * (gx - 1),
+        out_shape=[pltpu.HBM((rows, lanes), jnp.float32)] * count,
+        compiler_params=LIMIT,
         name="pack",
-    )(me, *([fields] * (gx - 1)))
-
-
-def x_body(gy, me_ref, where_ref, own_ref, *refs):
-    others = refs[: X_RADIX - 1]
-    table_ref, line_ref, real_ref, imag_ref = refs[X_RADIX - 1], *refs[X_RADIX + PIECES :]
+    )(me, in_hbm(fields))
+
+
+def x_body(gy, first, columns, me_ref, where_ref, fields_ref, *refs):
+    others, table_ref = refs[: X_RADIX - 1], refs[X_RADIX - 1]
     outs = refs[X_RADIX : X_RADIX + PIECES]
+    line_ref, real_ref, imag_ref, semaphore = refs[X_RADIX + PIECES :]
     me = me_ref[0]
-    line_ref[me] = own_ref[0]
+    points, lanes = line_ref.shape[1:]
+    own = copy_all([(column_block(fields_ref, first, columns, me, lanes), line_ref.at[me])], semaphore)
     for step, ref in enumerate(others, 1):
         line_ref[jnp.bitwise_xor(me, step)] = ref[...]
-    points, lanes = own_ref.shape[1:]
+    own[0].wait()
     units = real_ref.shape[0] // X_RADIX
     half = math.sqrt(0.5)
     f = [line_ref[at] for at in range(X_RADIX)]
@@ -145,33 +176,27 @@
 
 
 def x_lines(me, where, fields, first, columns, others, table, gx, gy):
-    _, rows, width = fields.shape
-    lanes = width // columns
+    rows, lanes = others[0].shape
     kept = where.shape[0]
-
-    def own(_, me_ref, where_ref):
-        return (first + me_ref[0] // columns, 0, me_ref[0] % columns)
-
-    whole = lambda *shape: pl.BlockSpec(shape, lambda *_: (0,) * len(shape))
     out = (gx * gy, 2, kept // (gx * gy * PIECES), lanes)
     return pl.pallas_call(
-        partial(x_body, gy),
+        partial(x_body, gy, first, columns),
         grid_spec=pltpu.PrefetchScalarGridSpec(
             num_scalar_prefetch=2,
             grid=(1,),
-            in_specs=[pl.BlockSpec((1, rows, lanes), own)]
-            + [whole(rows, lanes)] * len(others)
-            + [whole(*table.shape)],
-            out_specs=[whole(*out)] * PIECES,
+            in_specs=[IN_HBM] + [IN_VMEM] * X_RADIX,
+            out_specs=[IN_VMEM] * PIECES,
             scratch_shapes=[
                 pltpu.VMEM((X_RADIX, rows, lanes), jnp.float32),
                 pltpu.VMEM((kept, lanes), jnp.float32),
                 pltpu.VMEM((kept, lanes), jnp.float32),
+                pltpu.SemaphoreType.DMA((1,)),
             ],
         ),
-        out_shape=[jax.ShapeDtypeStruct(out, jnp.float32)] * PIECES,
+        out_shape=[pltpu.HBM(out, jnp.float32)] * PIECES,
+        compiler_params=LIMIT,
         name="x_lines",
-    )(me, where, fields, *others, table)
+    )(me, where, in_hbm(fields), *on_chip(*others, table))
 
 
 def y_body(me_ref, in_ref, twiddle_ref, table_ref, *refs):
@@ -210,12 +235,11 @@
     whole = dot(high_ref[...], table_ref[0]) + dot(low_ref[...], table_ref[0]) + dot(high_ref[...], table_ref[1])
     for c in range(Y_RADIX):
         product = whole[c * 2 * block : (c + 1) * 2 * block]
-        real = product[:block, :short] + product[block:, short:]
-        imag = product[block:, :short] - product[:block, short:]
         for to in range(Y_RADIX):
-            piece = slice(to * (short // Y_RADIX), (to + 1) * (short // Y_RADIX))
-            wave_ref[c, to, :block] = real[:, piece]
-            wave_ref[c, to, block:] = imag[:, piece]
+            start = (to // 2 * Y_RADIX + to % 2) * LANES
+            by_cos, by_sin = slice(start, start + LANES), slice(start + 2 * LANES, start + 3 * LANES)
+            wave_ref[c, to, :block] = product[:block, by_cos] + product[block:, by_sin]
+            wave_ref[c, to, block:] = product[block:, by_cos] - product[:block, by_sin]
     lane = lax.broadcasted_iota(jnp.int32, (rows, LANES), 1)
     residue = lane % Y_RADIX
     for step in range(Y_RADIX):
@@ -237,7 +261,6 @@
     sources, _, rows, lanes = spectra.shape
     short = table.shape[1]
     levels = sources * lanes // (Y_RADIX * short)
-    whole = lambda *shape: pl.BlockSpec(shape, lambda *_: (0,) * len(shape))
     out = (2, levels, rows, short)
     tall = Y_RADIX * 2 * levels * rows
     return pl.pallas_call(
@@ -245,50 +268,61 @@
         grid_spec=pltpu.PrefetchScalarGridSpec(
             num_scalar_prefetch=1,
             grid=(1,),
-            in_specs=[whole(*spectra.shape), whole(*twiddles.shape), whole(*table.shape)],
-            out_specs=[whole(*out)] * Y_RADIX,
+            in_specs=[IN_VMEM] * 3,
+            out_specs=[IN_VMEM] * Y_RADIX,
             scratch_shapes=[
                 pltpu.VMEM((tall, short), jnp.bfloat16),
                 pltpu.VMEM((tall, short), jnp.bfloat16),
                 pltpu.VMEM((Y_RADIX, Y_RADIX, 2 * levels * rows, short // Y_RADIX), jnp.float32),
             ],
         ),
-        out_shape=[jax.ShapeDtypeStruct(out, jnp.float32)] * Y_RADIX,
+        out_shape=[pltpu.HBM(out, jnp.float32)] * Y_RADIX,
+        compiler_params=LIMIT,
         name="y_lines",
     )(me, spectra, twiddles, table)
 
 
-def finish_body(me_ref, *refs):
-    blocks, mask_ref, out_ref = refs[:Y_RADIX], refs[Y_RADIX], refs[-1]
-    rows = blocks[0].shape[2]
-    for step, ref in enumerate(blocks):
-        at = pl.ds(pl.multiple_of(jnp.bitwise_xor(me_ref[0], step) * rows, 8), rows)
-        weight = mask_ref[at, :].astype(jnp.float32)
-        for part in range(2):
-            out_ref[part, 0, at, :] = ref[part, 0] * weight
+def finish_body(piece, me_ref, *refs):
+    blocks, mask_ref, out_ref = refs[:Y_RADIX], refs[Y_RADIX], refs[-3]
+    out_buffer, out_semaphore = refs[-2:]
+    _, levels, rows, _ = blocks[0].shape
+    rows_out = rows * Y_RADIX
+    leaving = []
+    for level in range(levels):
+        for step in range(Y_RADIX):
+            at = pl.ds(pl.multiple_of(jnp.bitwise_xor(me_ref[0], step) * rows, rows), rows)
+            weight = mask_ref[at, :].astype(jnp.float32)
+            for part in range(2):
+                out_buffer[level, part, at, :] = blocks[step][part, level] * weight
+        target = out_ref.at[:, level, pl.ds(piece * rows_out, rows_out), :]
+        leaving += copy_all([(out_buffer.at[level], target)], out_semaphore.at[level])
+    for copy in leaving:
+        copy.wait()
 
 
 def finish(me, blocks, kept_mask, piece, stack_count, before):
     _, levels, rows, width = blocks[0].shape
     rows_out = rows * Y_RADIX
-    block = pl.BlockSpec((2, 1, rows, width), lambda level, me_ref: (0, level, 0, 0))
     extra = [] if before is None else [before]
     return pl.pallas_call(
-        finish_body,
+        partial(finish_body, piece),
         grid_spec=pltpu.PrefetchScalarGridSpec(
             num_scalar_prefetch=1,
-            grid=(levels,),
-            in_specs=[block] * Y_RADIX
-            + [pl.BlockSpec((rows_out, width), lambda level, me_ref: (piece, 0))]
-            + [pl.BlockSpec(memory_space=pl.ANY)] * len(extra),
-            out_specs=pl.BlockSpec(
-                (2, 1, rows_out, width), lambda level, me_ref: (0, level, piece, 0)
-            ),
+            grid=(1,),
+            in_specs=[IN_VMEM] * Y_RADIX
+            + [pl.BlockSpec((rows_out, width), lambda *_: (piece, 0))]
+            + [IN_HBM] * len(extra),
+            out_specs=IN_HBM,
+            scratch_shapes=[
+                pltpu.VMEM((levels, 2, rows_out, width), jnp.float32),
+                pltpu.SemaphoreType.DMA((levels, 1)),
+            ],
         ),
         out_shape=jax.ShapeDtypeStruct((2, stack_count) + kept_mask.shape, jnp.float32),
         input_output_aliases={} if before is None else {2 + Y_RADIX: 0},
+        compiler_params=LIMIT,
         name="finish",
-    )(me, *blocks, kept_mask, *extra)
+    )(me, in_hbm(blocks[0]), *on_chip(*blocks[1:]), kept_mask, *extra)
 
 
 def turn(values):
@@ -297,17 +331,18 @@
     return jnp.where(lane < LANES // 2, rolled, -rolled)
 
 
-def y_first_body(scale, me_ref, own_ref, *refs):
+def y_first_body(scale, first, me_ref, fields_ref, *refs):
     others = refs[: Y_RADIX - 1]
     twiddle_ref, table_ref = refs[Y_RADIX - 1 : Y_RADIX + 1]
     outs = refs[Y_RADIX + 1 : Y_RADIX + 1 + X_RADIX]
-    field_ref, wave_ref = refs[Y_RADIX + 1 + X_RADIX :]
+    field_ref, wave_ref, semaphore = refs[Y_RADIX + 1 + X_RADIX :]
     me_x, me_y = me_ref[0], me_ref[1]
-    rows, short = own_ref.shape[1:]
+    _, rows, short = field_ref.shape
     half = short // 2
-    field_ref[me_y] = own_ref[0]
+    own = copy_all([(column_block(fields_ref, first, 1, me_y, short), field_ref.at[me_y])], semaphore)
     for step, ref in enumerate(others, 1):
         field_ref[jnp.bitwise_xor(me_y, step)] = ref[...]
+    own[0].wait()
     even, odd = field_ref[0] + field_ref[2], field_ref[1] + field_ref[3]
     less, more = field_ref[0] - field_ref[2], field_ref[1] - field_ref[3]
     folded = ((even + odd, None), (less, -more), (even - odd, None), (less, more))
@@ -320,65 +355,63 @@
                 real, imag = real * cos + imag * sin, imag * cos - real * sin
         tall = real if imag is None else jnp.concatenate([real, imag], axis=0)
         high, low = split(tall)
-        parts = []
-        for span in (pl.ds(0, half), pl.ds(short, half)):
-            parts.append(dot(high, table_ref[0, :, span]) + dot(low, table_ref[0, :, span]) + dot(high, table_ref[1, :, span]))
-        by_cos, by_sin = parts
+        top, bottom = table_ref[0, :, :short], table_ref[1, :, :short]
+        product = dot(high, top) + dot(low, top) + dot(high, bottom)
+        by_cos, by_sin = product[:, :half], product[:, half:]
         if imag is None:
             point = lax.broadcasted_iota(jnp.int32, real.shape, 1)
             top = jnp.sum(jnp.where(point % 2 == 0, real, -real), axis=1, keepdims=True) * scale
             unit = lax.broadcasted_iota(jnp.int32, by_sin.shape, 1)
-            wave_ref[c, 0] = by_cos
-            wave_ref[c, 1] = jnp.where(unit == 0, top, -by_sin)
+            wave_ref[c] = by_cos
+            wave_ref[Y_RADIX + c] = jnp.where(unit == 0, top, -by_sin)
         else:
-            wave_ref[c, 0] = by_cos[:rows] + by_sin[rows:]
-            wave_ref[c, 1] = by_cos[rows:] - by_sin[:rows]
-    chunk = 32
+            wave_ref[c] = by_cos[:rows] + by_sin[rows:]
+            wave_ref[Y_RADIX + c] = by_cos[rows:] - by_sin[:rows]
+    chunk, group = 32, LANES // X_RADIX
 
     def place(at, carry):
         span = pl.ds(pl.multiple_of(at * chunk, chunk), chunk)
         lane = lax.broadcasted_iota(jnp.int32, (chunk, LANES), 1)
-        local = lane % (LANES // 2)
-        for step in range(X_RADIX):
-            to = jnp.bitwise_xor(me_x, step)
-            index = to * (LANES // 2 // Y_RADIX) + local // Y_RADIX
-            for side in range(2):
-                units = pl.ds(side * LANES, LANES)
-                value = None
-                for c in range(Y_RADIX):
-                    pair = [
-                        jnp.take_along_axis(wave_ref[c, part, span, units], index, axis=1, mode="promise_in_bounds")
-                        for part in range(2)
-                    ]
-                    both = jnp.where(lane < LANES // 2, *pair)
-                    value = both if c == 0 else jnp.where(lane % Y_RADIX == c, both, value)
-                outs[step][span, units] = value
+        for side in range(2):
+            units = pl.ds(side * LANES, LANES)
+            tiles = [wave_ref[number, span, units] for number in range(X_RADIX)]
+            for bit in (1, 2, 4):
+                upper = lane // (group * bit) % 2 == 1
+                for low in range(X_RADIX):
+                    if low & bit:
+                        continue
+                    one, two = tiles[low], tiles[low + bit]
+                    tiles[low] = jnp.where(upper, pltpu.roll(two, group * bit, 1), one)
+                    tiles[low + bit] = jnp.where(upper, two, pltpu.roll(one, LANES - group * bit, 1))
+            for number, tile in enumerate(tiles):
+                wave_ref[number, span, units] = tile
         return carry
 
     lax.fori_loop(0, rows // chunk, place, 0)
+    for step, out in enumerate(outs):
+        out[...] = wave_ref[jnp.bitwise_xor(me_x, step)]
 
 
 def y_first(me, scale, fields, first, others, twiddles, table):
-    _, rows, short = fields.shape
-    whole = lambda *shape: pl.BlockSpec(shape, lambda *_: (0,) * len(shape))
+    rows, short = others[0].shape
     out = (rows, 2 * LANES)
     return pl.pallas_call(
-        partial(y_first_body, scale),
+        partial(y_first_body, scale, first),
         grid_spec=pltpu.PrefetchScalarGridSpec(
             num_scalar_prefetch=1,
             grid=(1,),
-            in_specs=[pl.BlockSpec((1, rows, short), lambda _, me_ref: (first + me_ref[1], 0, 0))]
-            + [whole(rows, short)] * len(others)
-            + [whole(*twiddles.shape), whole(*table.shape)],
-            out_specs=[whole(*out)] * X_RADIX,
+            in_specs=[IN_HBM] + [IN_VMEM] * (Y_RADIX + 1),
+            out_specs=[IN_VMEM] * X_RADIX,
             scratch_shapes=[
                 pltpu.VMEM((Y_RADIX, rows, short), jnp.float32),
-                pltpu.VMEM((Y_RADIX, 2, rows, short // 2), jnp.float32),
+                pltpu.VMEM((X_RADIX, rows, 2 * LANES), jnp.float32),
+                pltpu.SemaphoreType.DMA((1,)),
             ],
         ),
-        out_shape=[jax.ShapeDtypeStruct(out, jnp.float32)] * X_RADIX,
+        out_shape=[pltpu.HBM(out, jnp.float32)] * X_RADIX,
+        compiler_params=LIMIT,
         name="y_first",
-    )(me, fields, *others, twiddles, table)
+    )(me, in_hbm(fields), *on_chip(*others), twiddles, table)
 
 
 def x_second_body(me_ref, where_ref, *refs):
@@ -450,79 +483,91 @@
 def x_second(me, where, blocks, table, gx):
     points, lanes = blocks[0].shape
     kept = where.shape[0]
-    whole = lambda *shape: pl.BlockSpec(shape, lambda *_: (0,) * len(shape))
     out = (gx * Y_RADIX, kept // gx, LANES)
     return pl.pallas_call(
         x_second_body,
         grid_spec=pltpu.PrefetchScalarGridSpec(
             num_scalar_prefetch=2,
             grid=(1,),
-            in_specs=[whole(points, lanes)] * X_RADIX + [whole(*table.shape)],
-            out_specs=whole(*out),
+            in_specs=[IN_VMEM] * (X_RADIX + 1),
+            out_specs=IN_VMEM,
             scratch_shapes=[
                 pltpu.VMEM((X_RADIX, points, lanes), jnp.float32),
                 pltpu.VMEM((Y_RADIX, kept, LANES), jnp.float32),
             ],
         ),
-        out_shape=jax.ShapeDtypeStruct(out, jnp.float32),
+        out_shape=pltpu.HBM(out, jnp.float32),
+        compiler_params=LIMIT,
         name="x_second",
-    )(me, where, *blocks, table)
-
-
-def finish_second_body(me_ref, in_ref, mask_ref, before_ref, out_ref):
+    )(me, where, in_hbm(blocks[0]), *on_chip(*blocks[1:]), table)
+
+
+def finish_second_body(first, me_ref, blocks_ref, mask_ref, before_ref, out_ref, *refs):
+    out_buffer, out_semaphore = refs
     mirrored = me_ref[0] >= Y_RADIX // 2
-    rows = mask_ref.shape[0]
-    chunk = 32
-
-    def place(at, carry):
+    _, levels, rows, _ = blocks_ref.shape
+    chunk, group = 32, LANES // X_RADIX
+
+    def place(level, at):
         span = pl.ds(pl.multiple_of(at * chunk, chunk), chunk)
         lane = lax.broadcasted_iota(jnp.int32, (chunk, LANES), 1)
         left = lane < LANES // 2
-        index = jnp.where(mirrored, (LANES - lane) % LANES, lane)
+        wanted = jnp.where(mirrored, (LANES - lane) % LANES, lane)
+        local = wanted % (LANES // 2)
+        index = wanted - local + local % Y_RADIX * group + local // Y_RADIX
         for tile in range(Y_RADIX):
             body = jnp.where(mirrored, Y_RADIX - 1 - tile, tile)
             head = jnp.where(mirrored, (Y_RADIX - tile) % Y_RADIX, tile)
-            here, there = in_ref[2 * body, 0, span, :], in_ref[2 * body + 1, 0, span, :]
-            start = in_ref[2 * head, 0, span, :]
+            here, there = blocks_ref[2 * body, level, span, :], blocks_ref[2 * body + 1, level, span, :]
+            start = blocks_ref[2 * head, level, span, :]
             real = jnp.where(left, here, pltpu.roll(there, LANES // 2, 1))
             imag = jnp.where(left, pltpu.roll(here, LANES // 2, 1), there)
             lanes = pl.ds(tile * LANES, LANES)
             weight = mask_ref[span, lanes].astype(jnp.float32)
             for part, (values, edge) in enumerate(((real, start), (imag, pltpu.roll(start, LANES // 2, 1)))):
                 values = jnp.take_along_axis(values, index, axis=1, mode="promise_in_bounds")
-                out_ref[part, 0, span, lanes] = jnp.where(lane == 0, edge, values) * weight
-        return carry
-
-    lax.fori_loop(0, rows // chunk, place, 0)
+                out_buffer[level, part, span, lanes] = jnp.where(lane == 0, edge, values) * weight
+
+    leaving = []
+    for level in range(levels):
+
+        def step(at, carry):
+            place(level, at)
+            return carry
+
+        lax.fori_loop(0, rows // chunk, step, 0)
+        leaving += copy_all([(out_buffer.at[level], out_ref.at[:, first + level])], out_semaphore.at[level])
+    for copy in leaving:
+        copy.wait()
 
 
 def finish_second(me, blocks, kept_mask, first, before):
-    gx, levels, rows, lanes = blocks.shape
+    _, levels, _, _ = blocks.shape
     return pl.pallas_call(
-        finish_second_body,
+        partial(finish_second_body, first),
         grid_spec=pltpu.PrefetchScalarGridSpec(
             num_scalar_prefetch=1,
-            grid=(levels,),
-            in_specs=[
-                pl.BlockSpec((gx, 1, rows, lanes), lambda level, me_ref: (0, level, 0, 0)),
-                pl.BlockSpec(kept_mask.shape, lambda level, me_ref: (0, 0)),
-                pl.BlockSpec(memory_space=pl.ANY),
+            grid=(1,),
+            in_specs=[IN_VMEM, IN_VMEM, IN_HBM],
+            out_specs=IN_HBM,
+            scratch_shapes=[
+                pltpu.VMEM((levels, 2) + kept_mask.shape, jnp.float32),
+                pltpu.SemaphoreType.DMA((levels, 1)),
             ],
-            out_specs=pl.BlockSpec(
-                (2, 1) + kept_mask.shape, lambda level, me_ref: (0, first + level, 0, 0)
-            ),
         ),
         out_shape=jax.ShapeDtypeStruct(before.shape, jnp.float32),
         input_output_aliases={3: 0},
+        compiler_params=LIMIT,
         name="finish_second",
-    )(me, blocks, kept_mask, before)
+    )(me, *on_chip(blocks), kept_mask, before)
 
 
 def exchange(blocks, axis, size):
-    return [
-        lax.ppermute(block, axis, [(at, at ^ step) for at in range(size)])
-        for step, block in enumerate(blocks, 1)
-    ]
+    arrived = {}
+    for step in sorted(range(1, size), key=lambda step: (step < size // 2, step)):
+        pairs = [(at, at ^ step) for at in range(size)]
+        arrived[step] = lax.ppermute(blocks[step - 1], axis, pairs)
+    return [arrived[step] for step in range(1, size)]
 
 
 def fast_shards(gx, gy, nx, ny, fields, wave_order, kept_mask):

time: 302 us -> 289 us (0.957)
  Pallas kernels: 60.9 us -> 49.3 us
  waiting for transfers between devices: 137 us -> 145 us
  local copies, waits for them, and re-layouts: 7.09 us -> 0.91 us
  other arithmetic: 14.2 us -> 9.91 us
    ppermute x23, waiting for transfers between devices: 137 us -> 145 us  [exchange(): arrived[step] = lax.ppermute(blocks[step - 1], axis, pairs)]
    pallas_call x7, Pallas kernels: 39.7 us -> 32.2 us  [the longest x1 9.52 us: y_first(): pl.pallas_call(partial(y_first_body, scale, first), grid_spec=pltpu.Prefe...]
    unnamed x56 -> x14, local copies, waits for them, and re-layouts: 7.09 us -> 0.72 us
    concatenate x1 -> x0, other arithmetic: 4.15 us -> none  [y_table(): return jnp.stack(two_parts(jnp.concatenate([cos, sin], axis=1) * scale))]
    cos x2 -> x3, other arithmetic: 4.23 us -> 8.38 us  [roots(): return (jnp.cos(angles), jnp.sin(angles))]
  transfers between devices with their start and end apart: 25 -> 25, of which waited for: 10 -> 10; matrix products, arithmetic and copies ran while one was open for 5% -> 4% of each run, Pallas kernels for 15% -> 13%
where the time goes in v2:
time: 289 us; the launch traced here: 286 us
  waiting for transfers between devices  145 us (50%)
  starting transfers between devices  49.6 us (17%)
  Pallas kernels  49.3 us (17%)
  blocking collectives  31 us (11%)
  other arithmetic  9.91 us (3%)
    ppermute x23, waiting for transfers between devices, exchange(): arrived[step] = lax.ppermute(blocks[step - 1], axis, pairs)  145 us
    ppermute x23, starting transfers between devices, exchange(): arrived[step] = lax.ppermute(blocks[step - 1], axis, pairs)  31.1 us
    all_to_all x1, blocking collectives, fast_shards(): lax.all_to_all(spectra[piece], whole, split_axis=0, concat_axis=0, tiled=...  31 us
    all_to_all x1, starting transfers between devices, fast_shards(): lax.all_to_all(owned, whole, split_axis=0, concat_axis=0, tiled=True)  13.8 us
    pallas_call x1, Pallas kernels, y_first(): pl.pallas_call(partial(y_first_body, scale, first), grid_spec=pltpu.Prefe...  9.52 us
    pallas_call x2, Pallas kernels, y_lines(): pl.pallas_call(y_body, grid_spec=pltpu.PrefetchScalarGridSpec(num_scalar_...  9.42 us
    cos x3, other arithmetic, roots(): return (jnp.cos(angles), jnp.sin(angles))  8.38 us
    pallas_call x1, Pallas kernels, x_lines(): pl.pallas_call(partial(x_body, gy, first, columns), grid_spec=pltpu.Prefe...  8.06 us
  transfers between devices with their start and end apart: 25, of which 10 were waited for; matrix products, arithmetic and copies ran while one was open for 4% of the time, Pallas kernels for 13%

profile of v2, /device:TPU:0, one launch (start us, length us, event | category | flops | bytes accessed | tf_op | source)
XLA Modules:
  0.0 285.9 jit_solution(3537341402710862604)
XLA Ops:
  0.0 2.8 pack.2
  3.3 2.6 collective-permute-start.1
  7.8 4.1 %fusion.11 = (f32[4,2,1,128,256]{4,3,2,1,0:T(8,128)S(1)}, f32[4,2,1,128,256]{4,3,2,1,0:T(8,128)S(1)}) fusion(s32[256]{0:T(256)S(1)} %iota_add_fusion.1, s32[4,2,128]{2,1,0:T(2,128)S(1)} %broadcast_add_fusion), kind=kLoop, calls=%fused_computation.33 | loop fusion | flops 3670016 | bytes 2102272 | tf_op jit(solution)/shard_map/cos | solution.py:21
  12.5 4.1 %fusion.9 = (f32[512,512]{1,0:T(8,128)S(1)}, f32[512,512]{1,0:T(8,128)S(1)}) fusion(s32[512]{0:T(512)S(1)} %iota_add_fusion), kind=kLoop, calls=%fused_computation.31 | loop fusion | flops 3670016 | bytes 2099200 | tf_op jit(solution)/shard_map/cos | solution.py:21
  18.5 2.6 collective-permute-start.5
  21.3 7.3 %collective-permute-done.5.refs_5_ = f32[256,256]{1,0:T(8,128)S(1)} collective-permute-done((f32[256,256]{1,0:T(8,128)S(1)}, f32[256,256]{1,0:T(8,128)S(1)}, u32[]{:S(2)}, u32[]{:S(2)}) %collective-permute-start.5) | collective-permute-done | bytes 262176 | tf_op jit(solution)/shard_map/ppermute | solution.py:569
  28.6 4.5 %collective-permute-done.6.refs_6_ = f32[256,256]{1,0:T(8,128)S(1)} collective-permute-done((f32[256,256]{1,0:T(8,128)S(1)}, f32[256,256]{1,0:T(8,128)S(1)}, u32[]{:S(2)}, u32[]{:S(2)}) %collective-permute-start.6) | collective-permute-done | bytes 262176 | tf_op jit(solution)/shard_map/ppermute | solution.py:569
  33.1 8.1 %x_lines.1 = (f32[32,2,16,256]{3,2,1,0:T(8,128)}, f32[32,2,16,256]{3,2,1,0:T(8,128)}) custom-call(s32[1]{0:T(128)} %bitcast.1.me_ref, s32[1024]{0:T(1024)S(1)} %fusion.16.where_ref, f32[8,256,512]{2,1,0:T(8,128)} %fields_ref.7, f32[256,256]{1,0:T(8,128)S(1)} %collective-permute-done.refs_0_, f32[256,256]{1,0:T(8,128)S(1)} %collective-permute-done.1.refs_1_, ...), custom_call_target="tpu_custom_call" | custom-call | tf_op jit(solution)/shard_map/x_lines/pallas_call | solution.py:182
  41.2 31.0 %all_to_all.15.in_ref = f32[32,2,16,256]{3,2,1,0:T(8,128)S(1)} all-to-all(f32[32,2,16,256]{3,2,1,0:T(8,128)} %get-tuple-element.44), channel_id=1, replica_groups=mesh['gx'=8,'gy'=4] {'gx','gy'}, dimensions={0} | all-to-all | bytes 2097152 | tf_op jit(solution)/shard_map/all_to_all | solution.py:593
  72.2 4.7 %all-to-all-start.2 = ((f32[32,2,16,256]{3,2,1,0:T(8,128)}), f32[32,2,16,256]{3,2,1,0:T(8,128)}, u32[]{:S(2)}, u32[]{:S(2)}) async-start(f32[32,2,16,256]{3,2,1,0:T(8,128)} %get-tuple-element.62), calls=%async_computation.2 | async-start | bytes 2097152 | tf_op jit(solution)/shard_map/all_to_all | solution.py:593
  76.9 2.5 pack.3
  81.2 2.4 collective-permute-start.11
  83.9 30.4 %collective-permute-done.10.refs_0_ = f32[256,512]{1,0:T(8,128)S(1)} collective-permute-done((f32[256,512]{1,0:T(8,128)}, f32[256,512]{1,0:T(8,128)S(1)}, u32[]{:S(2)}, u32[]{:S(2)}) %collective-permute-start.10) | collective-permute-done | bytes 524320 | tf_op jit(solution)/shard_map/ppermute | solution.py:569
  114.3 22.9 %collective-permute-done.11.refs_1_ = f32[256,512]{1,0:T(8,128)S(1)} collective-permute-done((f32[256,512]{1,0:T(8,128)}, f32[256,512]{1,0:T(8,128)S(1)}, u32[]{:S(2)}, u32[]{:S(2)}) %collective-permute-start.11) | collective-permute-done | bytes 524320 | tf_op jit(solution)/shard_map/ppermute | solution.py:569
  137.2 9.5 %y_first.1 = (f32[256,256]{1,0:T(8,128)}, f32[256,256]{1,0:T(8,128)}, f32[256,256]{1,0:T(8,128)}, f32[256,256]{1,0:T(8,128)}, f32[256,256]{1,0:T(8,128)}, /*inde...) custom-call(s32[2]{0:T(128)S(1)} %pad_add_fusion.me_ref, f32[8,256,512]{2,1,0:T(8,128)} %fields_ref.7, ...), custom_call_target="tpu_custom_call" | custom-call | tf_op jit(solution)/shard_map/y_first/pallas_call | solution.py:398
  150.4 2.4 collective-permute-start.18
  152.8 3.5 %collective-permute-done.14.refs_2_ = f32[256,256]{1,0:T(8,128)S(1)} collective-permute-done((f32[256,256]{1,0:T(8,128)}, f32[256,256]{1,0:T(8,128)S(1)}, u32[]{:S(2)}, u32[]{:S(2)}) %collective-permute-start.14) | collective-permute-done | bytes 262176 | tf_op jit(solution)/shard_map/ppermute | solution.py:569
  157.3 3.7 %collective-permute-done.15.refs_3_ = f32[256,256]{1,0:T(8,128)S(1)} collective-permute-done((f32[256,256]{1,0:T(8,128)}, f32[256,256]{1,0:T(8,128)S(1)}, u32[]{:S(2)}, u32[]{:S(2)}) %collective-permute-start.15) | collective-permute-done | bytes 262176 | tf_op jit(solution)/shard_map/ppermute | solution.py:569
  161.0 12.7 %collective-permute-done.17.refs_5_ = f32[256,256]{1,0:T(8,128)S(1)} collective-permute-done((f32[256,256]{1,0:T(8,128)}, f32[256,256]{1,0:T(8,128)S(1)}, u32[]{:S(2)}, u32[]{:S(2)}) %collective-permute-start.17) | collective-permute-done | bytes 262176 | tf_op jit(solution)/shard_map/ppermute | solution.py:569
  173.7 7.7 %x_second.1 = f32[32,128,128]{2,1,0:T(8,128)} custom-call(s32[1]{0:T(128)} %bitcast.1.me_ref, s32[1024]{0:T(1024)S(1)} %fusion.16.where_ref, f32[256,256]{1,0:T(8,128)} %get-tuple-element.54.refs_0_, f32[256,256]{1,0:T(8,128)S(1)} %collective-permute-done.13.refs_1_, f32[256,256]{1,0:T(8,128)S(1)} %collective-permute-done.14.refs_2_, ...), custom_call_target="tpu_custom_call" | custom-call | tf_op jit(solution)/shard_map/x_second/pallas_call | solution.py:487
  181.5 13.8 %all-to-all-start.1 = ((f32[32,128,128]{2,1,0:T(8,128)}), f32[32,128,128]{2,1,0:T(8,128)}, u32[]{:S(2)}, u32[]{:S(2)}) async-start(f32[32,128,128]{2,1,0:T(8,128)} %x_second.1), calls=%async_computation.1 | async-start | bytes 4194304 | tf_op jit(solution)/shard_map/all_to_all | solution.py:597
  195.3 5.3 %y_lines.3 = (f32[2,4,16,512]{3,2,1,0:T(8,128)}, f32[2,4,16,512]{3,2,1,0:T(8,128)}, f32[2,4,16,512]{3,2,1,0:T(8,128)}, f32[2,4,16,512]{3,2,1,0:T(8,128)}) custom-call(s32[1]{0:T(128)} %bitcast.me_ref, f32[32,2,16,256]{3,2,1,0:T(8,128)} %all-to-all-done.2.in_ref, f32[8,512]{1,0:T(8,128)S(1)} %pad_maximum_fusion.3.twiddle_ref.refs_3_, ...), custom_call_target="tpu_custom_call" | custom-call | tf_op jit(solution)/shard_map/y_lines/pallas_call | solution.py:266
  202.1 2.4 collective-permute-start.21
  205.0 4.1 %y_lines.2 = (f32[2,4,16,512]{3,2,1,0:T(8,128)}, f32[2,4,16,512]{3,2,1,0:T(8,128)}, f32[2,4,16,512]{3,2,1,0:T(8,128)}, f32[2,4,16,512]{3,2,1,0:T(8,128)}) custom-call(s32[1]{0:T(128)} %bitcast.me_ref, f32[32,2,16,256]{3,2,1,0:T(8,128)S(1)} %all_to_all.15.in_ref, f32[8,512]{1,0:T(8,128)S(1)} %pad_maximum_fusion.3.twiddle_ref.refs_3_, ...), custom_call_target="tpu_custom_call" | custom-call | tf_op jit(solution)/shard_map/y_lines/pallas_call | solution.py:266
  209.7 3.3 %collective-permute-start.8 = (f32[2,4,16,512]{3,2,1,0:T(8,128)}, f32[2,4,16,512]{3,2,1,0:T(8,128)S(1)}, u32[]{:S(2)}, u32[]{:S(2)}) collective-permute-start(f32[2,4,16,512]{3,2,1,0:T(8,128)} %get-tuple-element.49), channel_id=1, source_target_pairs={{0,2},{1,3},{2,0},{3,1},{4,6},{5,7},{6,4},{7,5},{8,10},{9,11},{10,... | collective-permute-start | bytes 786440 | tf_op jit(solution)/shard_map/ppermute | solution.py:569
  213.0 22.7 %collective-permute-done.20.refs_1_ = f32[2,4,16,512]{3,2,1,0:T(8,128)S(1)} collective-permute-done((f32[2,4,16,512]{3,2,1,0:T(8,128)}, f32[2,4,16,512]{3,2,1,0:T(8,128)S(1)}, u32[]{:S(2)}, u32[]{:S(2)}) %collective-permute-start.20) | collective-permute-done | bytes 262176 | tf_op jit(solution)/shard_map/ppermute | solution.py:569
  235.7 3.6 %collective-permute-start.9 = (f32[2,4,16,512]{3,2,1,0:T(8,128)}, f32[2,4,16,512]{3,2,1,0:T(8,128)S(1)}, u32[]{:S(2)}, u32[]{:S(2)}) collective-permute-start(f32[2,4,16,512]{3,2,1,0:T(8,128)} %get-tuple-element.50), channel_id=1, source_target_pairs={{0,3},{1,2},{2,1},{3,0},{4,7},{5,6},{6,5},{7,4},{8,11},{9,10},{10,... | collective-permute-start | bytes 786440 | tf_op jit(solution)/shard_map/ppermute | solution.py:569
  239.3 33.2 %collective-permute-done.21.refs_2_ = f32[2,4,16,512]{3,2,1,0:T(8,128)S(1)} collective-permute-done((f32[2,4,16,512]{3,2,1,0:T(8,128)}, f32[2,4,16,512]{3,2,1,0:T(8,128)S(1)}, u32[]{:S(2)}, u32[]{:S(2)}) %collective-permute-start.21) | collective-permute-done | bytes 262176 | tf_op jit(solution)/shard_map/ppermute | solution.py:569
  272.5 2.0 finish.2.before_ref
  274.5 5.4 %finish_second.1.refs_5_ = f32[2,8,128,512]{3,2,1,0:T(8,128)} custom-call(s32[1]{0:T(128)} %bitcast.me_ref, f32[8,4,128,128]{3,2,1,0:T(8,128)} %bitcast.7.blocks_ref, s32[128,512]{1,0:T(8,128)S(1)} %copy-done.2, f32[2,8,128,512]{3,2,1,0:T(8,128)} %finish.2.before_ref), custom_call_target="tpu_custom_call", output_to_operand_aliasing={{}: (3, {})} | custom-call | tf_op jit(solution)/shard_map/finish_second/pallas_call | solution.py:546
  279.9 3.8 %collective-permute-done.8.refs_2_ = f32[2,4,16,512]{3,2,1,0:T(8,128)S(1)} collective-permute-done((f32[2,4,16,512]{3,2,1,0:T(8,128)}, f32[2,4,16,512]{3,2,1,0:T(8,128)S(1)}, u32[]{:S(2)}, u32[]{:S(2)}) %collective-permute-start.8) | collective-permute-done | bytes 262176 | tf_op jit(solution)/shard_map/ppermute | solution.py:569
  283.7 2.0 finish.3
  (59 shorter events, 14.3 us)
Async XLA Ops:
  0.0 7.7 %copy-start.4 = (s32[4,2]{1,0:T(4,128)S(1)}, s32[4,2]{1,0:T(4,128)}, u32[]{:S(2)}) copy-start(s32[4,2]{1,0:T(4,128)} %constant.94.clone) | copy-start | bytes 100
  2.8 15.1 %collective-permute-start = (f32[256,256]{1,0:T(8,128)}, f32[256,256]{1,0:T(8,128)S(1)}, u32[]{:S(2)}, u32[]{:S(2)}) collective-permute-start(f32[256,256]{1,0:T(8,128)} %get-tuple-element.36), channel_id=1, source_target_pairs={{0,4},{4,0},{8,12},{12,8},{16,20},{20,16},{24,28},{28,24},{1,5},{5... | collective-permute-start | bytes 786440 | tf_op jit(solution)/shard_map/ppermute | solution.py:569
  3.3 17.8 %collective-permute-start.1 = (f32[256,256]{1,0:T(8,128)}, f32[256,256]{1,0:T(8,128)S(1)}, u32[]{:S(2)}, u32[]{:S(2)}) collective-permute-start(f32[256,256]{1,0:T(8,128)} %get-tuple-element.37), channel_id=1, source_target_pairs={{0,8},{4,12},{8,0},{12,4},{16,24},{20,28},{24,16},{28,20},{1,9},{5... | collective-permute-start | bytes 786440 | tf_op jit(solution)/shard_map/ppermute | solution.py:569
  5.9 15.4 %collective-permute-start.2 = (f32[256,256]{1,0:T(8,128)}, f32[256,256]{1,0:T(8,128)S(1)}, u32[]{:S(2)}, u32[]{:S(2)}) collective-permute-start(f32[256,256]{1,0:T(8,128)} %get-tuple-element.38), channel_id=1, source_target_pairs={{0,12},{4,8},{8,4},{12,0},{16,28},{20,24},{24,20},{28,16},{1,13},{... | collective-permute-start | bytes 786440 | tf_op jit(solution)/shard_map/ppermute | solution.py:569
  5.9 15.4 %collective-permute-start.3 = (f32[256,256]{1,0:T(8,128)}, f32[256,256]{1,0:T(8,128)S(1)}, u32[]{:S(2)}, u32[]{:S(2)}) collective-permute-start(f32[256,256]{1,0:T(8,128)} %get-tuple-element.39), channel_id=1, source_target_pairs={{0,16},{4,20},{8,24},{12,28},{16,0},{20,4},{24,8},{28,12},{1,17},{... | collective-permute-start | bytes 786440 | tf_op jit(solution)/shard_map/ppermute | solution.py:569
  7.7 13.6 %collective-permute-start.4 = (f32[256,256]{1,0:T(8,128)}, f32[256,256]{1,0:T(8,128)S(1)}, u32[]{:S(2)}, u32[]{:S(2)}) collective-permute-start(f32[256,256]{1,0:T(8,128)} %get-tuple-element.40), channel_id=1, source_target_pairs={{0,20},{4,16},{8,28},{12,24},{16,4},{20,0},{24,12},{28,8},{1,21},{... | collective-permute-start | bytes 786440 | tf_op jit(solution)/shard_map/ppermute | solution.py:569
  16.8 16.3 %copy-start = (bf16[4,512,512]{2,1,0:T(8,128)(2,1)}, bf16[4,512,512]{2,1,0:T(8,128)(2,1)S(1)}, u32[]{:S(2)}) copy-start(bf16[4,512,512]{2,1,0:T(8,128)(2,1)S(1)} %pad_maximum_fusion.1.refs_7_.refs_8_) | copy-start | bytes 6291460
  17.5 1.0 copy-start.6
  17.5 3.6 %copy-start.5 = (f32[256,256]{1,0:T(8,128)S(1)}, f32[256,256]{1,0:T(8,128)}, u32[]{:S(2)}) copy-start(f32[256,256]{1,0:T(8,128)} %get-tuple-element.42) | copy-start | bytes 786436
  17.5 3.8 %copy-start.3 = (s32[1024]{0:T(1024)S(1)}, s32[1024]{0:T(1024)}, u32[]{:S(2)}) copy-start(s32[1024]{0:T(1024)} %param.5) | copy-start | bytes 12292
  18.5 10.1 %collective-permute-start.5 = (f32[256,256]{1,0:T(8,128)S(1)}, f32[256,256]{1,0:T(8,128)S(1)}, u32[]{:S(2)}, u32[]{:S(2)}) collective-permute-start(f32[256,256]{1,0:T(8,128)S(1)} %copy-done.6), channel_id=1, source_target_pairs={{0,24},{4,28},{8,16},{12,20},{16,8},{20,12},{24,0},{28,4},{1,25},{... | collective-permute-start | bytes 786440 | tf_op jit(solution)/shard_map/ppermute | solution.py:569
  21.1 12.0 %collective-permute-start.6 = (f32[256,256]{1,0:T(8,128)S(1)}, f32[256,256]{1,0:T(8,128)S(1)}, u32[]{:S(2)}, u32[]{:S(2)}) collective-permute-start(f32[256,256]{1,0:T(8,128)S(1)} %copy-done.5), channel_id=1, source_target_pairs={{0,28},{4,24},{8,20},{12,16},{16,12},{20,8},{24,4},{28,0},{1,29},{... | collective-permute-start | bytes 786440 | tf_op jit(solution)/shard_map/ppermute | solution.py:569
  72.2 109.3 %all-to-all-start.2 = ((f32[32,2,16,256]{3,2,1,0:T(8,128)}), f32[32,2,16,256]{3,2,1,0:T(8,128)}, u32[]{:S(2)}, u32[]{:S(2)}) async-start(f32[32,2,16,256]{3,2,1,0:T(8,128)} %get-tuple-element.62), calls=%async_computation.2 | async-start | bytes 2097152 | tf_op jit(solution)/shard_map/all_to_all | solution.py:593
  79.4 34.9 %collective-permute-start.10 = (f32[256,512]{1,0:T(8,128)}, f32[256,512]{1,0:T(8,128)S(1)}, u32[]{:S(2)}, u32[]{:S(2)}) collective-permute-start(f32[256,512]{1,0:T(8,128)} %get-tuple-element.51), channel_id=1, source_target_pairs={{0,1},{1,0},{2,3},{3,2},{4,5},{5,4},{6,7},{7,6},{8,9},{9,8},{10,11... | collective-permute-start | bytes 1572872 | tf_op jit(solution)/shard_map/ppermute | solution.py:569
  81.2 56.1 %collective-permute-start.11 = (f32[256,512]{1,0:T(8,128)}, f32[256,512]{1,0:T(8,128)S(1)}, u32[]{:S(2)}, u32[]{:S(2)}) collective-permute-start(f32[256,512]{1,0:T(8,128)} %get-tuple-element.52), channel_id=1, source_target_pairs={{0,2},{1,3},{2,0},{3,1},{4,6},{5,7},{6,4},{7,5},{8,10},{9,11},{10,... | collective-permute-start | bytes 1572872 | tf_op jit(solution)/shard_map/ppermute | solution.py:569
  83.6 53.7 %collective-permute-start.12 = (f32[256,512]{1,0:T(8,128)}, f32[256,512]{1,0:T(8,128)S(1)}, u32[]{:S(2)}, u32[]{:S(2)}) collective-permute-start(f32[256,512]{1,0:T(8,128)} %get-tuple-element.53), channel_id=1, source_target_pairs={{0,3},{1,2},{2,1},{3,0},{4,7},{5,6},{6,5},{7,4},{8,11},{9,10},{10,... | collective-permute-start | bytes 1572872 | tf_op jit(solution)/shard_map/ppermute | solution.py:569
  83.9 89.8 %copy-start.1 = (bf16[4,512,512]{2,1,0:T(8,128)(2,1)S(1)}, bf16[4,512,512]{2,1,0:T(8,128)(2,1)}, u32[]{:S(2)}) copy-start(bf16[4,512,512]{2,1,0:T(8,128)(2,1)} %copy-done) | copy-start | bytes 6291460
  146.7 3.6 %collective-permute-start.13 = (f32[256,256]{1,0:T(8,128)}, f32[256,256]{1,0:T(8,128)S(1)}, u32[]{:S(2)}, u32[]{:S(2)}) collective-permute-start(f32[256,256]{1,0:T(8,128)} %get-tuple-element.55), channel_id=1, source_target_pairs={{0,4},{4,0},{8,12},{12,8},{16,20},{20,16},{24,28},{28,24},{1,5},{5... | collective-permute-start | bytes 786440 | tf_op jit(solution)/shard_map/ppermute | solution.py:569
  146.8 9.5 %collective-permute-start.14 = (f32[256,256]{1,0:T(8,128)}, f32[256,256]{1,0:T(8,128)S(1)}, u32[]{:S(2)}, u32[]{:S(2)}) collective-permute-start(f32[256,256]{1,0:T(8,128)} %get-tuple-element.56), channel_id=1, source_target_pairs={{0,8},{4,12},{8,0},{12,4},{16,24},{20,28},{24,16},{28,20},{1,9},{5... | collective-permute-start | bytes 786440 | tf_op jit(solution)/shard_map/ppermute | solution.py:569
  148.4 12.6 %collective-permute-start.15 = (f32[256,256]{1,0:T(8,128)}, f32[256,256]{1,0:T(8,128)S(1)}, u32[]{:S(2)}, u32[]{:S(2)}) collective-permute-start(f32[256,256]{1,0:T(8,128)} %get-tuple-element.57), channel_id=1, source_target_pairs={{0,12},{4,8},{8,4},{12,0},{16,28},{20,24},{24,20},{28,16},{1,13},{... | collective-permute-start | bytes 786440 | tf_op jit(solution)/shard_map/ppermute | solution.py:569
  148.7 12.3 %collective-permute-start.16 = (f32[256,256]{1,0:T(8,128)}, f32[256,256]{1,0:T(8,128)S(1)}, u32[]{:S(2)}, u32[]{:S(2)}) collective-permute-start(f32[256,256]{1,0:T(8,128)} %get-tuple-element.58), channel_id=1, source_target_pairs={{0,16},{4,20},{8,24},{12,28},{16,0},{20,4},{24,8},{28,12},{1,17},{... | collective-permute-start | bytes 786440 | tf_op jit(solution)/shard_map/ppermute | solution.py:569
  150.2 23.5 %collective-permute-start.17 = (f32[256,256]{1,0:T(8,128)}, f32[256,256]{1,0:T(8,128)S(1)}, u32[]{:S(2)}, u32[]{:S(2)}) collective-permute-start(f32[256,256]{1,0:T(8,128)} %get-tuple-element.59), channel_id=1, source_target_pairs={{0,20},{4,16},{8,28},{12,24},{16,4},{20,0},{24,12},{28,8},{1,21},{... | collective-permute-start | bytes 786440 | tf_op jit(solution)/shard_map/ppermute | solution.py:569
  150.4 23.3 %collective-permute-start.18 = (f32[256,256]{1,0:T(8,128)}, f32[256,256]{1,0:T(8,128)S(1)}, u32[]{:S(2)}, u32[]{:S(2)}) collective-permute-start(f32[256,256]{1,0:T(8,128)} %get-tuple-element.60), channel_id=1, source_target_pairs={{0,24},{4,28},{8,16},{12,20},{16,8},{20,12},{24,0},{28,4},{1,25},{... | collective-permute-start | bytes 786440 | tf_op jit(solution)/shard_map/ppermute | solution.py:569
  156.3 17.4 %collective-permute-start.19 = (f32[256,256]{1,0:T(8,128)}, f32[256,256]{1,0:T(8,128)S(1)}, u32[]{:S(2)}, u32[]{:S(2)}) collective-permute-start(f32[256,256]{1,0:T(8,128)} %get-tuple-element.61), channel_id=1, source_target_pairs={{0,28},{4,24},{8,20},{12,16},{16,12},{20,8},{24,4},{28,0},{1,29},{... | collective-permute-start | bytes 786440 | tf_op jit(solution)/shard_map/ppermute | solution.py:569
  181.5 93.0 %all-to-all-start.1 = ((f32[32,128,128]{2,1,0:T(8,128)}), f32[32,128,128]{2,1,0:T(8,128)}, u32[]{:S(2)}, u32[]{:S(2)}) async-start(f32[32,128,128]{2,1,0:T(8,128)} %x_second.1), calls=%async_computation.1 | async-start | bytes 4194304 | tf_op jit(solution)/shard_map/all_to_all | solution.py:597
  200.6 71.9 %copy-start.2 = (s32[128,512]{1,0:T(8,128)S(1)}, s32[128,512]{1,0:T(8,128)}, u32[]{:S(2)}) copy-start(s32[128,512]{1,0:T(8,128)} %refs_4_.3) | copy-start | bytes 786436
  200.6 35.1 %collective-permute-start.20 = (f32[2,4,16,512]{3,2,1,0:T(8,128)}, f32[2,4,16,512]{3,2,1,0:T(8,128)S(1)}, u32[]{:S(2)}, u32[]{:S(2)}) collective-permute-start(f32[2,4,16,512]{3,2,1,0:T(8,128)} %get-tuple-element.64), channel_id=1, source_target_pairs={{0,1},{1,0},{2,3},{3,2},{4,5},{5,4},{6,7},{7,6},{8,9},{9,8},{10,11... | collective-permute-start | bytes 786440 | tf_op jit(solution)/shard_map/ppermute | solution.py:569
  202.1 70.4 %collective-permute-start.21 = (f32[2,4,16,512]{3,2,1,0:T(8,128)}, f32[2,4,16,512]{3,2,1,0:T(8,128)S(1)}, u32[]{:S(2)}, u32[]{:S(2)}) collective-permute-start(f32[2,4,16,512]{3,2,1,0:T(8,128)} %get-tuple-element.65), channel_id=1, source_target_pairs={{0,2},{1,3},{2,0},{3,1},{4,6},{5,7},{6,4},{7,5},{8,10},{9,11},{10,... | collective-permute-start | bytes 786440 | tf_op jit(solution)/shard_map/ppermute | solution.py:569
  204.5 68.0 %collective-permute-start.22 = (f32[2,4,16,512]{3,2,1,0:T(8,128)}, f32[2,4,16,512]{3,2,1,0:T(8,128)S(1)}, u32[]{:S(2)}, u32[]{:S(2)}) collective-permute-start(f32[2,4,16,512]{3,2,1,0:T(8,128)} %get-tuple-element.66), channel_id=1, source_target_pairs={{0,3},{1,2},{2,1},{3,0},{4,7},{5,6},{6,5},{7,4},{8,11},{9,10},{10,... | collective-permute-start | bytes 786440 | tf_op jit(solution)/shard_map/ppermute | solution.py:569
  209.1 70.8 %collective-permute-start.7 = (f32[2,4,16,512]{3,2,1,0:T(8,128)}, f32[2,4,16,512]{3,2,1,0:T(8,128)S(1)}, u32[]{:S(2)}, u32[]{:S(2)}) collective-permute-start(f32[2,4,16,512]{3,2,1,0:T(8,128)} %get-tuple-element.48), channel_id=1, source_target_pairs={{0,1},{1,0},{2,3},{3,2},{4,5},{5,4},{6,7},{7,6},{8,9},{9,8},{10,11... | collective-permute-start | bytes 786440 | tf_op jit(solution)/shard_map/ppermute | solution.py:569
  209.7 74.1 %collective-permute-start.8 = (f32[2,4,16,512]{3,2,1,0:T(8,128)}, f32[2,4,16,512]{3,2,1,0:T(8,128)S(1)}, u32[]{:S(2)}, u32[]{:S(2)}) collective-permute-start(f32[2,4,16,512]{3,2,1,0:T(8,128)} %get-tuple-element.49), channel_id=1, source_target_pairs={{0,2},{1,3},{2,0},{3,1},{4,6},{5,7},{6,4},{7,5},{8,10},{9,11},{10,... | collective-permute-start | bytes 786440 | tf_op jit(solution)/shard_map/ppermute | solution.py:569
  235.7 48.1 %collective-permute-start.9 = (f32[2,4,16,512]{3,2,1,0:T(8,128)}, f32[2,4,16,512]{3,2,1,0:T(8,128)S(1)}, u32[]{:S(2)}, u32[]{:S(2)}) collective-permute-start(f32[2,4,16,512]{3,2,1,0:T(8,128)} %get-tuple-element.50), channel_id=1, source_target_pairs={{0,3},{1,2},{2,1},{3,0},{4,7},{5,6},{6,5},{7,4},{8,11},{9,10},{10,... | collective-permute-start | bytes 786440 | tf_op jit(solution)/shard_map/ppermute | solution.py:569

commit v3 on v2

--- a/solution.py
+++ b/solution.py
@@ -117,6 +117,27 @@
         out_shape=[pltpu.HBM((rows, lanes), jnp.float32)] * count,
         compiler_params=LIMIT,
         name="pack",
+    )(me, in_hbm(fields))
+
+
+def one_body(first, step, me_ref, fields_ref, out_ref, semaphore):
+    place = first + jnp.bitwise_xor(me_ref[0], step)
+    copy_all([(fields_ref.at[place], out_ref)], semaphore)[0].wait()
+
+
+def pack_one(me, fields, first, step):
+    return pl.pallas_call(
+        partial(one_body, first, step),
+        grid_spec=pltpu.PrefetchScalarGridSpec(
+            num_scalar_prefetch=1,
+            grid=(1,),
+            in_specs=[IN_HBM],
+            out_specs=IN_VMEM,
+            scratch_shapes=[pltpu.SemaphoreType.DMA((1,))],
+        ),
+        out_shape=pltpu.VMEM(fields.shape[1:], jnp.float32),
+        compiler_params=LIMIT,
+        name="pack_one",
     )(me, in_hbm(fields))
 
 
@@ -279,7 +300,7 @@
         out_shape=[pltpu.HBM(out, jnp.float32)] * Y_RADIX,
         compiler_params=LIMIT,
         name="y_lines",
-    )(me, spectra, twiddles, table)
+    )(me, in_hbm(spectra), twiddles, table)
 
 
 def finish_body(piece, me_ref, *refs):
@@ -291,7 +312,8 @@
     for level in range(levels):
         for step in range(Y_RADIX):
             at = pl.ds(pl.multiple_of(jnp.bitwise_xor(me_ref[0], step) * rows, rows), rows)
-            weight = mask_ref[at, :].astype(jnp.float32)
+            masked = pl.multiple_of(piece * rows_out + jnp.bitwise_xor(me_ref[0], step) * rows, rows)
+            weight = mask_ref[pl.ds(masked, rows), :].astype(jnp.float32)
             for part in range(2):
                 out_buffer[level, part, at, :] = blocks[step][part, level] * weight
         target = out_ref.at[:, level, pl.ds(piece * rows_out, rows_out), :]
@@ -310,7 +332,7 @@
             num_scalar_prefetch=1,
             grid=(1,),
             in_specs=[IN_VMEM] * Y_RADIX
-            + [pl.BlockSpec((rows_out, width), lambda *_: (piece, 0))]
+            + [IN_VMEM]
             + [IN_HBM] * len(extra),
             out_specs=IN_HBM,
             scratch_shapes=[
@@ -322,7 +344,7 @@
         input_output_aliases={} if before is None else {2 + Y_RADIX: 0},
         compiler_params=LIMIT,
         name="finish",
-    )(me, in_hbm(blocks[0]), *on_chip(*blocks[1:]), kept_mask, *extra)
+    )(me, *on_chip(*blocks, kept_mask), *extra)
 
 
 def turn(values):
@@ -583,7 +605,14 @@
     scale = 1.0 / math.sqrt(nx * ny)
     whole = ("gx", "gy")
     second = levels
-    fields_second = exchange(pack(y_me, fields, second, 1), "gy", gy)
+    leaving = []
+    for step in range(1, gy):
+        if step == gy // 2:
+            leaving.append(pack_one(y_me, fields, second, step))
+            continue
+        place = second + jnp.bitwise_xor(me_y, step)
+        leaving.append(lax.dynamic_index_in_dim(fields, place, 0, keepdims=False))
+    fields_second = exchange(leaving, "gy", gy)
     lines = exchange(pack(x_me, fields, 0, columns), "gx", gx)
     tables = x_table(nx, kept, zero), y_table(ny, scale, zero), y_twiddles(ny, zero)
     table_x, table_y, twiddles = lax.optimization_barrier(tables)

time: 289 us -> 288 us (level)
  transfers between devices with their start and end apart: 25 -> 25, of which waited for: 10 -> 9; matrix products, arithmetic and copies ran while one was open for 4% -> 4% of each run, Pallas kernels for 13% -> 12%
where the time goes in v3:
time: 288 us; the launch traced here: 285 us
  waiting for transfers between devices  145 us (50%)
  starting transfers between devices  49.4 us (17%)
  Pallas kernels  47.3 us (16%)
  blocking collectives  31.1 us (11%)
  other arithmetic  9.91 us (3%)
    ppermute x23, waiting for transfers between devices, exchange(): arrived[step] = lax.ppermute(blocks[step - 1], axis, pairs)  145 us
    all_to_all x1, blocking collectives, fast_shards(): lax.all_to_all(spectra[piece], whole, split_axis=0, concat_axis=0, tiled=...  31.1 us
    ppermute x23, starting transfers between devices, exchange(): arrived[step] = lax.ppermute(blocks[step - 1], axis, pairs)  31 us
    all_to_all x1, starting transfers between devices, fast_shards(): lax.all_to_all(owned, whole, split_axis=0, concat_axis=0, tiled=True)  13.8 us
    pallas_call x2, Pallas kernels, y_lines(): pl.pallas_call(y_body, grid_spec=pltpu.PrefetchScalarGridSpec(num_scalar_...  10.6 us
    pallas_call x1, Pallas kernels, y_first(): pl.pallas_call(partial(y_first_body, scale, first), grid_spec=pltpu.Prefe...  9.54 us
    cos x3, other arithmetic, roots(): return (jnp.cos(angles), jnp.sin(angles))  8.38 us
    pallas_call x1, Pallas kernels, x_lines(): pl.pallas_call(partial(x_body, gy, first, columns), grid_spec=pltpu.Prefe...  8.07 us
  transfers between devices with their start and end apart: 25, of which 9 were waited for; matrix products, arithmetic and copies ran while one was open for 4% of the time, Pallas kernels for 12%

profile of v3, /device:TPU:0, one launch (start us, length us, event | category | flops | bytes accessed | tf_op | source)
XLA Modules:
  0.0 285.1 jit_solution(2187077873854949654)
XLA Ops:
  0.0 2.8 pack.1
  3.3 2.6 collective-permute-start.1
  5.9 1.8 collective-permute-start.3
  7.8 4.1 %fusion.11 = (f32[4,2,1,128,256]{4,3,2,1,0:T(8,128)S(1)}, f32[4,2,1,128,256]{4,3,2,1,0:T(8,128)S(1)}) fusion(s32[256]{0:T(256)S(1)} %iota_add_fusion.1, s32[4,2,128]{2,1,0:T(2,128)S(1)} %broadcast_add_fusion), kind=kLoop, calls=%fused_computation.35 | loop fusion | flops 3670016 | bytes 2102272 | tf_op jit(solution)/shard_map/cos | solution.py:21
  12.5 4.1 %fusion.9 = (f32[512,512]{1,0:T(8,128)S(1)}, f32[512,512]{1,0:T(8,128)S(1)}) fusion(s32[512]{0:T(512)S(1)} %iota_add_fusion), kind=kLoop, calls=%fused_computation.33 | loop fusion | flops 3670016 | bytes 2099200 | tf_op jit(solution)/shard_map/cos | solution.py:21
  18.5 2.6 collective-permute-start.5
  21.3 7.3 %collective-permute-done.5.refs_5_ = f32[256,256]{1,0:T(8,128)S(1)} collective-permute-done((f32[256,256]{1,0:T(8,128)S(1)}, f32[256,256]{1,0:T(8,128)S(1)}, u32[]{:S(2)}, u32[]{:S(2)}) %collective-permute-start.5) | collective-permute-done | bytes 262176 | tf_op jit(solution)/shard_map/ppermute | solution.py:591
  28.6 4.5 %collective-permute-done.6.refs_6_ = f32[256,256]{1,0:T(8,128)S(1)} collective-permute-done((f32[256,256]{1,0:T(8,128)S(1)}, f32[256,256]{1,0:T(8,128)S(1)}, u32[]{:S(2)}, u32[]{:S(2)}) %collective-permute-start.6) | collective-permute-done | bytes 262176 | tf_op jit(solution)/shard_map/ppermute | solution.py:591
  33.1 8.1 %x_lines.1 = (f32[32,2,16,256]{3,2,1,0:T(8,128)}, f32[32,2,16,256]{3,2,1,0:T(8,128)}) custom-call(s32[1]{0:T(128)} %bitcast.1.me_ref, s32[1024]{0:T(1024)S(1)} %fusion.16.where_ref, f32[8,256,512]{2,1,0:T(8,128)} %fields_ref.7, f32[256,256]{1,0:T(8,128)S(1)} %collective-permute-done.refs_0_, f32[256,256]{1,0:T(8,128)S(1)} %collective-permute-done.1.refs_1_, ...), custom_call_target="tpu_custom_call" | custom-call | tf_op jit(solution)/shard_map/x_lines/pallas_call | solution.py:203
  41.2 31.1 %all_to_all.15.in_ref = f32[32,2,16,256]{3,2,1,0:T(8,128)} all-to-all(f32[32,2,16,256]{3,2,1,0:T(8,128)} %get-tuple-element.41), channel_id=1, replica_groups=mesh['gx'=8,'gy'=4] {'gx','gy'}, dimensions={0} | all-to-all | bytes 2097152 | tf_op jit(solution)/shard_map/all_to_all | solution.py:622
  72.3 4.7 %all-to-all-start.2 = ((f32[32,2,16,256]{3,2,1,0:T(8,128)}), f32[32,2,16,256]{3,2,1,0:T(8,128)}, u32[]{:S(2)}, u32[]{:S(2)}) async-start(f32[32,2,16,256]{3,2,1,0:T(8,128)} %get-tuple-element.56), calls=%async_computation.2 | async-start | bytes 2097152 | tf_op jit(solution)/shard_map/all_to_all | solution.py:622
  78.1 2.7 collective-permute-start.11
  82.0 1.5 collective-permute-start.12
  83.7 53.6 %collective-permute-done.11.refs_1_ = f32[256,512]{1,0:T(8,128)S(1)} collective-permute-done((f32[256,512]{1,0:T(8,128)S(1)}, f32[256,512]{1,0:T(8,128)S(1)}, u32[]{:S(2)}, u32[]{:S(2)}) %collective-permute-start.11) | collective-permute-done | bytes 524320 | tf_op jit(solution)/shard_map/ppermute | solution.py:591
  137.4 9.5 %y_first.1 = (f32[256,256]{1,0:T(8,128)}, f32[256,256]{1,0:T(8,128)}, f32[256,256]{1,0:T(8,128)}, f32[256,256]{1,0:T(8,128)}, f32[256,256]{1,0:T(8,128)}, /*inde...) custom-call(s32[2]{0:T(128)S(1)} %pad_add_fusion.me_ref, f32[8,256,512]{2,1,0:T(8,128)} %fields_ref.7, ...), custom_call_target="tpu_custom_call" | custom-call | tf_op jit(solution)/shard_map/y_first/pallas_call | solution.py:420
  147.0 1.5 collective-permute-start.14
  150.5 2.4 collective-permute-start.18
  152.9 3.5 %collective-permute-done.14.refs_2_ = f32[256,256]{1,0:T(8,128)S(1)} collective-permute-done((f32[256,256]{1,0:T(8,128)}, f32[256,256]{1,0:T(8,128)S(1)}, u32[]{:S(2)}, u32[]{:S(2)}) %collective-permute-start.14) | collective-permute-done | bytes 262176 | tf_op jit(solution)/shard_map/ppermute | solution.py:591
  157.5 3.7 %collective-permute-done.15.refs_3_ = f32[256,256]{1,0:T(8,128)S(1)} collective-permute-done((f32[256,256]{1,0:T(8,128)}, f32[256,256]{1,0:T(8,128)S(1)}, u32[]{:S(2)}, u32[]{:S(2)}) %collective-permute-start.15) | collective-permute-done | bytes 262176 | tf_op jit(solution)/shard_map/ppermute | solution.py:591
  161.2 12.7 %collective-permute-done.17.refs_5_ = f32[256,256]{1,0:T(8,128)S(1)} collective-permute-done((f32[256,256]{1,0:T(8,128)}, f32[256,256]{1,0:T(8,128)S(1)}, u32[]{:S(2)}, u32[]{:S(2)}) %collective-permute-start.17) | collective-permute-done | bytes 262176 | tf_op jit(solution)/shard_map/ppermute | solution.py:591
  173.9 7.7 %x_second.1 = f32[32,128,128]{2,1,0:T(8,128)} custom-call(s32[1]{0:T(128)} %bitcast.1.me_ref, s32[1024]{0:T(1024)S(1)} %fusion.16.where_ref, f32[256,256]{1,0:T(8,128)} %get-tuple-element.48.refs_0_, f32[256,256]{1,0:T(8,128)S(1)} %collective-permute-done.13.refs_1_, f32[256,256]{1,0:T(8,128)S(1)} %collective-permute-done.14.refs_2_, ...), custom_call_target="tpu_custom_call" | custom-call | tf_op jit(solution)/shard_map/x_second/pallas_call | solution.py:509
  181.6 13.8 %all-to-all-start.1 = ((f32[32,128,128]{2,1,0:T(8,128)}), f32[32,128,128]{2,1,0:T(8,128)}, u32[]{:S(2)}, u32[]{:S(2)}) async-start(f32[32,128,128]{2,1,0:T(8,128)} %x_second.1), calls=%async_computation.1 | async-start | bytes 4194304 | tf_op jit(solution)/shard_map/all_to_all | solution.py:626
  195.4 5.3 %y_lines.3 = (f32[2,4,16,512]{3,2,1,0:T(8,128)}, f32[2,4,16,512]{3,2,1,0:T(8,128)}, f32[2,4,16,512]{3,2,1,0:T(8,128)}, f32[2,4,16,512]{3,2,1,0:T(8,128)}) custom-call(s32[1]{0:T(128)} %bitcast.me_ref, f32[32,2,16,256]{3,2,1,0:T(8,128)} %all-to-all-done.2.in_ref, f32[8,512]{1,0:T(8,128)S(1)} %pad_maximum_fusion.3.twiddle_ref.refs_3_, ...), custom_call_target="tpu_custom_call" | custom-call | tf_op jit(solution)/shard_map/y_lines/pallas_call | solution.py:287
  200.7 1.5 collective-permute-start.20
  202.2 2.4 collective-permute-start.21
  205.1 5.3 %y_lines.2 = (f32[2,4,16,512]{3,2,1,0:T(8,128)}, f32[2,4,16,512]{3,2,1,0:T(8,128)}, f32[2,4,16,512]{3,2,1,0:T(8,128)}, f32[2,4,16,512]{3,2,1,0:T(8,128)}) custom-call(s32[1]{0:T(128)} %bitcast.me_ref, f32[32,2,16,256]{3,2,1,0:T(8,128)} %all_to_all.15.in_ref, f32[8,512]{1,0:T(8,128)S(1)} %pad_maximum_fusion.3.twiddle_ref.refs_3_, ...), custom_call_target="tpu_custom_call" | custom-call | tf_op jit(solution)/shard_map/y_lines/pallas_call | solution.py:287
  211.0 3.3 %collective-permute-start.8 = (f32[2,4,16,512]{3,2,1,0:T(8,128)}, f32[2,4,16,512]{3,2,1,0:T(8,128)S(1)}, u32[]{:S(2)}, u32[]{:S(2)}) collective-permute-start(f32[2,4,16,512]{3,2,1,0:T(8,128)} %get-tuple-element.46), channel_id=1, source_target_pairs={{0,2},{1,3},{2,0},{3,1},{4,6},{5,7},{6,4},{7,5},{8,10},{9,11},{10,... | collective-permute-start | bytes 786440 | tf_op jit(solution)/shard_map/ppermute | solution.py:591
  214.3 21.5 %collective-permute-done.20.refs_1_ = f32[2,4,16,512]{3,2,1,0:T(8,128)S(1)} collective-permute-done((f32[2,4,16,512]{3,2,1,0:T(8,128)}, f32[2,4,16,512]{3,2,1,0:T(8,128)S(1)}, u32[]{:S(2)}, u32[]{:S(2)}) %collective-permute-start.20) | collective-permute-done | bytes 262176 | tf_op jit(solution)/shard_map/ppermute | solution.py:591
  235.8 3.6 %collective-permute-start.9 = (f32[2,4,16,512]{3,2,1,0:T(8,128)}, f32[2,4,16,512]{3,2,1,0:T(8,128)S(1)}, u32[]{:S(2)}, u32[]{:S(2)}) collective-permute-start(f32[2,4,16,512]{3,2,1,0:T(8,128)} %get-tuple-element.47), channel_id=1, source_target_pairs={{0,3},{1,2},{2,1},{3,0},{4,7},{5,6},{6,5},{7,4},{8,11},{9,10},{10,... | collective-permute-start | bytes 786440 | tf_op jit(solution)/shard_map/ppermute | solution.py:591
  239.4 33.2 %collective-permute-done.21.refs_2_ = f32[2,4,16,512]{3,2,1,0:T(8,128)S(1)} collective-permute-done((f32[2,4,16,512]{3,2,1,0:T(8,128)}, f32[2,4,16,512]{3,2,1,0:T(8,128)S(1)}, u32[]{:S(2)}, u32[]{:S(2)}) %collective-permute-start.21) | collective-permute-done | bytes 262176 | tf_op jit(solution)/shard_map/ppermute | solution.py:591
  273.7 5.4 %finish_second.1.refs_5_ = f32[2,8,128,512]{3,2,1,0:T(8,128)} custom-call(s32[1]{0:T(128)} %bitcast.me_ref, f32[8,4,128,128]{3,2,1,0:T(8,128)} %bitcast.9.blocks_ref, s32[128,512]{1,0:T(8,128)S(1)} %copy-done.2, f32[2,8,128,512]{3,2,1,0:T(8,128)} %finish.2.before_ref), custom_call_target="tpu_custom_call", output_to_operand_aliasing={{}: (3, {})} | custom-call | tf_op jit(solution)/shard_map/finish_second/pallas_call | solution.py:568
  279.2 4.7 %collective-permute-done.8.refs_2_ = f32[2,4,16,512]{3,2,1,0:T(8,128)S(1)} collective-permute-done((f32[2,4,16,512]{3,2,1,0:T(8,128)}, f32[2,4,16,512]{3,2,1,0:T(8,128)S(1)}, u32[]{:S(2)}, u32[]{:S(2)}) %collective-permute-start.8) | collective-permute-done | bytes 262176 | tf_op jit(solution)/shard_map/ppermute | solution.py:591
  (64 shorter events, 12.0 us)
Async XLA Ops:
  0.0 7.7 %copy-start.6 = (s32[4,2]{1,0:T(4,128)S(1)}, s32[4,2]{1,0:T(4,128)}, u32[]{:S(2)}) copy-start(s32[4,2]{1,0:T(4,128)} %constant.107.clone) | copy-start | bytes 100
  2.8 15.1 %collective-permute-start = (f32[256,256]{1,0:T(8,128)}, f32[256,256]{1,0:T(8,128)S(1)}, u32[]{:S(2)}, u32[]{:S(2)}) collective-permute-start(f32[256,256]{1,0:T(8,128)} %get-tuple-element.33), channel_id=1, source_target_pairs={{0,4},{4,0},{8,12},{12,8},{16,20},{20,16},{24,28},{28,24},{1,5},{5... | collective-permute-start | bytes 786440 | tf_op jit(solution)/shard_map/ppermute | solution.py:591
  3.3 17.8 %collective-permute-start.1 = (f32[256,256]{1,0:T(8,128)}, f32[256,256]{1,0:T(8,128)S(1)}, u32[]{:S(2)}, u32[]{:S(2)}) collective-permute-start(f32[256,256]{1,0:T(8,128)} %get-tuple-element.34), channel_id=1, source_target_pairs={{0,8},{4,12},{8,0},{12,4},{16,24},{20,28},{24,16},{28,20},{1,9},{5... | collective-permute-start | bytes 786440 | tf_op jit(solution)/shard_map/ppermute | solution.py:591
  5.9 15.4 %collective-permute-start.2 = (f32[256,256]{1,0:T(8,128)}, f32[256,256]{1,0:T(8,128)S(1)}, u32[]{:S(2)}, u32[]{:S(2)}) collective-permute-start(f32[256,256]{1,0:T(8,128)} %get-tuple-element.35), channel_id=1, source_target_pairs={{0,12},{4,8},{8,4},{12,0},{16,28},{20,24},{24,20},{28,16},{1,13},{... | collective-permute-start | bytes 786440 | tf_op jit(solution)/shard_map/ppermute | solution.py:591
  5.9 15.4 %collective-permute-start.3 = (f32[256,256]{1,0:T(8,128)}, f32[256,256]{1,0:T(8,128)S(1)}, u32[]{:S(2)}, u32[]{:S(2)}) collective-permute-start(f32[256,256]{1,0:T(8,128)} %get-tuple-element.36), channel_id=1, source_target_pairs={{0,16},{4,20},{8,24},{12,28},{16,0},{20,4},{24,8},{28,12},{1,17},{... | collective-permute-start | bytes 786440 | tf_op jit(solution)/shard_map/ppermute | solution.py:591
  7.7 13.6 %collective-permute-start.4 = (f32[256,256]{1,0:T(8,128)}, f32[256,256]{1,0:T(8,128)S(1)}, u32[]{:S(2)}, u32[]{:S(2)}) collective-permute-start(f32[256,256]{1,0:T(8,128)} %get-tuple-element.37), channel_id=1, source_target_pairs={{0,20},{4,16},{8,28},{12,24},{16,4},{20,0},{24,12},{28,8},{1,21},{... | collective-permute-start | bytes 786440 | tf_op jit(solution)/shard_map/ppermute | solution.py:591
  16.9 16.3 %copy-start = (bf16[4,512,512]{2,1,0:T(8,128)(2,1)}, bf16[4,512,512]{2,1,0:T(8,128)(2,1)S(1)}, u32[]{:S(2)}) copy-start(bf16[4,512,512]{2,1,0:T(8,128)(2,1)S(1)} %pad_maximum_fusion.1.refs_7_.refs_8_) | copy-start | bytes 6291460
  17.5 3.8 %copy-start.5 = (s32[1024]{0:T(1024)S(1)}, s32[1024]{0:T(1024)}, u32[]{:S(2)}) copy-start(s32[1024]{0:T(1024)} %param.5) | copy-start | bytes 12292
  18.5 10.1 %collective-permute-start.5 = (f32[256,256]{1,0:T(8,128)S(1)}, f32[256,256]{1,0:T(8,128)S(1)}, u32[]{:S(2)}, u32[]{:S(2)}) collective-permute-start(f32[256,256]{1,0:T(8,128)S(1)} %copy-done.8), channel_id=1, source_target_pairs={{0,24},{4,28},{8,16},{12,20},{16,8},{20,12},{24,0},{28,4},{1,25},{... | collective-permute-start | bytes 786440 | tf_op jit(solution)/shard_map/ppermute | solution.py:591
  21.2 12.0 %collective-permute-start.6 = (f32[256,256]{1,0:T(8,128)S(1)}, f32[256,256]{1,0:T(8,128)S(1)}, u32[]{:S(2)}, u32[]{:S(2)}) collective-permute-start(f32[256,256]{1,0:T(8,128)S(1)} %copy-done.7), channel_id=1, source_target_pairs={{0,28},{4,24},{8,20},{12,16},{16,12},{20,8},{24,4},{28,0},{1,29},{... | collective-permute-start | bytes 786440 | tf_op jit(solution)/shard_map/ppermute | solution.py:591
  72.3 109.3 %all-to-all-start.2 = ((f32[32,2,16,256]{3,2,1,0:T(8,128)}), f32[32,2,16,256]{3,2,1,0:T(8,128)}, u32[]{:S(2)}, u32[]{:S(2)}) async-start(f32[32,2,16,256]{3,2,1,0:T(8,128)} %get-tuple-element.56), calls=%async_computation.2 | async-start | bytes 2097152 | tf_op jit(solution)/shard_map/all_to_all | solution.py:622
  78.1 59.3 %collective-permute-start.11 = (f32[256,512]{1,0:T(8,128)S(1)}, f32[256,512]{1,0:T(8,128)S(1)}, u32[]{:S(2)}, u32[]{:S(2)}) collective-permute-start(f32[256,512]{1,0:T(8,128)S(1)} %pack_one.1), channel_id=1, source_target_pairs={{0,2},{1,3},{2,0},{3,1},{4,6},{5,7},{6,4},{7,5},{8,10},{9,11},{10,... | collective-permute-start | bytes 1572872 | tf_op jit(solution)/shard_map/ppermute | solution.py:591
  82.0 55.4 %collective-permute-start.12 = (f32[256,512]{1,0:T(8,128)S(1)}, f32[256,512]{1,0:T(8,128)S(1)}, u32[]{:S(2)}, u32[]{:S(2)}) collective-permute-start(f32[256,512]{1,0:T(8,128)S(1)} %get-tuple-element.61), channel_id=1, source_target_pairs={{0,3},{1,2},{2,1},{3,0},{4,7},{5,6},{6,5},{7,4},{8,11},{9,10},{10,... | collective-permute-start | bytes 1572872 | tf_op jit(solution)/shard_map/ppermute | solution.py:591
  83.5 53.8 %collective-permute-start.10 = (f32[256,512]{1,0:T(8,128)S(1)}, f32[256,512]{1,0:T(8,128)S(1)}, u32[]{:S(2)}, u32[]{:S(2)}) collective-permute-start(f32[256,512]{1,0:T(8,128)S(1)} %get-tuple-element.62), channel_id=1, source_target_pairs={{0,1},{1,0},{2,3},{3,2},{4,5},{5,4},{6,7},{7,6},{8,9},{9,8},{10,11... | collective-permute-start | bytes 1572872 | tf_op jit(solution)/shard_map/ppermute | solution.py:591
  83.7 90.1 %copy-start.1 = (bf16[4,512,512]{2,1,0:T(8,128)(2,1)S(1)}, bf16[4,512,512]{2,1,0:T(8,128)(2,1)}, u32[]{:S(2)}) copy-start(bf16[4,512,512]{2,1,0:T(8,128)(2,1)} %copy-done) | copy-start | bytes 6291460
  146.9 3.6 %collective-permute-start.13 = (f32[256,256]{1,0:T(8,128)}, f32[256,256]{1,0:T(8,128)S(1)}, u32[]{:S(2)}, u32[]{:S(2)}) collective-permute-start(f32[256,256]{1,0:T(8,128)} %get-tuple-element.49), channel_id=1, source_target_pairs={{0,4},{4,0},{8,12},{12,8},{16,20},{20,16},{24,28},{28,24},{1,5},{5... | collective-permute-start | bytes 786440 | tf_op jit(solution)/shard_map/ppermute | solution.py:591
  147.0 9.5 %collective-permute-start.14 = (f32[256,256]{1,0:T(8,128)}, f32[256,256]{1,0:T(8,128)S(1)}, u32[]{:S(2)}, u32[]{:S(2)}) collective-permute-start(f32[256,256]{1,0:T(8,128)} %get-tuple-element.50), channel_id=1, source_target_pairs={{0,8},{4,12},{8,0},{12,4},{16,24},{20,28},{24,16},{28,20},{1,9},{5... | collective-permute-start | bytes 786440 | tf_op jit(solution)/shard_map/ppermute | solution.py:591
  148.5 12.6 %collective-permute-start.15 = (f32[256,256]{1,0:T(8,128)}, f32[256,256]{1,0:T(8,128)S(1)}, u32[]{:S(2)}, u32[]{:S(2)}) collective-permute-start(f32[256,256]{1,0:T(8,128)} %get-tuple-element.51), channel_id=1, source_target_pairs={{0,12},{4,8},{8,4},{12,0},{16,28},{20,24},{24,20},{28,16},{1,13},{... | collective-permute-start | bytes 786440 | tf_op jit(solution)/shard_map/ppermute | solution.py:591
  148.8 12.3 %collective-permute-start.16 = (f32[256,256]{1,0:T(8,128)}, f32[256,256]{1,0:T(8,128)S(1)}, u32[]{:S(2)}, u32[]{:S(2)}) collective-permute-start(f32[256,256]{1,0:T(8,128)} %get-tuple-element.52), channel_id=1, source_target_pairs={{0,16},{4,20},{8,24},{12,28},{16,0},{20,4},{24,8},{28,12},{1,17},{... | collective-permute-start | bytes 786440 | tf_op jit(solution)/shard_map/ppermute | solution.py:591
  150.3 23.5 %collective-permute-start.17 = (f32[256,256]{1,0:T(8,128)}, f32[256,256]{1,0:T(8,128)S(1)}, u32[]{:S(2)}, u32[]{:S(2)}) collective-permute-start(f32[256,256]{1,0:T(8,128)} %get-tuple-element.53), channel_id=1, source_target_pairs={{0,20},{4,16},{8,28},{12,24},{16,4},{20,0},{24,12},{28,8},{1,21},{... | collective-permute-start | bytes 786440 | tf_op jit(solution)/shard_map/ppermute | solution.py:591
  150.5 23.3 %collective-permute-start.18 = (f32[256,256]{1,0:T(8,128)}, f32[256,256]{1,0:T(8,128)S(1)}, u32[]{:S(2)}, u32[]{:S(2)}) collective-permute-start(f32[256,256]{1,0:T(8,128)} %get-tuple-element.54), channel_id=1, source_target_pairs={{0,24},{4,28},{8,16},{12,20},{16,8},{20,12},{24,0},{28,4},{1,25},{... | collective-permute-start | bytes 786440 | tf_op jit(solution)/shard_map/ppermute | solution.py:591
  156.4 17.4 %collective-permute-start.19 = (f32[256,256]{1,0:T(8,128)}, f32[256,256]{1,0:T(8,128)S(1)}, u32[]{:S(2)}, u32[]{:S(2)}) collective-permute-start(f32[256,256]{1,0:T(8,128)} %get-tuple-element.55), channel_id=1, source_target_pairs={{0,28},{4,24},{8,20},{12,16},{16,12},{20,8},{24,4},{28,0},{1,29},{... | collective-permute-start | bytes 786440 | tf_op jit(solution)/shard_map/ppermute | solution.py:591
  181.6 92.1 %all-to-all-start.1 = ((f32[32,128,128]{2,1,0:T(8,128)}), f32[32,128,128]{2,1,0:T(8,128)}, u32[]{:S(2)}, u32[]{:S(2)}) async-start(f32[32,128,128]{2,1,0:T(8,128)} %x_second.1), calls=%async_computation.1 | async-start | bytes 4194304 | tf_op jit(solution)/shard_map/all_to_all | solution.py:626
  200.7 71.9 %copy-start.2 = (s32[128,512]{1,0:T(8,128)S(1)}, s32[128,512]{1,0:T(8,128)}, u32[]{:S(2)}) copy-start(s32[128,512]{1,0:T(8,128)} %refs_4_.3) | copy-start | bytes 786436
  200.7 71.9 %copy-start.4 = (f32[2,4,16,512]{3,2,1,0:T(8,128)S(1)}, f32[2,4,16,512]{3,2,1,0:T(8,128)}, u32[]{:S(2)}) copy-start(f32[2,4,16,512]{3,2,1,0:T(8,128)} %get-tuple-element.57.refs_0_) | copy-start | bytes 786436
  200.7 35.1 %collective-permute-start.20 = (f32[2,4,16,512]{3,2,1,0:T(8,128)}, f32[2,4,16,512]{3,2,1,0:T(8,128)S(1)}, u32[]{:S(2)}, u32[]{:S(2)}) collective-permute-start(f32[2,4,16,512]{3,2,1,0:T(8,128)} %get-tuple-element.58), channel_id=1, source_target_pairs={{0,1},{1,0},{2,3},{3,2},{4,5},{5,4},{6,7},{7,6},{8,9},{9,8},{10,11... | collective-permute-start | bytes 786440 | tf_op jit(solution)/shard_map/ppermute | solution.py:591
  202.2 70.4 %collective-permute-start.21 = (f32[2,4,16,512]{3,2,1,0:T(8,128)}, f32[2,4,16,512]{3,2,1,0:T(8,128)S(1)}, u32[]{:S(2)}, u32[]{:S(2)}) collective-permute-start(f32[2,4,16,512]{3,2,1,0:T(8,128)} %get-tuple-element.59), channel_id=1, source_target_pairs={{0,2},{1,3},{2,0},{3,1},{4,6},{5,7},{6,4},{7,5},{8,10},{9,11},{10,... | collective-permute-start | bytes 786440 | tf_op jit(solution)/shard_map/ppermute | solution.py:591
  204.6 68.0 %collective-permute-start.22 = (f32[2,4,16,512]{3,2,1,0:T(8,128)}, f32[2,4,16,512]{3,2,1,0:T(8,128)S(1)}, u32[]{:S(2)}, u32[]{:S(2)}) collective-permute-start(f32[2,4,16,512]{3,2,1,0:T(8,128)} %get-tuple-element.60), channel_id=1, source_target_pairs={{0,3},{1,2},{2,1},{3,0},{4,7},{5,6},{6,5},{7,4},{8,11},{9,10},{10,... | collective-permute-start | bytes 786440 | tf_op jit(solution)/shard_map/ppermute | solution.py:591
  210.4 68.7 %collective-permute-start.7 = (f32[2,4,16,512]{3,2,1,0:T(8,128)}, f32[2,4,16,512]{3,2,1,0:T(8,128)S(1)}, u32[]{:S(2)}, u32[]{:S(2)}) collective-permute-start(f32[2,4,16,512]{3,2,1,0:T(8,128)} %get-tuple-element.45), channel_id=1, source_target_pairs={{0,1},{1,0},{2,3},{3,2},{4,5},{5,4},{6,7},{7,6},{8,9},{9,8},{10,11... | collective-permute-start | bytes 786440 | tf_op jit(solution)/shard_map/ppermute | solution.py:591
  211.0 72.9 %collective-permute-start.8 = (f32[2,4,16,512]{3,2,1,0:T(8,128)}, f32[2,4,16,512]{3,2,1,0:T(8,128)S(1)}, u32[]{:S(2)}, u32[]{:S(2)}) collective-permute-start(f32[2,4,16,512]{3,2,1,0:T(8,128)} %get-tuple-element.46), channel_id=1, source_target_pairs={{0,2},{1,3},{2,0},{3,1},{4,6},{5,7},{6,4},{7,5},{8,10},{9,11},{10,... | collective-permute-start | bytes 786440 | tf_op jit(solution)/shard_map/ppermute | solution.py:591
  235.8 48.1 %collective-permute-start.9 = (f32[2,4,16,512]{3,2,1,0:T(8,128)}, f32[2,4,16,512]{3,2,1,0:T(8,128)S(1)}, u32[]{:S(2)}, u32[]{:S(2)}) collective-permute-start(f32[2,4,16,512]{3,2,1,0:T(8,128)} %get-tuple-element.47), channel_id=1, source_target_pairs={{0,3},{1,2},{2,1},{3,0},{4,7},{5,6},{6,5},{7,4},{8,11},{9,10},{10,... | collective-permute-start | bytes 786440 | tf_op jit(solution)/shard_map/ppermute | solution.py:591
  273.7 10.2 %copy-start.3 = (f32[2,4,16,512]{3,2,1,0:T(8,128)S(1)}, f32[2,4,16,512]{3,2,1,0:T(8,128)}, u32[]{:S(2)}) copy-start(f32[2,4,16,512]{3,2,1,0:T(8,128)} %get-tuple-element.44.refs_0_) | copy-start | bytes 786436
  (2 other events, 4.7 us)

commit v4 on v3

--- a/solution.py
+++ b/solution.py
@@ -114,7 +114,10 @@
             out_specs=[IN_VMEM] * count,
             scratch_shapes=[pltpu.SemaphoreType.DMA((count,))],
         ),
-        out_shape=[pltpu.HBM((rows, lanes), jnp.float32)] * count,
+        out_shape=[
+            (pltpu.VMEM if step > count // 2 else pltpu.HBM)((rows, lanes), jnp.float32)
+            for step in range(1, count + 1)
+        ],
         compiler_params=LIMIT,
         name="pack",
     )(me, in_hbm(fields))
@@ -297,7 +300,7 @@
                 pltpu.VMEM((Y_RADIX, Y_RADIX, 2 * levels * rows, short // Y_RADIX), jnp.float32),
             ],
         ),
-        out_shape=[pltpu.HBM(out, jnp.float32)] * Y_RADIX,
+        out_shape=[pltpu.HBM(out, jnp.float32)] + [pltpu.VMEM(out, jnp.float32)] * (Y_RADIX - 1),
         compiler_params=LIMIT,
         name="y_lines",
     )(me, in_hbm(spectra), twiddles, table)

time: 288 us -> 290 us (level)
  no operation moved by 1% of the time
where the time goes in v4:
time: 290 us; the launch traced here: 286 us
  waiting for transfers between devices  145 us (50%)
  starting transfers between devices  49.4 us (17%)
  Pallas kernels  46.8 us (16%)
  blocking collectives  31.2 us (11%)
  other arithmetic  9.91 us (3%)
  local copies, waits for them, and re-layouts  3.62 us (1%)
    ppermute x23, waiting for transfers between devices, exchange(): arrived[step] = lax.ppermute(blocks[step - 1], axis, pairs)  145 us
    all_to_all x1, blocking collectives, fast_shards(): lax.all_to_all(spectra[piece], whole, split_axis=0, concat_axis=0, tiled=...  31.2 us
    ppermute x23, starting transfers between devices, exchange(): arrived[step] = lax.ppermute(blocks[step - 1], axis, pairs)  30.9 us
    all_to_all x1, starting transfers between devices, fast_shards(): lax.all_to_all(owned, whole, split_axis=0, concat_axis=0, tiled=True)  13.8 us
    pallas_call x2, Pallas kernels, y_lines(): pl.pallas_call(y_body, grid_spec=pltpu.PrefetchScalarGridSpec(num_scalar_...  10.4 us
    pallas_call x1, Pallas kernels, y_first(): pl.pallas_call(partial(y_first_body, scale, first), grid_spec=pltpu.Prefe...  9.54 us
    cos x3, other arithmetic, roots(): return (jnp.cos(angles), jnp.sin(angles))  8.38 us
    pallas_call x1, Pallas kernels, x_lines(): pl.pallas_call(partial(x_body, gy, first, columns), grid_spec=pltpu.Prefe...  8.07 us
  transfers between devices with their start and end apart: 25, of which 9 were waited for; matrix products, arithmetic and copies ran while one was open for 4% of the time, Pallas kernels for 12%

profile of v4, /device:TPU:0, one launch (start us, length us, event | category | flops | bytes accessed | tf_op | source)
XLA Modules:
  0.0 286.3 jit_solution(4747443475944863491)
XLA Ops:
  0.0 2.6 pack.1
  4.5 2.5 collective-permute-start.1
  7.1 1.8 collective-permute-start.3
  9.0 4.1 %fusion.11 = (f32[4,2,1,128,256]{4,3,2,1,0:T(8,128)S(1)}, f32[4,2,1,128,256]{4,3,2,1,0:T(8,128)S(1)}) fusion(s32[256]{0:T(256)S(1)} %iota_add_fusion.1, s32[4,2,128]{2,1,0:T(2,128)S(1)} %broadcast_add_fusion), kind=kLoop, calls=%fused_computation.35 | loop fusion | flops 3670016 | bytes 2102272 | tf_op jit(solution)/shard_map/cos | solution.py:21
  13.7 4.1 %fusion.9 = (f32[512,512]{1,0:T(8,128)S(1)}, f32[512,512]{1,0:T(8,128)S(1)}) fusion(s32[512]{0:T(512)S(1)} %iota_add_fusion), kind=kLoop, calls=%fused_computation.33 | loop fusion | flops 3670016 | bytes 2099200 | tf_op jit(solution)/shard_map/cos | solution.py:21
  19.7 2.6 collective-permute-start.5
  22.5 7.3 %collective-permute-done.5.refs_5_ = f32[256,256]{1,0:T(8,128)S(1)} collective-permute-done((f32[256,256]{1,0:T(8,128)S(1)}, f32[256,256]{1,0:T(8,128)S(1)}, u32[]{:S(2)}, u32[]{:S(2)}) %collective-permute-start.5) | collective-permute-done | bytes 262176 | tf_op jit(solution)/shard_map/ppermute | solution.py:594
  29.8 4.5 %collective-permute-done.6.refs_6_ = f32[256,256]{1,0:T(8,128)S(1)} collective-permute-done((f32[256,256]{1,0:T(8,128)S(1)}, f32[256,256]{1,0:T(8,128)S(1)}, u32[]{:S(2)}, u32[]{:S(2)}) %collective-permute-start.6) | collective-permute-done | bytes 262176 | tf_op jit(solution)/shard_map/ppermute | solution.py:594
  34.3 8.1 %x_lines.1 = (f32[32,2,16,256]{3,2,1,0:T(8,128)}, f32[32,2,16,256]{3,2,1,0:T(8,128)}) custom-call(s32[1]{0:T(128)} %bitcast.1.me_ref, s32[1024]{0:T(1024)S(1)} %fusion.16.where_ref, f32[8,256,512]{2,1,0:T(8,128)} %fields_ref.7, f32[256,256]{1,0:T(8,128)S(1)} %collective-permute-done.refs_0_, f32[256,256]{1,0:T(8,128)S(1)} %collective-permute-done.1.refs_1_, ...), custom_call_target="tpu_custom_call" | custom-call | tf_op jit(solution)/shard_map/x_lines/pallas_call | solution.py:206
  42.4 31.2 %all_to_all.15.in_ref = f32[32,2,16,256]{3,2,1,0:T(8,128)} all-to-all(f32[32,2,16,256]{3,2,1,0:T(8,128)} %get-tuple-element.41), channel_id=1, replica_groups=mesh['gx'=8,'gy'=4] {'gx','gy'}, dimensions={0} | all-to-all | bytes 2097152 | tf_op jit(solution)/shard_map/all_to_all | solution.py:625
  73.6 4.7 %all-to-all-start.2 = ((f32[32,2,16,256]{3,2,1,0:T(8,128)}), f32[32,2,16,256]{3,2,1,0:T(8,128)}, u32[]{:S(2)}, u32[]{:S(2)}) async-start(f32[32,2,16,256]{3,2,1,0:T(8,128)} %get-tuple-element.56), calls=%async_computation.2 | async-start | bytes 2097152 | tf_op jit(solution)/shard_map/all_to_all | solution.py:625
  79.3 2.7 collective-permute-start.11
  83.3 1.5 collective-permute-start.12
  85.0 53.6 %collective-permute-done.11.refs_1_ = f32[256,512]{1,0:T(8,128)S(1)} collective-permute-done((f32[256,512]{1,0:T(8,128)S(1)}, f32[256,512]{1,0:T(8,128)S(1)}, u32[]{:S(2)}, u32[]{:S(2)}) %collective-permute-start.11) | collective-permute-done | bytes 524320 | tf_op jit(solution)/shard_map/ppermute | solution.py:594
  138.6 9.5 %y_first.1 = (f32[256,256]{1,0:T(8,128)}, f32[256,256]{1,0:T(8,128)}, f32[256,256]{1,0:T(8,128)}, f32[256,256]{1,0:T(8,128)}, f32[256,256]{1,0:T(8,128)}, /*inde...) custom-call(s32[2]{0:T(128)S(1)} %pad_add_fusion.me_ref, f32[8,256,512]{2,1,0:T(8,128)} %fields_ref.7, ...), custom_call_target="tpu_custom_call" | custom-call | tf_op jit(solution)/shard_map/y_first/pallas_call | solution.py:423
  148.2 1.5 collective-permute-start.14
  151.8 2.4 collective-permute-start.18
  154.2 3.5 %collective-permute-done.14.refs_2_ = f32[256,256]{1,0:T(8,128)S(1)} collective-permute-done((f32[256,256]{1,0:T(8,128)}, f32[256,256]{1,0:T(8,128)S(1)}, u32[]{:S(2)}, u32[]{:S(2)}) %collective-permute-start.14) | collective-permute-done | bytes 262176 | tf_op jit(solution)/shard_map/ppermute | solution.py:594
  158.7 3.7 %collective-permute-done.15.refs_3_ = f32[256,256]{1,0:T(8,128)S(1)} collective-permute-done((f32[256,256]{1,0:T(8,128)}, f32[256,256]{1,0:T(8,128)S(1)}, u32[]{:S(2)}, u32[]{:S(2)}) %collective-permute-start.15) | collective-permute-done | bytes 262176 | tf_op jit(solution)/shard_map/ppermute | solution.py:594
  162.4 12.7 %collective-permute-done.17.refs_5_ = f32[256,256]{1,0:T(8,128)S(1)} collective-permute-done((f32[256,256]{1,0:T(8,128)}, f32[256,256]{1,0:T(8,128)S(1)}, u32[]{:S(2)}, u32[]{:S(2)}) %collective-permute-start.17) | collective-permute-done | bytes 262176 | tf_op jit(solution)/shard_map/ppermute | solution.py:594
  175.1 7.7 %x_second.1 = f32[32,128,128]{2,1,0:T(8,128)} custom-call(s32[1]{0:T(128)} %bitcast.1.me_ref, s32[1024]{0:T(1024)S(1)} %fusion.16.where_ref, f32[256,256]{1,0:T(8,128)} %get-tuple-element.48.refs_0_, f32[256,256]{1,0:T(8,128)S(1)} %collective-permute-done.13.refs_1_, f32[256,256]{1,0:T(8,128)S(1)} %collective-permute-done.14.refs_2_, ...), custom_call_target="tpu_custom_call" | custom-call | tf_op jit(solution)/shard_map/x_second/pallas_call | solution.py:512
  182.8 13.8 %all-to-all-start.1 = ((f32[32,128,128]{2,1,0:T(8,128)}), f32[32,128,128]{2,1,0:T(8,128)}, u32[]{:S(2)}, u32[]{:S(2)}) async-start(f32[32,128,128]{2,1,0:T(8,128)} %x_second.1), calls=%async_computation.1 | async-start | bytes 4194304 | tf_op jit(solution)/shard_map/all_to_all | solution.py:629
  196.7 5.2 %y_lines.3 = (f32[2,4,16,512]{3,2,1,0:T(8,128)}, f32[2,4,16,512]{3,2,1,0:T(8,128)S(1)}, f32[2,4,16,512]{3,2,1,0:T(8,128)S(1)}, f32[2,4,16,512]{3,2,1,0:T(8,128)S(1)}) custom-call(s32[1]{0:T(128)} %bitcast.me_ref, f32[32,2,16,256]{3,2,1,0:T(8,128)} %all-to-all-done.2.in_ref, f32[8,512]{1,0:T(8,128)S(1)} %pad_maximum_fusion.3.twiddle_ref.refs_3_, ...), custom_call_target="tpu_custom_call" | custom-call | tf_op jit(solution)/shard_map/y_lines/pallas_call | solution.py:290
  201.9 1.5 collective-permute-start.20
  203.4 2.4 collective-permute-start.21
  206.2 5.2 %y_lines.2 = (f32[2,4,16,512]{3,2,1,0:T(8,128)}, f32[2,4,16,512]{3,2,1,0:T(8,128)S(1)}, f32[2,4,16,512]{3,2,1,0:T(8,128)S(1)}, f32[2,4,16,512]{3,2,1,0:T(8,128)S(1)}) custom-call(s32[1]{0:T(128)} %bitcast.me_ref, f32[32,2,16,256]{3,2,1,0:T(8,128)} %all_to_all.15.in_ref, f32[8,512]{1,0:T(8,128)S(1)} %pad_maximum_fusion.3.twiddle_ref.refs_3_, ...), custom_call_target="tpu_custom_call" | custom-call | tf_op jit(solution)/shard_map/y_lines/pallas_call | solution.py:290
  212.0 3.3 %collective-permute-start.8 = (f32[2,4,16,512]{3,2,1,0:T(8,128)S(1)}, f32[2,4,16,512]{3,2,1,0:T(8,128)S(1)}, u32[]{:S(2)}, u32[]{:S(2)}) collective-permute-start(f32[2,4,16,512]{3,2,1,0:T(8,128)S(1)} %get-tuple-element.46), channel_id=1, source_target_pairs={{0,2},{1,3},{2,0},{3,1},{4,6},{5,7},{6,4},{7,5},{8,10},{9,11},{10,... | collective-permute-start | bytes 786440 | tf_op jit(solution)/shard_map/ppermute | solution.py:594
  215.4 21.6 %collective-permute-done.20.refs_1_ = f32[2,4,16,512]{3,2,1,0:T(8,128)S(1)} collective-permute-done((f32[2,4,16,512]{3,2,1,0:T(8,128)S(1)}, f32[2,4,16,512]{3,2,1,0:T(8,128)S(1)}, u32[]{:S(2)}, u32[]{:S(2)}) %collective-permute-start.20) | collective-permute-done | bytes 262176 | tf_op jit(solution)/shard_map/ppermute | solution.py:594
  237.0 3.6 %collective-permute-start.9 = (f32[2,4,16,512]{3,2,1,0:T(8,128)S(1)}, f32[2,4,16,512]{3,2,1,0:T(8,128)S(1)}, u32[]{:S(2)}, u32[]{:S(2)}) collective-permute-start(f32[2,4,16,512]{3,2,1,0:T(8,128)S(1)} %get-tuple-element.47), channel_id=1, source_target_pairs={{0,3},{1,2},{2,1},{3,0},{4,7},{5,6},{6,5},{7,4},{8,11},{9,10},{10,... | collective-permute-start | bytes 786440 | tf_op jit(solution)/shard_map/ppermute | solution.py:594
  240.6 33.3 %collective-permute-done.21.refs_2_ = f32[2,4,16,512]{3,2,1,0:T(8,128)S(1)} collective-permute-done((f32[2,4,16,512]{3,2,1,0:T(8,128)S(1)}, f32[2,4,16,512]{3,2,1,0:T(8,128)S(1)}, u32[]{:S(2)}, u32[]{:S(2)}) %collective-permute-start.21) | collective-permute-done | bytes 262176 | tf_op jit(solution)/shard_map/ppermute | solution.py:594
  275.0 5.4 %finish_second.1.refs_5_ = f32[2,8,128,512]{3,2,1,0:T(8,128)} custom-call(s32[1]{0:T(128)} %bitcast.me_ref, f32[8,4,128,128]{3,2,1,0:T(8,128)} %bitcast.9.blocks_ref, s32[128,512]{1,0:T(8,128)S(1)} %copy-done.2, f32[2,8,128,512]{3,2,1,0:T(8,128)} %finish.2.before_ref), custom_call_target="tpu_custom_call", output_to_operand_aliasing={{}: (3, {})} | custom-call | tf_op jit(solution)/shard_map/finish_second/pallas_call | solution.py:571
  280.4 4.7 %collective-permute-done.8.refs_2_ = f32[2,4,16,512]{3,2,1,0:T(8,128)S(1)} collective-permute-done((f32[2,4,16,512]{3,2,1,0:T(8,128)S(1)}, f32[2,4,16,512]{3,2,1,0:T(8,128)S(1)}, u32[]{:S(2)}, u32[]{:S(2)}) %collective-permute-start.8) | collective-permute-done | bytes 262176 | tf_op jit(solution)/shard_map/ppermute | solution.py:594
  (68 shorter events, 13.5 us)
Async XLA Ops:
  0.0 8.9 %copy-start.10 = (s32[4,2]{1,0:T(4,128)S(1)}, s32[4,2]{1,0:T(4,128)}, u32[]{:S(2)}) copy-start(s32[4,2]{1,0:T(4,128)} %constant.107.clone) | copy-start | bytes 100
  4.0 15.0 %collective-permute-start = (f32[256,256]{1,0:T(8,128)}, f32[256,256]{1,0:T(8,128)S(1)}, u32[]{:S(2)}, u32[]{:S(2)}) collective-permute-start(f32[256,256]{1,0:T(8,128)} %get-tuple-element.33), channel_id=1, source_target_pairs={{0,4},{4,0},{8,12},{12,8},{16,20},{20,16},{24,28},{28,24},{1,5},{5... | collective-permute-start | bytes 786440 | tf_op jit(solution)/shard_map/ppermute | solution.py:594
  4.5 17.7 %collective-permute-start.1 = (f32[256,256]{1,0:T(8,128)}, f32[256,256]{1,0:T(8,128)S(1)}, u32[]{:S(2)}, u32[]{:S(2)}) collective-permute-start(f32[256,256]{1,0:T(8,128)} %get-tuple-element.34), channel_id=1, source_target_pairs={{0,8},{4,12},{8,0},{12,4},{16,24},{20,28},{24,16},{28,20},{1,9},{5... | collective-permute-start | bytes 786440 | tf_op jit(solution)/shard_map/ppermute | solution.py:594
  7.0 15.5 %collective-permute-start.2 = (f32[256,256]{1,0:T(8,128)}, f32[256,256]{1,0:T(8,128)S(1)}, u32[]{:S(2)}, u32[]{:S(2)}) collective-permute-start(f32[256,256]{1,0:T(8,128)} %get-tuple-element.35), channel_id=1, source_target_pairs={{0,12},{4,8},{8,4},{12,0},{16,28},{20,24},{24,20},{28,16},{1,13},{... | collective-permute-start | bytes 786440 | tf_op jit(solution)/shard_map/ppermute | solution.py:594
  7.1 15.4 %collective-permute-start.3 = (f32[256,256]{1,0:T(8,128)}, f32[256,256]{1,0:T(8,128)S(1)}, u32[]{:S(2)}, u32[]{:S(2)}) collective-permute-start(f32[256,256]{1,0:T(8,128)} %get-tuple-element.36), channel_id=1, source_target_pairs={{0,16},{4,20},{8,24},{12,28},{16,0},{20,4},{24,8},{28,12},{1,17},{... | collective-permute-start | bytes 786440 | tf_op jit(solution)/shard_map/ppermute | solution.py:594
  8.9 13.6 %collective-permute-start.4 = (f32[256,256]{1,0:T(8,128)}, f32[256,256]{1,0:T(8,128)S(1)}, u32[]{:S(2)}, u32[]{:S(2)}) collective-permute-start(f32[256,256]{1,0:T(8,128)} %get-tuple-element.37), channel_id=1, source_target_pairs={{0,20},{4,16},{8,28},{12,24},{16,4},{20,0},{24,12},{28,8},{1,21},{... | collective-permute-start | bytes 786440 | tf_op jit(solution)/shard_map/ppermute | solution.py:594
  18.0 16.3 %copy-start = (bf16[4,512,512]{2,1,0:T(8,128)(2,1)}, bf16[4,512,512]{2,1,0:T(8,128)(2,1)S(1)}, u32[]{:S(2)}) copy-start(bf16[4,512,512]{2,1,0:T(8,128)(2,1)S(1)} %pad_maximum_fusion.1.refs_7_.refs_8_) | copy-start | bytes 6291460
  18.7 3.8 %copy-start.9 = (s32[1024]{0:T(1024)S(1)}, s32[1024]{0:T(1024)}, u32[]{:S(2)}) copy-start(s32[1024]{0:T(1024)} %param.5) | copy-start | bytes 12292
  19.7 10.1 %collective-permute-start.5 = (f32[256,256]{1,0:T(8,128)S(1)}, f32[256,256]{1,0:T(8,128)S(1)}, u32[]{:S(2)}, u32[]{:S(2)}) collective-permute-start(f32[256,256]{1,0:T(8,128)S(1)} %copy-done.8), channel_id=1, source_target_pairs={{0,24},{4,28},{8,16},{12,20},{16,8},{20,12},{24,0},{28,4},{1,25},{... | collective-permute-start | bytes 786440 | tf_op jit(solution)/shard_map/ppermute | solution.py:594
  22.3 12.0 %collective-permute-start.6 = (f32[256,256]{1,0:T(8,128)S(1)}, f32[256,256]{1,0:T(8,128)S(1)}, u32[]{:S(2)}, u32[]{:S(2)}) collective-permute-start(f32[256,256]{1,0:T(8,128)S(1)} %copy-done.6), channel_id=1, source_target_pairs={{0,28},{4,24},{8,20},{12,16},{16,12},{20,8},{24,4},{28,0},{1,29},{... | collective-permute-start | bytes 786440 | tf_op jit(solution)/shard_map/ppermute | solution.py:594
  73.6 109.3 %all-to-all-start.2 = ((f32[32,2,16,256]{3,2,1,0:T(8,128)}), f32[32,2,16,256]{3,2,1,0:T(8,128)}, u32[]{:S(2)}, u32[]{:S(2)}) async-start(f32[32,2,16,256]{3,2,1,0:T(8,128)} %get-tuple-element.56), calls=%async_computation.2 | async-start | bytes 2097152 | tf_op jit(solution)/shard_map/all_to_all | solution.py:625
  79.3 59.3 %collective-permute-start.11 = (f32[256,512]{1,0:T(8,128)S(1)}, f32[256,512]{1,0:T(8,128)S(1)}, u32[]{:S(2)}, u32[]{:S(2)}) collective-permute-start(f32[256,512]{1,0:T(8,128)S(1)} %pack_one.1), channel_id=1, source_target_pairs={{0,2},{1,3},{2,0},{3,1},{4,6},{5,7},{6,4},{7,5},{8,10},{9,11},{10,... | collective-permute-start | bytes 1572872 | tf_op jit(solution)/shard_map/ppermute | solution.py:594
  83.3 55.4 %collective-permute-start.12 = (f32[256,512]{1,0:T(8,128)S(1)}, f32[256,512]{1,0:T(8,128)S(1)}, u32[]{:S(2)}, u32[]{:S(2)}) collective-permute-start(f32[256,512]{1,0:T(8,128)S(1)} %get-tuple-element.61), channel_id=1, source_target_pairs={{0,3},{1,2},{2,1},{3,0},{4,7},{5,6},{6,5},{7,4},{8,11},{9,10},{10,... | collective-permute-start | bytes 1572872 | tf_op jit(solution)/shard_map/ppermute | solution.py:594
  84.8 53.8 %collective-permute-start.10 = (f32[256,512]{1,0:T(8,128)S(1)}, f32[256,512]{1,0:T(8,128)S(1)}, u32[]{:S(2)}, u32[]{:S(2)}) collective-permute-start(f32[256,512]{1,0:T(8,128)S(1)} %get-tuple-element.62), channel_id=1, source_target_pairs={{0,1},{1,0},{2,3},{3,2},{4,5},{5,4},{6,7},{7,6},{8,9},{9,8},{10,11... | collective-permute-start | bytes 1572872 | tf_op jit(solution)/shard_map/ppermute | solution.py:594
  85.0 90.1 %copy-start.1 = (bf16[4,512,512]{2,1,0:T(8,128)(2,1)S(1)}, bf16[4,512,512]{2,1,0:T(8,128)(2,1)}, u32[]{:S(2)}) copy-start(bf16[4,512,512]{2,1,0:T(8,128)(2,1)} %copy-done) | copy-start | bytes 6291460
  148.2 3.6 %collective-permute-start.13 = (f32[256,256]{1,0:T(8,128)}, f32[256,256]{1,0:T(8,128)S(1)}, u32[]{:S(2)}, u32[]{:S(2)}) collective-permute-start(f32[256,256]{1,0:T(8,128)} %get-tuple-element.49), channel_id=1, source_target_pairs={{0,4},{4,0},{8,12},{12,8},{16,20},{20,16},{24,28},{28,24},{1,5},{5... | collective-permute-start | bytes 786440 | tf_op jit(solution)/shard_map/ppermute | solution.py:594
  148.2 9.5 %collective-permute-start.14 = (f32[256,256]{1,0:T(8,128)}, f32[256,256]{1,0:T(8,128)S(1)}, u32[]{:S(2)}, u32[]{:S(2)}) collective-permute-start(f32[256,256]{1,0:T(8,128)} %get-tuple-element.50), channel_id=1, source_target_pairs={{0,8},{4,12},{8,0},{12,4},{16,24},{20,28},{24,16},{28,20},{1,9},{5... | collective-permute-start | bytes 786440 | tf_op jit(solution)/shard_map/ppermute | solution.py:594
  149.8 12.6 %collective-permute-start.15 = (f32[256,256]{1,0:T(8,128)}, f32[256,256]{1,0:T(8,128)S(1)}, u32[]{:S(2)}, u32[]{:S(2)}) collective-permute-start(f32[256,256]{1,0:T(8,128)} %get-tuple-element.51), channel_id=1, source_target_pairs={{0,12},{4,8},{8,4},{12,0},{16,28},{20,24},{24,20},{28,16},{1,13},{... | collective-permute-start | bytes 786440 | tf_op jit(solution)/shard_map/ppermute | solution.py:594
  150.1 12.3 %collective-permute-start.16 = (f32[256,256]{1,0:T(8,128)}, f32[256,256]{1,0:T(8,128)S(1)}, u32[]{:S(2)}, u32[]{:S(2)}) collective-permute-start(f32[256,256]{1,0:T(8,128)} %get-tuple-element.52), channel_id=1, source_target_pairs={{0,16},{4,20},{8,24},{12,28},{16,0},{20,4},{24,8},{28,12},{1,17},{... | collective-permute-start | bytes 786440 | tf_op jit(solution)/shard_map/ppermute | solution.py:594
  151.6 23.5 %collective-permute-start.17 = (f32[256,256]{1,0:T(8,128)}, f32[256,256]{1,0:T(8,128)S(1)}, u32[]{:S(2)}, u32[]{:S(2)}) collective-permute-start(f32[256,256]{1,0:T(8,128)} %get-tuple-element.53), channel_id=1, source_target_pairs={{0,20},{4,16},{8,28},{12,24},{16,4},{20,0},{24,12},{28,8},{1,21},{... | collective-permute-start | bytes 786440 | tf_op jit(solution)/shard_map/ppermute | solution.py:594
  151.8 23.3 %collective-permute-start.18 = (f32[256,256]{1,0:T(8,128)}, f32[256,256]{1,0:T(8,128)S(1)}, u32[]{:S(2)}, u32[]{:S(2)}) collective-permute-start(f32[256,256]{1,0:T(8,128)} %get-tuple-element.54), channel_id=1, source_target_pairs={{0,24},{4,28},{8,16},{12,20},{16,8},{20,12},{24,0},{28,4},{1,25},{... | collective-permute-start | bytes 786440 | tf_op jit(solution)/shard_map/ppermute | solution.py:594
  157.7 17.4 %collective-permute-start.19 = (f32[256,256]{1,0:T(8,128)}, f32[256,256]{1,0:T(8,128)S(1)}, u32[]{:S(2)}, u32[]{:S(2)}) collective-permute-start(f32[256,256]{1,0:T(8,128)} %get-tuple-element.55), channel_id=1, source_target_pairs={{0,28},{4,24},{8,20},{12,16},{16,12},{20,8},{24,4},{28,0},{1,29},{... | collective-permute-start | bytes 786440 | tf_op jit(solution)/shard_map/ppermute | solution.py:594
  182.8 92.1 %all-to-all-start.1 = ((f32[32,128,128]{2,1,0:T(8,128)}), f32[32,128,128]{2,1,0:T(8,128)}, u32[]{:S(2)}, u32[]{:S(2)}) async-start(f32[32,128,128]{2,1,0:T(8,128)} %x_second.1), calls=%async_computation.1 | async-start | bytes 4194304 | tf_op jit(solution)/shard_map/all_to_all | solution.py:629
  201.9 72.1 %copy-start.2 = (s32[128,512]{1,0:T(8,128)S(1)}, s32[128,512]{1,0:T(8,128)}, u32[]{:S(2)}) copy-start(s32[128,512]{1,0:T(8,128)} %refs_4_.3) | copy-start | bytes 786436
  201.9 72.1 %copy-start.4 = (f32[2,4,16,512]{3,2,1,0:T(8,128)S(1)}, f32[2,4,16,512]{3,2,1,0:T(8,128)}, u32[]{:S(2)}) copy-start(f32[2,4,16,512]{3,2,1,0:T(8,128)} %get-tuple-element.57.refs_0_) | copy-start | bytes 786436
  201.9 35.1 %collective-permute-start.20 = (f32[2,4,16,512]{3,2,1,0:T(8,128)S(1)}, f32[2,4,16,512]{3,2,1,0:T(8,128)S(1)}, u32[]{:S(2)}, u32[]{:S(2)}) collective-permute-start(f32[2,4,16,512]{3,2,1,0:T(8,128)S(1)} %get-tuple-element.58), channel_id=1, source_target_pairs={{0,1},{1,0},{2,3},{3,2},{4,5},{5,4},{6,7},{7,6},{8,9},{9,8},{10,11... | collective-permute-start | bytes 786440 | tf_op jit(solution)/shard_map/ppermute | solution.py:594
  203.4 70.5 %collective-permute-start.21 = (f32[2,4,16,512]{3,2,1,0:T(8,128)S(1)}, f32[2,4,16,512]{3,2,1,0:T(8,128)S(1)}, u32[]{:S(2)}, u32[]{:S(2)}) collective-permute-start(f32[2,4,16,512]{3,2,1,0:T(8,128)S(1)} %get-tuple-element.59), channel_id=1, source_target_pairs={{0,2},{1,3},{2,0},{3,1},{4,6},{5,7},{6,4},{7,5},{8,10},{9,11},{10,... | collective-permute-start | bytes 786440 | tf_op jit(solution)/shard_map/ppermute | solution.py:594
  205.8 68.1 %collective-permute-start.22 = (f32[2,4,16,512]{3,2,1,0:T(8,128)S(1)}, f32[2,4,16,512]{3,2,1,0:T(8,128)S(1)}, u32[]{:S(2)}, u32[]{:S(2)}) collective-permute-start(f32[2,4,16,512]{3,2,1,0:T(8,128)S(1)} %get-tuple-element.60), channel_id=1, source_target_pairs={{0,3},{1,2},{2,1},{3,0},{4,7},{5,6},{6,5},{7,4},{8,11},{9,10},{10,... | collective-permute-start | bytes 786440 | tf_op jit(solution)/shard_map/ppermute | solution.py:594
  211.5 68.9 %collective-permute-start.7 = (f32[2,4,16,512]{3,2,1,0:T(8,128)S(1)}, f32[2,4,16,512]{3,2,1,0:T(8,128)S(1)}, u32[]{:S(2)}, u32[]{:S(2)}) collective-permute-start(f32[2,4,16,512]{3,2,1,0:T(8,128)S(1)} %get-tuple-element.45), channel_id=1, source_target_pairs={{0,1},{1,0},{2,3},{3,2},{4,5},{5,4},{6,7},{7,6},{8,9},{9,8},{10,11... | collective-permute-start | bytes 786440 | tf_op jit(solution)/shard_map/ppermute | solution.py:594
  212.0 73.1 %collective-permute-start.8 = (f32[2,4,16,512]{3,2,1,0:T(8,128)S(1)}, f32[2,4,16,512]{3,2,1,0:T(8,128)S(1)}, u32[]{:S(2)}, u32[]{:S(2)}) collective-permute-start(f32[2,4,16,512]{3,2,1,0:T(8,128)S(1)} %get-tuple-element.46), channel_id=1, source_target_pairs={{0,2},{1,3},{2,0},{3,1},{4,6},{5,7},{6,4},{7,5},{8,10},{9,11},{10,... | collective-permute-start | bytes 786440 | tf_op jit(solution)/shard_map/ppermute | solution.py:594
  237.0 48.2 %collective-permute-start.9 = (f32[2,4,16,512]{3,2,1,0:T(8,128)S(1)}, f32[2,4,16,512]{3,2,1,0:T(8,128)S(1)}, u32[]{:S(2)}, u32[]{:S(2)}) collective-permute-start(f32[2,4,16,512]{3,2,1,0:T(8,128)S(1)} %get-tuple-element.47), channel_id=1, source_target_pairs={{0,3},{1,2},{2,1},{3,0},{4,7},{5,6},{6,5},{7,4},{8,11},{9,10},{10,... | collective-permute-start | bytes 786440 | tf_op jit(solution)/shard_map/ppermute | solution.py:594
  275.0 10.2 %copy-start.3 = (f32[2,4,16,512]{3,2,1,0:T(8,128)S(1)}, f32[2,4,16,512]{3,2,1,0:T(8,128)}, u32[]{:S(2)}) copy-start(f32[2,4,16,512]{3,2,1,0:T(8,128)} %get-tuple-element.44.refs_0_) | copy-start | bytes 786436
  (4 other events, 6.0 us)
